TPU v7x, 256 devices: a whole 4x4x8 slice. The times are simulated.
256 devices in a mesh: dp: 8 (over z), head: 32 (over y, x, core).
Axes of the slice: x: 4, y: 4, z: 8, core: 2. Of those that a mesh axis runs over, the one named last changes fastest.
Arguments:
- residual: float32 [192, 4096], P('dp', 'head'), parts along dimension 0, may hold values from -70 to 70
- norm_gain: float32 [4096], replicated, may hold values from 0.5 to 1.5
- w_query: bfloat16 [8, 256, 4096], P(None, 'head'), may hold values from -0.09375 to 0.09375
- w_key: bfloat16 [8, 256, 4096], P(None, 'head'), may hold values from -0.09375 to 0.09375
- w_value: bfloat16 [4096, 4096], P(None, 'head'), may hold values from -0.09375 to 0.09375
- w_gate: bfloat16 [4096, 4096], P(None, 'head'), may hold values from -0.09375 to 0.09375
- w_input: bfloat16 [8, 4096], replicated, may hold values from -0.09375 to 0.09375
- w_forget: bfloat16 [8, 4096], replicated, may hold values from -0.09375 to 0.09375
- b_input: float32 [8], replicated, may hold values from -2 to -0.5
- b_forget: float32 [8], replicated, may hold values from 0.5 to 4
- w_out: bfloat16 [4096, 4096], P('head'), may hold values from -0.1875 to 0.1875
- memory: bfloat16 [192, 8, 256, 512], P('dp', None, 'head'), parts along dimension 0, may hold values from -0.59765625 to 0.59765625
- normalizer: float32 [192, 8, 256], P('dp', None, 'head'), parts along dimension 0, may hold values from -0.6 to 0.6
- stabilizer: float32 [192, 8], P('dp'), parts along dimension 0, may hold values from -0.5 to 0.5
Outputs:
- res_out: float32 [192, 4096], P('dp', 'head'), parts along dimension 0
- mem_out: bfloat16 [192, 8, 256, 512], P('dp', None, 'head'), parts along dimension 0
- norm_out: float32 [192, 8, 256], P('dp', None, 'head'), parts along dimension 0
- stab_out: float32 [192, 8], P('dp'), parts along dimension 0
There are 8 independent parts, one for each index of `dp`. A program takes and returns all parts, laid end to end along the dimension named above; an argument that names none is the same for every part. Nothing has to cross between parts.
All inputs are finite; a program needn't handle non-finite values.
Results may differ from a plain program's by a relative error of at most 0.0095.
Values may be sent and summed in bfloat16 or wider, within the bound.
No kernel may reach another device: no remote copies, remote signals or barrier semaphores. Data moves between devices by JAX's collectives and lax.ppermute only.
A program may use at most 64 MiB of HBM per device.

v0:
```python
import math

import jax
import jax.numpy as jnp
from jax import lax
from jax.sharding import PartitionSpec as P

H = 8
DK = 256
DV = 512


epsilon = 1e-06


def laid_out(pieces, dim):
    pieces = jnp.moveaxis(pieces, 0, dim)
    shape = pieces.shape
    return pieces.reshape(*shape[:dim], shape[dim] * shape[dim + 1], *shape[dim + 2 :])


def sent_to_all(value, axis):
    count = lax.axis_size(axis)
    return lax.all_to_all(
        jnp.broadcast_to(value[None], (count, *value.shape)), axis, 0, 0, tiled=True
    )


def gathered_copies(value, axis, dim):
    return laid_out(sent_to_all(value, axis), dim)


def split_up(value, dim, count):
    shape = value.shape
    pieces = value.reshape(*shape[:dim], count, shape[dim] // count, *shape[dim + 1 :])
    return jnp.moveaxis(pieces, dim, 0)


def sum_at_owner(value, axis, dim):
    pieces = split_up(value, dim, lax.axis_size(axis))
    arrived = lax.all_to_all(pieces, axis, split_axis=0, concat_axis=0, tiled=True)
    return arrived.astype(jnp.float32).sum(axis=0)


def taken_together(value, axis):
    everything = sent_to_all(value, axis)
    return jnp.sum(everything, axis=0)


def body(
    residual,
    norm_gain,
    w_query,
    w_key,
    w_value,
    w_gate,
    w_input,
    w_forget,
    b_input,
    b_forget,
    w_out,
    memory,
    normalizer,
    stabilizer,
):
    dev_index = lax.axis_index("head")
    group_size = lax.axis_size("head")
    batch_size = residual.shape[0]
    gathered = gathered_copies(residual, "head", 1)
    row_scale = lax.rsqrt(jnp.mean(gathered * gathered, axis=1, keepdims=True) + epsilon)
    x_norm = (gathered * row_scale * norm_gain).astype(jnp.bfloat16)
    query_vec = jnp.einsum("bd,hkd->bhk", x_norm, w_query, preferred_element_type=jnp.float32)
    key_vec = jnp.einsum(
        "bd,hkd->bhk", x_norm, w_key, preferred_element_type=jnp.float32
    ) / math.sqrt(DK)
    value_part = jnp.dot(x_norm, w_value, preferred_element_type=jnp.float32).astype(jnp.bfloat16)
    value_vec = gathered_copies(value_part, "head", 1)
    contract = (((1,), (1,)), ((), ()))
    input_pre = (
        lax.dot_general(x_norm, w_input, contract, preferred_element_type=jnp.float32) + b_input
    )
    forget_pre = (
        lax.dot_general(x_norm, w_forget, contract, preferred_element_type=jnp.float32) + b_forget
    )
    log_forget = jax.nn.log_sigmoid(forget_pre)
    stab_new = jnp.maximum(log_forget + stabilizer, input_pre)
    input_gate = jnp.exp(input_pre - stab_new)
    forget_gate = jnp.exp(log_forget + stabilizer - stab_new)
    value_heads = value_vec.astype(jnp.float32).reshape(batch_size, H, DV)
    memory_full = (
        forget_gate[:, :, None, None] * memory.astype(jnp.float32)
        + input_gate[:, :, None, None] * key_vec[:, :, :, None] * value_heads[:, :, None, :]
    )
    norm_new = forget_gate[:, :, None] * normalizer + input_gate[:, :, None] * key_vec
    numerator = jnp.sum(memory_full * query_vec[:, :, :, None], axis=2).reshape(batch_size, H * DV)
    denom_part = jnp.sum(norm_new * query_vec, axis=2)
    share_width = H * DV // group_size
    head_pick = dev_index * share_width // DV
    col_share = sum_at_owner(numerator.astype(jnp.bfloat16), "head", 1)
    denom_all = taken_together(denom_part, "head")
    denom_mine = lax.dynamic_slice_in_dim(denom_all, head_pick, 1, 1)
    stab_mine = lax.dynamic_slice_in_dim(stab_new, head_pick, 1, 1)
    readout = col_share / jnp.maximum(jnp.abs(denom_mine), jnp.exp(-stab_mine))
    out_gate = jax.nn.sigmoid(jnp.dot(x_norm, w_gate, preferred_element_type=jnp.float32))
    hidden = (out_gate * readout).astype(jnp.bfloat16)
    branch_out = sum_at_owner(
        lax.dot_general(
            w_out, hidden, (((0,), (1,)), ((), ())), preferred_element_type=jnp.float32
        ).astype(jnp.bfloat16),
        "head",
        0,
    )
    res_out = residual + branch_out.T
    return (res_out, memory_full.astype(jnp.bfloat16), norm_new, stab_new)


def solution(mesh):
    in_specs = (
        P("dp", "head"),
        P(),
        P(None, "head", None),
        P(None, "head", None),
        P(None, "head"),
        P(None, "head"),
        P(),
        P(),
        P(),
        P(),
        P("head", None),
        P("dp", None, "head", None),
        P("dp", None, "head"),
        P("dp", None),
    )
    out_specs = (P("dp", "head"), P("dp", None, "head", None), P("dp", None, "head"), P("dp", None))
    return jax.shard_map(body, mesh=mesh, in_specs=in_specs, out_specs=out_specs, check_vma=False)
```

profile of v0, /device:TPU:1, one launch (start us, length us, event | category | flops | bytes accessed | tf_op | source)
XLA Modules:
  0.0 78.3 jit_solution(12892682699413815252)
XLA Ops:
  0.6 0.0 copy-start
  0.6 0.0 copy-start.8
  0.7 0.0 copy-start.13
  0.7 0.0 copy-start.10
  0.7 0.0 copy-start.12
  0.7 0.8 %broadcast_in_dim.6 = f32[32,24,128]{2,1,0:T(8,128)S(1)} broadcast(f32[24,128]{1,0:T(8,128)} %param.14), dimensions={1,2} | broadcast | bytes 405504 | tf_op jit(solution)/shard_map/broadcast_in_dim | solution.py:25
  1.6 0.0 copy-start.5
  1.6 0.0 copy-start.7
  1.6 18.7 %all_to_all.25 = f32[32,24,128]{2,1,0:T(8,128)S(1)} all-to-all(f32[32,24,128]{2,1,0:T(8,128)S(1)} %broadcast_in_dim.6), channel_id=1, replica_groups=mesh['dp'=8,'head'=32] {'head'}, dimensions={0} | all-to-all | bytes 786432 | tf_op jit(solution)/shard_map/all_to_all | solution.py:24
  20.2 0.1 fusion.10
  20.4 0.0 copy-start.2
  20.4 0.1 fusion.9
  20.5 0.0 copy-done.13
  20.5 0.0 copy-done.10
  20.6 0.2 convolution_add_fusion
  20.7 0.0 copy-done.12
  20.8 0.2 subtract_exponential_fusion
  20.9 0.0 copy-start.9
  21.0 0.3 convolution_multiply_fusion
  21.3 0.8 %multiply_reduce_fusion.1 = (f32[24,8]{0,1:T(8,128)S(1)}, f32[24,8,8]{0,2,1:T(8,128)}, f32[24,8,8]{0,2,1:T(8,128)S(1)}) fusion(f32[24,8,8]{0,2,1:T(8,128)S(1)} %convolution_multiply_fusion, f32[24,8,8]{0,2,1:T(8,128)S(1)} %copy-done.7, f32[24,8]{0,1:T(8,128)S(1)} %get-tuple-element.6, bf16[8,8,4096]{2,1,0:T(8,128)(2,1)S(1)} %copy-done.5, ...), kind=kOutput, calls=%fused_computation.28 | convolution fusion | flops 12588864 | bytes 747008 | tf_op jit(solution)/shard_map/bd,hkd->bhk/dot_general | solution.py:72
  22.1 0.8 reshape.53
  22.8 3.8 %all-to-all-start.3 = ((f32[32,1,192]{2,1,0:T(1,128)}), f32[32,1,192]{2,1,0:T(1,128)S(1)}, u32[]{:S(2)}, u32[]{:S(2)}) async-start(f32[32,1,192]{2,1,0:T(1,128)} %reshape.53), calls=%async_computation.3 | async-start | bytes 65536 | tf_op jit(solution)/shard_map/all_to_all | solution.py:24
  26.6 0.0 copy-done.2
  26.6 0.3 convolution_convert_fusion.1
  26.9 7.1 %all-to-all-done.3 = f32[32,1,192]{2,1,0:T(1,128)S(1)} async-done(((f32[32,1,192]{2,1,0:T(1,128)}), f32[32,1,192]{2,1,0:T(1,128)S(1)}, u32[]{:S(2)}, u32[]{:S(2)}) %all-to-all-start.3) | async-done | bytes 24608 | tf_op jit(solution)/shard_map/all_to_all | solution.py:24
  34.0 0.7 broadcast_in_dim.7
  34.7 4.0 %all-to-all-start.1 = ((bf16[32,24,128]{2,1,0:T(8,128)(2,1)}), bf16[32,24,128]{2,1,0:T(8,128)(2,1)S(1)}, u32[]{:S(2)}, u32[]{:S(2)}) async-start(bf16[32,24,128]{2,1,0:T(8,128)(2,1)} %broadcast_in_dim.7), calls=%async_computation.1 | async-start | bytes 393216 | tf_op jit(solution)/shard_map/all_to_all | solution.py:24
  38.8 0.1 copy.26
  38.9 0.7 copy.27
  39.6 0.7 copy.29
  40.3 0.5 broadcast.48
  40.8 0.7 reduce.1
  41.5 0.1 reshape.54
  41.6 5.5 %all-to-all-done.1 = bf16[32,24,128]{2,1,0:T(8,128)(2,1)S(1)} async-done(((bf16[32,24,128]{2,1,0:T(8,128)(2,1)}), bf16[32,24,128]{2,1,0:T(8,128)(2,1)S(1)}, u32[]{:S(2)}, u32[]{:S(2)}) %all-to-all-start.1) | async-done | bytes 196640 | tf_op jit(solution)/shard_map/all_to_all | solution.py:24
  47.1 0.8 %copy.28 = f32[24,32,128]{2,1,0:T(8,128)} copy(f32[24,32,128]{2,0,1:T(8,128)S(1)} %convert_bitcast_fusion) | data formatting | bytes 786432 | tf_op jit(solution)/shard_map/convert_element_type | solution.py:89
  48.0 1.1 %reshape.51 = f32[24,8,512]{2,1,0:T(8,128)S(1)} reshape(f32[24,32,128]{2,1,0:T(8,128)} %copy.28) | data formatting | bytes 786432 | tf_op jit(solution)/shard_map/convert_element_type | solution.py:89
  49.0 3.2 %fusion = (bf16[24,8,8,512]{3,2,1,0:T(8,128)(2,1)}, bf16[24,8,512]{2,1,0:T(8,128)(2,1)S(1)}) fusion(bf16[24,8,8,512]{3,2,1,0:T(8,128)(2,1)S(1)} %copy-done.1, f32[24,8,512]{2,1,0:T(8,128)S(1)} %reshape.51, f32[24,8,8]{2,1,0:T(8,128)} %copy.27, f32[24,8]{1,0:T(8,128)S(1)} %copy.26, f32[24,8,8]{2,1,0:T(8,128)} %copy.29), kind=kLoop, calls=%fused_computation.3 | loop fusion | flops 5406720 | bytes 3748608 | tf_op jit(solution)/shard_map/convert_element_type | solution.py:114
  52.2 0.0 copy-start.3
  52.3 0.1 convert_element_type.54
  52.4 0.8 copy.30
  53.1 3.8 %all-to-all-start.2 = ((bf16[32,24,128]{2,1,0:T(8,128)(2,1)}), bf16[32,24,128]{2,1,0:T(8,128)(2,1)S(1)}, u32[]{:S(2)}, u32[]{:S(2)}) async-start(bf16[32,24,128]{2,1,0:T(8,128)(2,1)} %copy.30), calls=%async_computation.2 | async-start | bytes 393216 | tf_op jit(solution)/shard_map/all_to_all | solution.py:41
  57.0 8.2 %all-to-all-done.2 = bf16[32,24,128]{2,1,0:T(8,128)(2,1)S(1)} async-done(((bf16[32,24,128]{2,1,0:T(8,128)(2,1)}), bf16[32,24,128]{2,1,0:T(8,128)(2,1)S(1)}, u32[]{:S(2)}, u32[]{:S(2)}) %all-to-all-start.2) | async-done | bytes 196640 | tf_op jit(solution)/shard_map/all_to_all | solution.py:41
  65.2 0.0 copy-done
  65.2 0.0 copy-done.3
  65.2 0.0 copy-start.6
  65.3 0.5 fusion.1
  65.8 11.8 %all_to_all.26 = bf16[32,128,24]{1,2,0:T(8,128)(2,1)S(1)} all-to-all(bf16[32,128,24]{1,2,0:T(8,128)(2,1)S(1)} %bitcast.49), channel_id=1, replica_groups=mesh['dp'=8,'head'=32] {'head'}, dimensions={0} | all-to-all | bytes 393216 | tf_op jit(solution)/shard_map/all_to_all | solution.py:41
  77.7 0.6 bitcast_add_fusion
  (22 shorter events, 0.2 us)
Async XLA Ops:
  0.6 64.6 %copy-start = (bf16[128,4096]{1,0:T(8,128)(2,1)S(1)}, bf16[128,4096]{1,0:T(8,128)(2,1)}, u32[]{:S(2)}) copy-start(bf16[128,4096]{1,0:T(8,128)(2,1)} %param.24) | copy-start | bytes 3145732
  0.6 19.8 %copy-start.8 = (f32[4096]{0:T(1024)S(1)}, f32[4096]{0:T(1024)}, u32[]{:S(2)}) copy-start(f32[4096]{0:T(1024)} %param.15) | copy-start | bytes 49156
  0.7 19.9 %copy-start.13 = (f32[8]{0:T(128)S(1)}, f32[8]{0:T(128)}, u32[]{:S(2)}) copy-start(f32[8]{0:T(128)} %param.22) | copy-start | bytes 100
  0.7 19.9 %copy-start.10 = (bf16[8,4096]{1,0:T(8,128)(2,1)S(1)}, bf16[8,4096]{1,0:T(8,128)(2,1)}, u32[]{:S(2)}) copy-start(bf16[8,4096]{1,0:T(8,128)(2,1)} %param.20) | copy-start | bytes 196612
  0.7 20.0 %copy-start.12 = (f32[24,8]{0,1:T(8,128)S(1)}, f32[24,8]{0,1:T(8,128)}, u32[]{:S(2)}) copy-start(f32[24,8]{0,1:T(8,128)} %param.27) | copy-start | bytes 2308
  0.7 20.0 %copy-start.14 = (f32[8]{0:T(128)S(1)}, f32[8]{0:T(128)}, u32[]{:S(2)}) copy-start(f32[8]{0:T(128)} %param.23) | copy-start | bytes 100
  0.7 20.0 %copy-start.11 = (bf16[8,4096]{1,0:T(8,128)(2,1)S(1)}, bf16[8,4096]{1,0:T(8,128)(2,1)}, u32[]{:S(2)}) copy-start(bf16[8,4096]{1,0:T(8,128)(2,1)} %param.21) | copy-start | bytes 196612
  0.7 20.3 %copy-start.4 = (bf16[8,8,4096]{2,1,0:T(8,128)(2,1)S(1)}, bf16[8,8,4096]{2,1,0:T(8,128)(2,1)}, u32[]{:S(2)}) copy-start(bf16[8,8,4096]{2,1,0:T(8,128)(2,1)} %param.17) | copy-start | bytes 1572868
  1.6 19.7 %copy-start.5 = (bf16[8,8,4096]{2,1,0:T(8,128)(2,1)S(1)}, bf16[8,8,4096]{2,1,0:T(8,128)(2,1)}, u32[]{:S(2)}) copy-start(bf16[8,8,4096]{2,1,0:T(8,128)(2,1)} %param.16) | copy-start | bytes 1572868
  1.6 19.7 %copy-start.7 = (f32[24,8,8]{0,2,1:T(8,128)S(1)}, f32[24,8,8]{0,2,1:T(8,128)}, u32[]{:S(2)}) copy-start(f32[24,8,8]{0,2,1:T(8,128)} %param.26) | copy-start | bytes 18436
  20.4 6.2 %copy-start.2 = (bf16[4096,128]{1,0:T(8,128)(2,1)S(1)}, bf16[4096,128]{1,0:T(8,128)(2,1)}, u32[]{:S(2)}) copy-start(bf16[4096,128]{1,0:T(8,128)(2,1)} %param.18) | copy-start | bytes 3145732
  20.9 36.0 %copy-start.9 = (f32[24,8]{0,1:T(8,128)}, f32[24,8]{0,1:T(8,128)S(1)}, u32[]{:S(2)}) copy-start(f32[24,8]{0,1:T(8,128)S(1)} %get-tuple-element.7) | copy-start | bytes 2308
  22.8 11.2 %all-to-all-start.3 = ((f32[32,1,192]{2,1,0:T(1,128)}), f32[32,1,192]{2,1,0:T(1,128)S(1)}, u32[]{:S(2)}, u32[]{:S(2)}) async-start(f32[32,1,192]{2,1,0:T(1,128)} %reshape.53), calls=%async_computation.3 | async-start | bytes 65536 | tf_op jit(solution)/shard_map/all_to_all | solution.py:24
  34.7 14.3 %copy-start.1 = (bf16[24,8,8,512]{3,2,1,0:T(8,128)(2,1)S(1)}, bf16[24,8,8,512]{3,2,1,0:T(8,128)(2,1)}, u32[]{:S(2)}) copy-start(bf16[24,8,8,512]{3,2,1,0:T(8,128)(2,1)} %param.25) | copy-start | bytes 4718596
  34.7 12.4 %all-to-all-start.1 = ((bf16[32,24,128]{2,1,0:T(8,128)(2,1)}), bf16[32,24,128]{2,1,0:T(8,128)(2,1)S(1)}, u32[]{:S(2)}, u32[]{:S(2)}) async-start(bf16[32,24,128]{2,1,0:T(8,128)(2,1)} %broadcast_in_dim.7), calls=%async_computation.1 | async-start | bytes 393216 | tf_op jit(solution)/shard_map/all_to_all | solution.py:24
  52.2 13.0 %copy-start.3 = (bf16[4096,128]{1,0:T(8,128)(2,1)S(1)}, bf16[4096,128]{1,0:T(8,128)(2,1)}, u32[]{:S(2)}) copy-start(bf16[4096,128]{1,0:T(8,128)(2,1)} %param.19) | copy-start | bytes 3145732
  53.1 12.0 %all-to-all-start.2 = ((bf16[32,24,128]{2,1,0:T(8,128)(2,1)}), bf16[32,24,128]{2,1,0:T(8,128)(2,1)S(1)}, u32[]{:S(2)}, u32[]{:S(2)}) async-start(bf16[32,24,128]{2,1,0:T(8,128)(2,1)} %copy.30), calls=%async_computation.2 | async-start | bytes 393216 | tf_op jit(solution)/shard_map/all_to_all | solution.py:41
  65.2 12.5 %copy-start.6 = (f32[24,128]{1,0:T(8,128)S(1)}, f32[24,128]{1,0:T(8,128)}, u32[]{:S(2)}) copy-start(f32[24,128]{1,0:T(8,128)} %param.14) | copy-start | bytes 36868
where the time goes:
time: 78.8 us; the launch traced here: 78.3 us
  blocking collectives  30.5 us (39%)
  waiting for transfers between devices  20.7 us (26%)
  starting transfers between devices  11.6 us (15%)
  local copies, waits for them, and re-layouts  7.32 us (9%)
  other arithmetic  4.95 us (6%)
  matrix products  2.2 us (3%)
  between operations  1.01 us (1%)
    all_to_all x1, blocking collectives, sent_to_all(): lax.all_to_all(jnp.broadcast_to(value[None], (count, *value.shape)), axis...  18.7 us
    all_to_all x2, waiting for transfers between devices, sent_to_all(): lax.all_to_all(jnp.broadcast_to(value[None], (count, *value.shape)), axis...  12.5 us
    all_to_all x1, blocking collectives, sum_at_owner(): lax.all_to_all(pieces, axis, split_axis=0, concat_axis=0, tiled=True)  11.8 us
    all_to_all x1, waiting for transfers between devices, sum_at_owner(): lax.all_to_all(pieces, axis, split_axis=0, concat_axis=0, tiled=True)  8.18 us
    all_to_all x2, starting transfers between devices, sent_to_all(): lax.all_to_all(jnp.broadcast_to(value[None], (count, *value.shape)), axis...  7.83 us
    all_to_all x1, starting transfers between devices, sum_at_owner(): lax.all_to_all(pieces, axis, split_axis=0, concat_axis=0, tiled=True)  3.8 us
    convert_element_type x1, other arithmetic, body(): return (res_out, memory_full.astype(jnp.bfloat16), norm_new, stab_new)  3.2 us
    convert_element_type x2, local copies, waits for them, and re-layouts, body(): value_heads = value_vec.astype(jnp.float32).reshape(batch_size, H, DV)  1.88 us
  transfers between devices with their start and end apart: 3, of which 3 were waited for; matrix products, arithmetic and copies ran while one was open for 4% of the time, Pallas kernels for 0%

commit v1 on v0

v1 whole, which is shorter than its diff:
```python
import math

import jax
import jax.numpy as jnp
from jax import lax
from jax.experimental import pallas as pl
from jax.experimental.pallas import tpu as pltpu
from jax.sharding import PartitionSpec as P

H = 8
DK = 256
DV = 512
EPSILON = 1e-06
F32 = jnp.float32
BF16 = jnp.bfloat16
STATS = 8


def exchange(pieces):
    return lax.all_to_all(pieces, "head", 0, 0, tiled=True)


def dot_last(left, right):
    return lax.dot_general(left, right, (((1,), (1,)), ((), ())), preferred_element_type=F32)


def dot(left, right):
    return jnp.dot(left, right, preferred_element_type=F32)


def column(row):
    n = row.shape[1]
    at_row = lax.broadcasted_iota(jnp.int32, (n, n), 0)
    at_col = lax.broadcasted_iota(jnp.int32, (n, n), 1)
    return jnp.sum(jnp.where(at_row == at_col, row, 0.0), axis=1, keepdims=True)


def split_hi_lo(value):
    high = value.astype(BF16).astype(F32)
    return high, value - high


def project_kernel(
    x_ref, gain_ref, wq_ref, wk_ref, wv_ref, wi_ref, wf_ref, bi_ref, bf_ref, mem_ref, nrm_ref, stab_ref,
    out_ref, value_ref, xn_ref, nrm_out_ref, stab_out_ref, fg_ref, ig_ref, f_rows_ref, ik_rows_ref,
    stats_ref,
):
    pieces, batch, width = x_ref.shape
    rows = wq_ref.shape[0] // H
    total = jnp.zeros((batch, width), F32)
    for j in range(pieces):
        x = x_ref[j].astype(F32)
        total = total + x * x
    mean = jnp.sum(total, axis=1, keepdims=True) / (pieces * width)
    scale = lax.rsqrt(mean + EPSILON)
    for j in range(pieces):
        cut = slice(j * width, (j + 1) * width)
        xn_ref[:, cut] = (x_ref[j].astype(F32) * scale * gain_ref[:, cut]).astype(BF16)
    x_norm = xn_ref[...]

    query = dot_last(x_norm, wq_ref[...])
    query_t = dot_last(wq_ref[...], x_norm)
    key_t = dot_last(wk_ref[...], x_norm) / math.sqrt(DK)
    input_pre = dot_last(wi_ref[...], x_norm) + column(bi_ref[...])
    forget_pre = dot_last(wf_ref[...], x_norm) + column(bf_ref[...])
    value = dot(x_norm, wv_ref[...]).astype(BF16)
    for j in range(pieces):
        value_ref[j] = value

    log_forget = jnp.minimum(forget_pre, 0.0) - jnp.log1p(jnp.exp(-jnp.abs(forget_pre)))
    kept = log_forget + stab_ref[...]
    stab_new = jnp.maximum(kept, input_pre)
    input_gate = jnp.exp(input_pre - stab_new)
    forget_gate = jnp.exp(kept - stab_new)
    stab_out_ref[...] = stab_new
    fg_ref[...] = forget_gate
    ig_ref[...] = input_gate

    stats_ref[...] = jnp.zeros(stats_ref.shape, F32)
    for h in range(H):
        part = slice(h * rows, (h + 1) * rows)
        key_h = key_t[part]
        query_h = query_t[part]
        f_h = jnp.broadcast_to(forget_gate[h : h + 1], (rows, batch))
        ik_h = input_gate[h : h + 1] * key_h
        norm_h = f_h * nrm_ref[part] + ik_h
        nrm_out_ref[part] = norm_h
        f_rows_ref[part] = f_h
        ik_rows_ref[part] = ik_h
        norm_query = jnp.sum(norm_h * query_h, axis=0, keepdims=True)
        key_query = jnp.sum(key_h * query_h, axis=0, keepdims=True)
        kinds = (*split_hi_lo(norm_query), *split_hi_lo(key_query))
        for k, kind in enumerate(kinds):
            stats_ref[h, k : k + 1, :batch] = kind

    spread = batch * rows
    high, low = split_hi_lo(query)
    both = jnp.concatenate([high, low], axis=0).astype(BF16)
    at_k = lax.broadcasted_iota(jnp.int32, (rows, spread), 0)
    at_n = lax.broadcasted_iota(jnp.int32, (rows, spread), 1)
    repeat = jnp.where(at_n % rows == at_k, 1.0, 0.0).astype(BF16)
    own_b = lax.broadcasted_iota(jnp.int32, (2 * batch, spread), 0) % batch
    own_n = lax.broadcasted_iota(jnp.int32, (2 * batch, spread), 1) // rows
    own = own_b == own_n
    share = pieces // H
    for h in range(H):
        wide = dot(both[:, h * rows : (h + 1) * rows], repeat)
        left = jnp.where(own, wide, 0.0).astype(BF16)
        memory = mem_ref[:, h].astype(F32).reshape(spread, share * width).astype(BF16)
        product = dot(left, memory)
        numer = (product[:batch] + product[batch:]).astype(BF16)
        stats = stats_ref[h].astype(BF16)
        for c in range(share):
            out_ref[h * share + c, :batch] = numer[:, c * width : (c + 1) * width]
            out_ref[h * share + c, batch:] = stats


def gate_kernel(head_ref, xn_ref, wg_ref, value_ref, fg_ref, ig_ref, stab_ref, sum_scale_ref, own_ref, floor_ref):
    head = head_ref[0]
    pick = lambda ref: column(ref[pl.ds(head, 1), :])
    gate = jax.nn.sigmoid(dot(xn_ref[...], wg_ref[...]))
    sum_scale_ref[...] = gate * pick(fg_ref)
    own_ref[...] = gate * pick(ig_ref) * value_ref[0].astype(F32)
    floor_ref[...] = jnp.broadcast_to(jnp.exp(-pick(stab_ref)), floor_ref.shape)


def output_kernel(in_ref, sum_scale_ref, own_ref, floor_ref, wo_ref, out_ref):
    pieces, batch, width = out_ref.shape
    total = jnp.zeros(in_ref.shape[1:], F32)
    for j in range(pieces):
        total = total + in_ref[j].astype(F32)
    norm_query = column(total[batch : batch + 1, :batch] + total[batch + 1 : batch + 2, :batch])
    key_query = column(total[batch + 2 : batch + 3, :batch] + total[batch + 3 : batch + 4, :batch])
    numer = sum_scale_ref[...] * total[:batch] + own_ref[...] * key_query
    hidden = (numer / jnp.maximum(jnp.abs(norm_query), floor_ref[...])).astype(BF16)
    for j in range(pieces):
        out_ref[j] = dot(hidden, wo_ref[:, j * width : (j + 1) * width]).astype(BF16)


def memory_kernel(mem_ref, value_ref, f_rows_ref, ik_rows_ref, out_ref, wide_ref):
    pieces, batch, width = value_ref.shape
    share = pieces // H
    rows = mem_ref.shape[2]
    for j in range(pieces):
        cut = slice((j % share) * width, (j % share + 1) * width)
        wide_ref[j // share, :, cut] = value_ref[j].astype(F32)

    def one_head(h, carry):
        at = pl.multiple_of(h * rows, rows)
        f_rows = f_rows_ref[pl.ds(at, rows), :]
        ik_rows = ik_rows_ref[pl.ds(at, rows), :]
        for b in range(batch):
            kept = f_rows[:, b : b + 1] * mem_ref[b, h].astype(F32)
            out_ref[b, h] = (kept + ik_rows[:, b : b + 1] * wide_ref[h, b : b + 1, :]).astype(BF16)
        return carry

    lax.fori_loop(0, H, one_head, 0)


def finish_kernel(in_ref, residual_ref, out_ref):
    total = residual_ref[...]
    acc = in_ref[0].astype(F32)
    for j in range(1, in_ref.shape[0]):
        acc = acc + in_ref[j].astype(F32)
    out_ref[...] = total + acc


def call(kernel, outs, n_in, scratch=(), smem=0, flops=1_000_000):
    return pl.pallas_call(
        kernel,
        out_shape=[jax.ShapeDtypeStruct(*out) for out in outs],
        in_specs=[pl.BlockSpec(memory_space=pltpu.SMEM)] * smem
        + [pl.BlockSpec(memory_space=pltpu.VMEM)] * n_in,
        out_specs=[pl.BlockSpec(memory_space=pltpu.VMEM)] * len(outs),
        scratch_shapes=list(scratch),
        compiler_params=pltpu.CompilerParams(vmem_limit_bytes=16 * 2**20),
        cost_estimate=pl.CostEstimate(flops=flops, bytes_accessed=2_000_000, transcendentals=0),
    )


def body(
    residual,
    norm_gain,
    w_query,
    w_key,
    w_value,
    w_gate,
    w_input,
    w_forget,
    b_input,
    b_forget,
    w_out,
    memory,
    normalizer,
    stabilizer,
):
    count = lax.axis_size("head")
    batch, width = residual.shape
    rows = w_query.shape[1]
    features = count * width
    head_mine = lax.axis_index("head") * width // DV
    gathered = exchange(jnp.broadcast_to(residual.astype(BF16)[None], (count, batch, width)))

    norm_t = normalizer.transpose(1, 2, 0).reshape(H * rows, batch)
    piece = ((count, batch, width), BF16)
    payload, values, x_norm, norm_new, stab_new, forget_gate, input_gate, f_rows, ik_rows = call(
        project_kernel,
        [
            ((count, batch + STATS, width), BF16),
            piece,
            ((batch, features), BF16),
            ((H * rows, batch), F32),
            ((H, batch), F32),
            ((H, batch), F32),
            ((H, batch), F32),
            ((H * rows, batch), F32),
            ((H * rows, batch), F32),
        ],
        12,
        scratch=[pltpu.VMEM((H, STATS, width), F32)],
        flops=100_000_000,
    )(
        gathered,
        norm_gain[None],
        w_query.reshape(H * rows, features),
        w_key.reshape(H * rows, features),
        w_value,
        w_input,
        w_forget,
        b_input[None],
        b_forget[None],
        memory,
        norm_t,
        stabilizer.T,
    )
    arrived = exchange(payload)
    value_heads = exchange(values)
    sum_scale, own, floor = call(
        gate_kernel, [((batch, width), F32)] * 3, 6, smem=1, flops=30_000_000
    )(head_mine[None].astype(jnp.int32), x_norm, w_gate, values, forget_gate, input_gate, stab_new)
    (branch,) = call(output_kernel, [piece], 5, flops=30_000_000)(
        arrived, sum_scale, own, floor, w_out
    )
    returned = exchange(branch)
    (mem_new,) = call(
        memory_kernel,
        [(memory.shape, BF16)],
        4,
        scratch=[pltpu.VMEM((H, batch, DV), F32)],
        flops=100_000_000,
    )(memory, value_heads, f_rows, ik_rows)
    (res_out,) = call(finish_kernel, [((batch, width), F32)], 2)(returned, residual)
    norm_out = norm_new.reshape(H, rows, batch).transpose(2, 0, 1)
    return res_out, mem_new, norm_out, stab_new.T


def solution(mesh):
    in_specs = (
        P("dp", "head"),
        P(),
        P(None, "head", None),
        P(None, "head", None),
        P(None, "head"),
        P(None, "head"),
        P(),
        P(),
        P(),
        P(),
        P("head", None),
        P("dp", None, "head", None),
        P("dp", None, "head"),
        P("dp", None),
    )
    out_specs = (P("dp", "head"), P("dp", None, "head", None), P("dp", None, "head"), P("dp", None))
    return jax.shard_map(body, mesh=mesh, in_specs=in_specs, out_specs=out_specs, check_vma=False)
```

time: 78.8 us -> 68.1 us (0.86)
  waiting for transfers between devices: 20.7 us -> 9.68 us
  Pallas kernels: 0 us -> 7.51 us
  local copies, waits for them, and re-layouts: 7.32 us -> 11.8 us
  other arithmetic: 4.95 us -> 0.71 us
  starting transfers between devices: 11.6 us -> 7.56 us
  matrix products: 2.2 us -> 0 us
  blocking collectives: 30.5 us -> 29.2 us
    all_to_all x3 -> x2, waiting for transfers between devices: 20.7 us -> 9.68 us  [exchange(): return lax.all_to_all(pieces, 'head', 0, 0, tiled=True)]
    unnamed x33 -> x32, local copies, waits for them, and re-layouts: 0.94 us -> 11.8 us
    pallas_call x0 -> x5, Pallas kernels: none -> 7.51 us  [the longest x1 2.35 us: body(): call(memory_kernel, [(memory.shape, BF16)], 4, scratch=[pltpu.VMEM((H, ba...]
    all_to_all x3 -> x2, starting transfers between devices: 11.6 us -> 7.56 us  [exchange(): return lax.all_to_all(pieces, 'head', 0, 0, tiled=True)]
    convert_element_type x3 -> x1, other arithmetic: 3.33 us -> 0.71 us  [body(): residual.astype(BF16)[None]]
    dot_general x6 -> x0, matrix products: 2.2 us -> none  [the longest x1 0.78 us: body(): jnp.einsum('bd,hkd->bhk', x_norm, w_query, preferred_element_type=jnp.flo...]
    convert_element_type x3 -> x0, local copies, waits for them, and re-layouts: 2.01 us -> none  [the longest x2 1.88 us: body(): value_heads = value_vec.astype(jnp.float32).reshape(batch_size, H, DV)]
    broadcast_in_dim x2 -> x1, local copies, waits for them, and re-layouts: 1.55 us -> 0.03 us  [body(): jnp.broadcast_to(residual.astype(BF16)[None], (count, batch, width))]
  transfers between devices with their start and end apart: 3 -> 2, of which waited for: 3 -> 2; matrix products, arithmetic and copies ran while one was open for 4% -> 0% of each run, Pallas kernels for 0% -> 7%
where the time goes in v1:
time: 68.1 us; the launch traced here: 67.2 us
  blocking collectives  29.2 us (43%)
  local copies, waits for them, and re-layouts  11.8 us (17%)
  waiting for transfers between devices  9.68 us (14%)
  starting transfers between devices  7.56 us (11%)
  Pallas kernels  7.51 us (11%)
  between operations  0.74 us (1%)
  other arithmetic  0.71 us (1%)
    all_to_all x2, blocking collectives, exchange(): return lax.all_to_all(pieces, 'head', 0, 0, tiled=True)  29.2 us
    unnamed x32, local copies, waits for them, and re-layouts  11.8 us
    all_to_all x2, waiting for transfers between devices, exchange(): return lax.all_to_all(pieces, 'head', 0, 0, tiled=True)  9.68 us
    all_to_all x2, starting transfers between devices, exchange(): return lax.all_to_all(pieces, 'head', 0, 0, tiled=True)  7.56 us
    pallas_call x1, Pallas kernels, body(): call(memory_kernel, [(memory.shape, BF16)], 4, scratch=[pltpu.VMEM((H, ba...  2.35 us
    pallas_call x1, Pallas kernels, body(): call(project_kernel, [((count, batch + STATS, width), BF16), piece, ((bat...  2.03 us
  transfers between devices with their start and end apart: 2, of which 2 were waited for; matrix products, arithmetic and copies ran while one was open for 0% of the time, Pallas kernels for 7%

profile of v1, /device:TPU:1, one launch (start us, length us, event | category | flops | bytes accessed | tf_op | source)
XLA Modules:
  0.0 67.2 jit_solution(7405364534680521534)
XLA Ops:
  0.6 0.7 %convert_element_type.3 = bf16[24,128]{1,0:T(8,128)(2,1)S(1)} convert(f32[24,128]{1,0:T(8,128)} %residual_ref.1) | non-fusion elementwise | flops 3072 | bytes 18432 | tf_op jit(solution)/shard_map/convert_element_type | solution.py:202
  1.4 16.6 %all_to_all.20.x_ref = bf16[32,24,128]{2,1,0:T(8,128)(2,1)S(1)} all-to-all(bf16[32,24,128]{2,1,0:T(8,128)(2,1)S(1)} %broadcast_in_dim.18), channel_id=1, replica_groups=mesh['dp'=8,'head'=32] {'head'}, dimensions={0} | all-to-all | bytes 393216 | tf_op jit(solution)/shard_map/all_to_all | solution.py:20
  18.0 0.0 copy-start
  18.0 1.4 %copy-done = bf16[24,8,8,512]{3,2,1,0:T(8,128)(2,1)S(1)} copy-done((bf16[24,8,8,512]{3,2,1,0:T(8,128)(2,1)S(1)}, bf16[24,8,8,512]{3,2,1,0:T(8,128)(2,1)}, u32[]{:S(2)}) %copy-start) | copy-done | bytes 1572888
  19.4 0.0 copy-start.4
  19.4 1.2 %copy-done.4 = bf16[4096,128]{1,0:T(8,128)(2,1)S(1)} copy-done((bf16[4096,128]{1,0:T(8,128)(2,1)S(1)}, bf16[4096,128]{1,0:T(8,128)(2,1)}, u32[]{:S(2)}) %copy-start.4) | copy-done | bytes 1048600
  20.6 0.0 copy-start.5
  20.6 1.0 %copy-done.5 = bf16[8,8,4096]{2,1,0:T(8,128)(2,1)S(1)} copy-done((bf16[8,8,4096]{2,1,0:T(8,128)(2,1)S(1)}, bf16[8,8,4096]{2,1,0:T(8,128)(2,1)}, u32[]{:S(2)}) %copy-start.5) | copy-done | bytes 524312
  21.7 0.0 copy-start.6
  21.7 1.0 %copy-done.6 = bf16[8,8,4096]{2,1,0:T(8,128)(2,1)S(1)} copy-done((bf16[8,8,4096]{2,1,0:T(8,128)(2,1)S(1)}, bf16[8,8,4096]{2,1,0:T(8,128)(2,1)}, u32[]{:S(2)}) %copy-start.6) | copy-done | bytes 524312
  22.7 0.0 copy-start.7
  22.7 0.8 %copy-done.7 = bf16[8,4096]{1,0:T(8,128)(2,1)S(1)} copy-done((bf16[8,4096]{1,0:T(8,128)(2,1)S(1)}, bf16[8,4096]{1,0:T(8,128)(2,1)}, u32[]{:S(2)}) %copy-start.7) | copy-done | bytes 65560
  23.5 0.0 copy-start.8
  23.6 0.8 %copy-done.8 = bf16[8,4096]{1,0:T(8,128)(2,1)S(1)} copy-done((bf16[8,4096]{1,0:T(8,128)(2,1)S(1)}, bf16[8,4096]{1,0:T(8,128)(2,1)}, u32[]{:S(2)}) %copy-start.8) | copy-done | bytes 65560
  24.4 0.0 copy-start.10
  24.4 0.8 %copy-done.10 = f32[24,8,8]{0,2,1:T(8,128)S(1)} copy-done((f32[24,8,8]{0,2,1:T(8,128)S(1)}, f32[24,8,8]{0,2,1:T(8,128)}, u32[]{:S(2)}) %copy-start.10) | copy-done | bytes 6168
  25.1 0.0 copy-start.11
  25.1 0.7 %copy-done.11 = f32[4096]{0:T(1024)S(1)} copy-done((f32[4096]{0:T(1024)S(1)}, f32[4096]{0:T(1024)}, u32[]{:S(2)}) %copy-start.11) | copy-done | bytes 16408
  25.9 0.0 copy-start.13
  25.9 0.7 %copy-done.13 = f32[24,8]{0,1:T(8,128)S(1)} copy-done((f32[24,8]{0,1:T(8,128)S(1)}, f32[24,8]{0,1:T(8,128)}, u32[]{:S(2)}) %copy-start.13) | copy-done | bytes 792
  26.6 0.0 copy-start.14
  26.6 0.7 copy-done.14
  27.2 0.0 copy-start.15
  27.2 0.7 copy-done.15
  27.9 2.0 %shard_map.165 = (bf16[32,32,128]{2,1,0:T(8,128)(2,1)S(1)}, bf16[32,24,128]{2,1,0:T(8,128)(2,1)}, bf16[24,4096]{1,0:T(8,128)(2,1)S(1)}, f32[64,24]{1,0:T(8,128)}...) custom-call(bf16[32,24,128]{2,1,0:T(8,128)(2,1)S(1)} %all_to_all.20., ...), custom_call_target="tpu_custom_call" | custom-call | flops 100000000 | bytes 2000000 | tf_op jit(solution)/shard_map/pallas_call | solution.py:206
  29.9 0.0 copy-start.2
  29.9 12.6 %all_to_all.21.in_ref = bf16[32,32,128]{2,1,0:T(8,128)(2,1)S(1)} all-to-all(bf16[32,32,128]{2,1,0:T(8,128)(2,1)S(1)} %get-tuple-element.16), channel_id=1, replica_groups=mesh['dp'=8,'head'=32] {'head'}, dimensions={0} | all-to-all | bytes 524288 | tf_op jit(solution)/shard_map/all_to_all | solution.py:20
  42.5 3.8 %all-to-all-start.3 = ((bf16[32,24,128]{2,1,0:T(8,128)(2,1)}), bf16[32,24,128]{2,1,0:T(8,128)(2,1)S(1)}, u32[]{:S(2)}, u32[]{:S(2)}) async-start(bf16[32,24,128]{2,1,0:T(8,128)(2,1)} %get-tuple-element.18.value_ref), calls=%async_computation.3 | async-start | bytes 393216 | tf_op jit(solution)/shard_map/all_to_all | solution.py:20
  46.3 0.0 copy-start.3
  46.3 1.2 %copy-done.3 = bf16[4096,128]{1,0:T(8,128)(2,1)S(1)} copy-done((bf16[4096,128]{1,0:T(8,128)(2,1)S(1)}, bf16[4096,128]{1,0:T(8,128)(2,1)}, u32[]{:S(2)}) %copy-start.3) | copy-done | bytes 1048600
  47.5 0.0 copy-start.12
  47.5 0.7 %copy-done.12 = f32[8,24]{1,0:T(8,128)S(1)} copy-done((f32[8,24]{1,0:T(8,128)S(1)}, f32[8,24]{1,0:T(8,128)}, u32[]{:S(2)}) %copy-start.12) | copy-done | bytes 792
  48.2 0.0 copy-start.1
  48.2 1.3 %shard_map.166 = (f32[24,128]{1,0:T(8,128)S(1)}, f32[24,128]{1,0:T(8,128)S(1)}, f32[24,128]{1,0:T(8,128)S(1)}) custom-call(s32[1]{0:T(128)} %bitcast.8.head_ref, bf16[24,4096]{1,0:T(8,128)(2,1)S(1)} %get-tuple-element.17.xn_ref, bf16[4096,128]{1,0:T(8,128)(2,1)S(1)} %copy-done.3, bf16[32,24,128]{2,1,0:T(8,128)(2,1)} %get-tuple-element.18.value_ref, ...), custom_call_target="tpu_custom_call" | custom-call | flops 30000000 | bytes 2000000 | tf_op jit(solution)/shard_map/pallas_call | solution.py:238
  49.5 0.0 copy-done.2
  49.6 1.2 %shard_map.167 = bf16[32,24,128]{2,1,0:T(8,128)(2,1)} custom-call(bf16[32,32,128]{2,1,0:T(8,128)(2,1)S(1)} %all_to_all.21.in_ref, f32[24,128]{1,0:T(8,128)S(1)} %get-tuple-element.22.sum_scale_ref, f32[24,128]{1,0:T(8,128)S(1)} %get-tuple-element.23.own_ref, f32[24,128]{1,0:T(8,128)S(1)} %get-tuple-element.24.floor_ref, bf16[128,4096]{1,0:T(8,128)(2,1)S(1)} %copy-done.2), custom_call_target="tpu_custom_call" | custom-call | flops 30000000 | bytes 2000000 | tf_op jit(solution)/shard_map/pallas_call | solution.py:241
  50.7 3.8 %all-to-all-done.3.value_ref = bf16[32,24,128]{2,1,0:T(8,128)(2,1)S(1)} async-done(((bf16[32,24,128]{2,1,0:T(8,128)(2,1)}), bf16[32,24,128]{2,1,0:T(8,128)(2,1)S(1)}, u32[]{:S(2)}, u32[]{:S(2)}) %all-to-all-start.3) | async-done | bytes 196640 | tf_op jit(solution)/shard_map/all_to_all | solution.py:20
  54.5 3.8 %all-to-all-start.2 = ((bf16[32,24,128]{2,1,0:T(8,128)(2,1)}), bf16[32,24,128]{2,1,0:T(8,128)(2,1)S(1)}, u32[]{:S(2)}, u32[]{:S(2)}) async-start(bf16[32,24,128]{2,1,0:T(8,128)(2,1)} %shard_map.167), calls=%async_computation.2 | async-start | bytes 393216 | tf_op jit(solution)/shard_map/all_to_all | solution.py:20
  58.4 0.0 copy-done.1
  58.4 0.0 copy-start.9
  58.4 2.4 %shard_map.169 = bf16[24,8,8,512]{3,2,1,0:T(8,128)(2,1)} custom-call(bf16[24,8,8,512]{3,2,1,0:T(8,128)(2,1)S(1)} %copy-done.1, bf16[32,24,128]{2,1,0:T(8,128)(2,1)S(1)} %all-to-all-done.3.value_ref, f32[64,24]{1,0:T(8,128)S(1)} %get-tuple-element.25.f_rows_ref, f32[64,24]{1,0:T(8,128)S(1)} %get-tuple-element.26.ik_rows_ref), custom_call_target="tpu_custom_call" | custom-call | flops 100000000 | bytes 2000000 | tf_op jit(solution)/shard_map/pallas_call | solution.py:245
  60.7 5.9 %all-to-all-done.2.in_ref = bf16[32,24,128]{2,1,0:T(8,128)(2,1)S(1)} async-done(((bf16[32,24,128]{2,1,0:T(8,128)(2,1)}), bf16[32,24,128]{2,1,0:T(8,128)(2,1)S(1)}, u32[]{:S(2)}, u32[]{:S(2)}) %all-to-all-start.2) | async-done | bytes 196640 | tf_op jit(solution)/shard_map/all_to_all | solution.py:20
  66.6 0.0 copy-done.9
  66.6 0.6 shard_map.168
  (1 shorter events, 0.0 us)
Async XLA Ops:
  18.0 1.4 %copy-start = (bf16[24,8,8,512]{3,2,1,0:T(8,128)(2,1)S(1)}, bf16[24,8,8,512]{3,2,1,0:T(8,128)(2,1)}, u32[]{:S(2)}) copy-start(bf16[24,8,8,512]{3,2,1,0:T(8,128)(2,1)} %mem_ref.3) | copy-start | bytes 4718596
  19.4 1.2 %copy-start.4 = (bf16[4096,128]{1,0:T(8,128)(2,1)S(1)}, bf16[4096,128]{1,0:T(8,128)(2,1)}, u32[]{:S(2)}) copy-start(bf16[4096,128]{1,0:T(8,128)(2,1)} %wv_ref.1) | copy-start | bytes 3145732
  20.6 1.0 %copy-start.5 = (bf16[8,8,4096]{2,1,0:T(8,128)(2,1)S(1)}, bf16[8,8,4096]{2,1,0:T(8,128)(2,1)}, u32[]{:S(2)}) copy-start(bf16[8,8,4096]{2,1,0:T(8,128)(2,1)} %param.16) | copy-start | bytes 1572868
  21.7 1.0 %copy-start.6 = (bf16[8,8,4096]{2,1,0:T(8,128)(2,1)S(1)}, bf16[8,8,4096]{2,1,0:T(8,128)(2,1)}, u32[]{:S(2)}) copy-start(bf16[8,8,4096]{2,1,0:T(8,128)(2,1)} %param.17) | copy-start | bytes 1572868
  22.7 0.8 %copy-start.7 = (bf16[8,4096]{1,0:T(8,128)(2,1)S(1)}, bf16[8,4096]{1,0:T(8,128)(2,1)}, u32[]{:S(2)}) copy-start(bf16[8,4096]{1,0:T(8,128)(2,1)} %wi_ref.1) | copy-start | bytes 196612
  23.5 0.8 %copy-start.8 = (bf16[8,4096]{1,0:T(8,128)(2,1)S(1)}, bf16[8,4096]{1,0:T(8,128)(2,1)}, u32[]{:S(2)}) copy-start(bf16[8,4096]{1,0:T(8,128)(2,1)} %wf_ref.1) | copy-start | bytes 196612
  24.4 0.8 %copy-start.10 = (f32[24,8,8]{0,2,1:T(8,128)S(1)}, f32[24,8,8]{0,2,1:T(8,128)}, u32[]{:S(2)}) copy-start(f32[24,8,8]{0,2,1:T(8,128)} %param.26) | copy-start | bytes 18436
  25.1 0.7 %copy-start.11 = (f32[4096]{0:T(1024)S(1)}, f32[4096]{0:T(1024)}, u32[]{:S(2)}) copy-start(f32[4096]{0:T(1024)} %param.15) | copy-start | bytes 49156
  25.9 0.7 %copy-start.13 = (f32[24,8]{0,1:T(8,128)S(1)}, f32[24,8]{0,1:T(8,128)}, u32[]{:S(2)}) copy-start(f32[24,8]{0,1:T(8,128)} %param.27) | copy-start | bytes 2308
  26.6 0.7 copy-start.14
  27.2 0.7 copy-start.15
  29.9 19.6 %copy-start.2 = (bf16[128,4096]{1,0:T(8,128)(2,1)S(1)}, bf16[128,4096]{1,0:T(8,128)(2,1)}, u32[]{:S(2)}) copy-start(bf16[128,4096]{1,0:T(8,128)(2,1)} %wo_ref.1) | copy-start | bytes 3145732
  42.5 12.0 %all-to-all-start.3 = ((bf16[32,24,128]{2,1,0:T(8,128)(2,1)}), bf16[32,24,128]{2,1,0:T(8,128)(2,1)S(1)}, u32[]{:S(2)}, u32[]{:S(2)}) async-start(bf16[32,24,128]{2,1,0:T(8,128)(2,1)} %get-tuple-element.18.value_ref), calls=%async_computation.3 | async-start | bytes 393216 | tf_op jit(solution)/shard_map/all_to_all | solution.py:20
  46.3 1.2 %copy-start.3 = (bf16[4096,128]{1,0:T(8,128)(2,1)S(1)}, bf16[4096,128]{1,0:T(8,128)(2,1)}, u32[]{:S(2)}) copy-start(bf16[4096,128]{1,0:T(8,128)(2,1)} %wg_ref.1) | copy-start | bytes 3145732
  47.5 0.7 %copy-start.12 = (f32[8,24]{1,0:T(8,128)S(1)}, f32[8,24]{1,0:T(8,128)}, u32[]{:S(2)}) copy-start(f32[8,24]{1,0:T(8,128)} %get-tuple-element.21.stab_ref) | copy-start | bytes 2308
  48.2 10.1 %copy-start.1 = (bf16[24,8,8,512]{3,2,1,0:T(8,128)(2,1)S(1)}, bf16[24,8,8,512]{3,2,1,0:T(8,128)(2,1)}, u32[]{:S(2)}) copy-start(bf16[24,8,8,512]{3,2,1,0:T(8,128)(2,1)} %mem_ref.3) | copy-start | bytes 4718596
  54.5 12.0 %all-to-all-start.2 = ((bf16[32,24,128]{2,1,0:T(8,128)(2,1)}), bf16[32,24,128]{2,1,0:T(8,128)(2,1)S(1)}, u32[]{:S(2)}, u32[]{:S(2)}) async-start(bf16[32,24,128]{2,1,0:T(8,128)(2,1)} %shard_map.167), calls=%async_computation.2 | async-start | bytes 393216 | tf_op jit(solution)/shard_map/all_to_all | solution.py:20
  58.4 8.2 %copy-start.9 = (f32[24,128]{1,0:T(8,128)S(1)}, f32[24,128]{1,0:T(8,128)}, u32[]{:S(2)}) copy-start(f32[24,128]{1,0:T(8,128)} %residual_ref.1) | copy-start | bytes 36868

commit v2 on v1

--- a/solution.py
+++ b/solution.py
@@ -40,11 +40,21 @@
     return high, value - high
 
 
+def fetch(sources, targets, sems):
+    copies = [pltpu.make_async_copy(s, t, sems.at[i]) for i, (s, t) in enumerate(zip(sources, targets))]
+    for copy in copies:
+        copy.start()
+    return copies
+
+
 def project_kernel(
-    x_ref, gain_ref, wq_ref, wk_ref, wv_ref, wi_ref, wf_ref, bi_ref, bf_ref, mem_ref, nrm_ref, stab_ref,
-    out_ref, value_ref, xn_ref, nrm_out_ref, stab_out_ref, fg_ref, ig_ref, f_rows_ref, ik_rows_ref,
-    stats_ref,
+    x_ref, gain_hbm, wi_hbm, wf_hbm, bi_hbm, bf_hbm, nrm_hbm, stab_hbm, wq_hbm, wk_hbm, mem_hbm,
+    out_ref, xn_ref, nrm_out_ref, stab_out_ref, fg_ref, ig_ref, f_rows_ref, ik_rows_ref,
+    stats_ref, gain_ref, wi_ref, wf_ref, bi_ref, bf_ref, nrm_ref, stab_ref, wq_ref, wk_ref, mem_ref, sems,
 ):
+    sources = (gain_hbm, wi_hbm, wf_hbm, bi_hbm, bf_hbm, nrm_hbm, stab_hbm, wq_hbm, wk_hbm, mem_hbm)
+    targets = (gain_ref, wi_ref, wf_ref, bi_ref, bf_ref, nrm_ref, stab_ref, wq_ref, wk_ref, mem_ref)
+    copies = fetch(sources, targets, sems)
     pieces, batch, width = x_ref.shape
     rows = wq_ref.shape[0] // H
     total = jnp.zeros((batch, width), F32)
@@ -53,20 +63,17 @@
         total = total + x * x
     mean = jnp.sum(total, axis=1, keepdims=True) / (pieces * width)
     scale = lax.rsqrt(mean + EPSILON)
+    stats_ref[...] = jnp.zeros(stats_ref.shape, F32)
+    copies[0].wait()
     for j in range(pieces):
         cut = slice(j * width, (j + 1) * width)
         xn_ref[:, cut] = (x_ref[j].astype(F32) * scale * gain_ref[:, cut]).astype(BF16)
     x_norm = xn_ref[...]
 
-    query = dot_last(x_norm, wq_ref[...])
-    query_t = dot_last(wq_ref[...], x_norm)
-    key_t = dot_last(wk_ref[...], x_norm) / math.sqrt(DK)
+    for copy in copies[1:7]:
+        copy.wait()
     input_pre = dot_last(wi_ref[...], x_norm) + column(bi_ref[...])
     forget_pre = dot_last(wf_ref[...], x_norm) + column(bf_ref[...])
-    value = dot(x_norm, wv_ref[...]).astype(BF16)
-    for j in range(pieces):
-        value_ref[j] = value
-
     log_forget = jnp.minimum(forget_pre, 0.0) - jnp.log1p(jnp.exp(-jnp.abs(forget_pre)))
     kept = log_forget + stab_ref[...]
     stab_new = jnp.maximum(kept, input_pre)
@@ -75,8 +82,12 @@
     stab_out_ref[...] = stab_new
     fg_ref[...] = forget_gate
     ig_ref[...] = input_gate
-
-    stats_ref[...] = jnp.zeros(stats_ref.shape, F32)
+    copies[7].wait()
+    query = dot_last(x_norm, wq_ref[...])
+    query_t = dot_last(wq_ref[...], x_norm)
+    copies[8].wait()
+    key_t = dot_last(wk_ref[...], x_norm) / math.sqrt(DK)
+
     for h in range(H):
         part = slice(h * rows, (h + 1) * rows)
         key_h = key_t[part]
@@ -103,6 +114,7 @@
     own_n = lax.broadcasted_iota(jnp.int32, (2 * batch, spread), 1) // rows
     own = own_b == own_n
     share = pieces // H
+    copies[9].wait()
     for h in range(H):
         wide = dot(both[:, h * rows : (h + 1) * rows], repeat)
         left = jnp.where(own, wide, 0.0).astype(BF16)
@@ -115,13 +127,25 @@
             out_ref[h * share + c, batch:] = stats
 
 
-def gate_kernel(head_ref, xn_ref, wg_ref, value_ref, fg_ref, ig_ref, stab_ref, sum_scale_ref, own_ref, floor_ref):
-    head = head_ref[0]
+def gate_kernel(
+    xn_ref, fg_ref, ig_ref, stab_ref, wv_hbm, wg_hbm,
+    values_ref, sum_scale_ref, own_ref, floor_ref,
+    wv_ref, wg_ref, sems,
+):
+    copies = fetch((wv_hbm, wg_hbm), (wv_ref, wg_ref), sems)
+    head = lax.axis_index("head") * xn_ref.shape[1] // lax.axis_size("head") // DV
     pick = lambda ref: column(ref[pl.ds(head, 1), :])
-    gate = jax.nn.sigmoid(dot(xn_ref[...], wg_ref[...]))
-    sum_scale_ref[...] = gate * pick(fg_ref)
-    own_ref[...] = gate * pick(ig_ref) * value_ref[0].astype(F32)
-    floor_ref[...] = jnp.broadcast_to(jnp.exp(-pick(stab_ref)), floor_ref.shape)
+    scales = [pick(ref) for ref in (fg_ref, ig_ref, stab_ref)]
+    floor_ref[...] = jnp.broadcast_to(jnp.exp(-scales[2]), floor_ref.shape)
+    x_norm = xn_ref[...]
+    copies[0].wait()
+    value = dot(x_norm, wv_ref[...]).astype(BF16)
+    for j in range(values_ref.shape[0]):
+        values_ref[j] = value
+    copies[1].wait()
+    gate = jax.nn.sigmoid(dot(x_norm, wg_ref[...]))
+    sum_scale_ref[...] = gate * scales[0]
+    own_ref[...] = gate * scales[1] * value.astype(F32)
 
 
 def output_kernel(in_ref, sum_scale_ref, own_ref, floor_ref, wo_ref, out_ref):
@@ -165,17 +189,25 @@
     out_ref[...] = total + acc
 
 
-def call(kernel, outs, n_in, scratch=(), smem=0, flops=1_000_000):
+def call(kernel, outs, n_in, n_hbm=0, scratch=(), flops=1_000_000):
     return pl.pallas_call(
         kernel,
         out_shape=[jax.ShapeDtypeStruct(*out) for out in outs],
-        in_specs=[pl.BlockSpec(memory_space=pltpu.SMEM)] * smem
-        + [pl.BlockSpec(memory_space=pltpu.VMEM)] * n_in,
+        in_specs=[pl.BlockSpec(memory_space=pltpu.VMEM)] * n_in
+        + [pl.BlockSpec(memory_space=pltpu.HBM)] * n_hbm,
         out_specs=[pl.BlockSpec(memory_space=pltpu.VMEM)] * len(outs),
         scratch_shapes=list(scratch),
         compiler_params=pltpu.CompilerParams(vmem_limit_bytes=16 * 2**20),
         cost_estimate=pl.CostEstimate(flops=flops, bytes_accessed=2_000_000, transcendentals=0),
     )
+
+
+def fetched(*arrays):
+    return [pltpu.VMEM(a.shape, a.dtype) for a in arrays] + [pltpu.SemaphoreType.DMA((len(arrays),))]
+
+
+def in_hbm(*arrays):
+    return [pltpu.with_memory_space_constraint(a, pltpu.HBM) for a in arrays]
 
 
 def body(
@@ -198,16 +230,25 @@
     batch, width = residual.shape
     rows = w_query.shape[1]
     features = count * width
-    head_mine = lax.axis_index("head") * width // DV
     gathered = exchange(jnp.broadcast_to(residual.astype(BF16)[None], (count, batch, width)))
 
-    norm_t = normalizer.transpose(1, 2, 0).reshape(H * rows, batch)
     piece = ((count, batch, width), BF16)
-    payload, values, x_norm, norm_new, stab_new, forget_gate, input_gate, f_rows, ik_rows = call(
+    sources = (
+        norm_gain[None],
+        w_input,
+        w_forget,
+        b_input[None],
+        b_forget[None],
+        normalizer.transpose(1, 2, 0).reshape(H * rows, batch),
+        stabilizer.T,
+        w_query.reshape(H * rows, features),
+        w_key.reshape(H * rows, features),
+        memory,
+    )
+    payload, x_norm, norm_new, stab_new, forget_gate, input_gate, f_rows, ik_rows = call(
         project_kernel,
         [
             ((count, batch + STATS, width), BF16),
-            piece,
             ((batch, features), BF16),
             ((H * rows, batch), F32),
             ((H, batch), F32),
@@ -216,28 +257,21 @@
             ((H * rows, batch), F32),
             ((H * rows, batch), F32),
         ],
-        12,
-        scratch=[pltpu.VMEM((H, STATS, width), F32)],
+        1,
+        len(sources),
+        scratch=[pltpu.VMEM((H, STATS, width), F32), *fetched(*sources)],
         flops=100_000_000,
-    )(
-        gathered,
-        norm_gain[None],
-        w_query.reshape(H * rows, features),
-        w_key.reshape(H * rows, features),
-        w_value,
-        w_input,
-        w_forget,
-        b_input[None],
-        b_forget[None],
-        memory,
-        norm_t,
-        stabilizer.T,
-    )
+    )(gathered, *in_hbm(*sources))
     arrived = exchange(payload)
+    values, sum_scale, own, floor = call(
+        gate_kernel,
+        [piece] + [((batch, width), F32)] * 3,
+        4,
+        2,
+        scratch=fetched(w_value, w_gate),
+        flops=100_000_000,
+    )(x_norm, forget_gate, input_gate, stab_new, *in_hbm(w_value, w_gate))
     value_heads = exchange(values)
-    sum_scale, own, floor = call(
-        gate_kernel, [((batch, width), F32)] * 3, 6, smem=1, flops=30_000_000
-    )(head_mine[None].astype(jnp.int32), x_norm, w_gate, values, forget_gate, input_gate, stab_new)
     (branch,) = call(output_kernel, [piece], 5, flops=30_000_000)(
         arrived, sum_scale, own, floor, w_out
     )

time: 68.1 us -> 60.3 us (0.89)
  blocking collectives: 29.2 us -> 16.6 us
  local copies, waits for them, and re-layouts: 11.8 us -> 0.73 us
  waiting for transfers between devices: 9.68 us -> 18.8 us
  starting transfers between devices: 7.56 us -> 11.5 us
  Pallas kernels: 7.51 us -> 10.5 us
    all_to_all x2 -> x1, blocking collectives: 29.2 us -> 16.6 us  [exchange(): return lax.all_to_all(pieces, 'head', 0, 0, tiled=True)]
    unnamed x32 -> x8, local copies, waits for them, and re-layouts: 11.8 us -> 0.7 us
    all_to_all x2 -> x3, waiting for transfers between devices: 9.68 us -> 18.8 us  [exchange(): return lax.all_to_all(pieces, 'head', 0, 0, tiled=True)]
    all_to_all x2 -> x3, starting transfers between devices: 7.56 us -> 11.5 us  [exchange(): return lax.all_to_all(pieces, 'head', 0, 0, tiled=True)]
    pallas_call x2, Pallas kernels: 3.35 us -> 6.36 us  [the longest x1 4.11 us: body(): call(project_kernel, [((count, batch + STATS, width), BF16), ((batch, fea...]
  transfers between devices with their start and end apart: 2 -> 3, of which waited for: 2 -> 3; matrix products, arithmetic and copies ran while one was open for 0% -> 0% of each run, Pallas kernels for 7% -> 10%
where the time goes in v2:
time: 60.3 us; the launch traced here: 59.7 us
  waiting for transfers between devices  18.8 us (31%)
  blocking collectives  16.6 us (28%)
  starting transfers between devices  11.5 us (19%)
  Pallas kernels  10.5 us (17%)
  local copies, waits for them, and re-layouts  0.73 us (1%)
  between operations  0.72 us (1%)
  other arithmetic  0.71 us (1%)
    all_to_all x3, waiting for transfers between devices, exchange(): return lax.all_to_all(pieces, 'head', 0, 0, tiled=True)  18.8 us
    all_to_all x1, blocking collectives, exchange(): return lax.all_to_all(pieces, 'head', 0, 0, tiled=True)  16.6 us
    all_to_all x3, starting transfers between devices, exchange(): return lax.all_to_all(pieces, 'head', 0, 0, tiled=True)  11.5 us
    pallas_call x1, Pallas kernels, body(): call(project_kernel, [((count, batch + STATS, width), BF16), ((batch, fea...  4.11 us
    pallas_call x1, Pallas kernels, body(): call(memory_kernel, [(memory.shape, BF16)], 4, scratch=[pltpu.VMEM((H, ba...  2.35 us
    pallas_call x1, Pallas kernels, body(): call(gate_kernel, [piece] + [((batch, width), F32)] * 3, 4, 2, scratch=fe...  2.25 us
  transfers between devices with their start and end apart: 3, of which 3 were waited for; matrix products, arithmetic and copies ran while one was open for 0% of the time, Pallas kernels for 10%

profile of v2, /device:TPU:1, one launch (start us, length us, event | category | flops | bytes accessed | tf_op | source)
XLA Modules:
  0.0 59.7 jit_solution(7103177447646775241)
XLA Ops:
  0.6 0.7 %convert_element_type.3 = bf16[24,128]{1,0:T(8,128)(2,1)S(1)} convert(f32[24,128]{1,0:T(8,128)} %residual_ref.1) | non-fusion elementwise | flops 3072 | bytes 18432 | tf_op jit(solution)/shard_map/convert_element_type | solution.py:233
  1.4 16.6 %all_to_all.20.x_ref = bf16[32,24,128]{2,1,0:T(8,128)(2,1)S(1)} all-to-all(bf16[32,24,128]{2,1,0:T(8,128)(2,1)S(1)} %broadcast_in_dim.15), channel_id=1, replica_groups=mesh['dp'=8,'head'=32] {'head'}, dimensions={0} | all-to-all | bytes 393216 | tf_op jit(solution)/shard_map/all_to_all | solution.py:20
  18.0 4.1 %shard_map.165 = (bf16[32,32,128]{2,1,0:T(8,128)(2,1)}, bf16[24,4096]{1,0:T(8,128)(2,1)S(1)}, f32[64,24]{1,0:T(8,128)}, f32[8,24]{1,0:T(8,128)}, f32[8,24]{1,0:T...) custom-call(bf16[32,24,128]{2,1,0:T(8,128)(2,1)S(1)} %all_to_all.20.x_ref, ...), custom_call_target="tpu_custom_call" | custom-call | flops 100000000 | bytes 2000000 | tf_op jit(solution)/shard_map/pallas_call | solution.py:248
  22.1 0.0 copy-start.1
  22.1 3.9 %all-to-all-start.1 = ((bf16[32,32,128]{2,1,0:T(8,128)(2,1)}), bf16[32,32,128]{2,1,0:T(8,128)(2,1)S(1)}, u32[]{:S(2)}, u32[]{:S(2)}) async-start(bf16[32,32,128]{2,1,0:T(8,128)(2,1)} %get-tuple-element.16), calls=%async_computation.1 | async-start | bytes 524288 | tf_op jit(solution)/shard_map/all_to_all | solution.py:20
  26.1 0.0 copy-start.3
  26.1 0.7 %copy-done.3 = f32[8,24]{1,0:T(8,128)S(1)} copy-done((f32[8,24]{1,0:T(8,128)S(1)}, f32[8,24]{1,0:T(8,128)}, u32[]{:S(2)}) %copy-start.3) | copy-done | bytes 792
  26.8 2.3 %shard_map.166 = (bf16[32,24,128]{2,1,0:T(8,128)(2,1)}, f32[24,128]{1,0:T(8,128)S(1)}, f32[24,128]{1,0:T(8,128)S(1)}, f32[24,128]{1,0:T(8,128)S(1)}) custom-call(bf16[24,4096]{1,0:T(8,128)(2,1)S(1)} %get-tuple-element.17.xn_ref, f32[8,24]{1,0:T(8,128)S(1)} %get-tuple-element.18.fg_ref, f32[8,24]{1,0:T(8,128)S(1)} %get-tuple-element.19.ig_ref, ...), custom_call_target="tpu_custom_call" | custom-call | flops 100000000 | bytes 2000000 | tf_op jit(solution)/shard_map/pallas_call | solution.py:266
  29.0 0.0 copy-start
  29.0 5.9 %all-to-all-done.1.in_ref = bf16[32,32,128]{2,1,0:T(8,128)(2,1)S(1)} async-done(((bf16[32,32,128]{2,1,0:T(8,128)(2,1)}), bf16[32,32,128]{2,1,0:T(8,128)(2,1)S(1)}, u32[]{:S(2)}, u32[]{:S(2)}) %all-to-all-start.1) | async-done | bytes 262176 | tf_op jit(solution)/shard_map/all_to_all | solution.py:20
  34.9 3.8 %all-to-all-start.3 = ((bf16[32,24,128]{2,1,0:T(8,128)(2,1)}), bf16[32,24,128]{2,1,0:T(8,128)(2,1)S(1)}, u32[]{:S(2)}, u32[]{:S(2)}) async-start(bf16[32,24,128]{2,1,0:T(8,128)(2,1)} %get-tuple-element.24), calls=%async_computation.3 | async-start | bytes 393216 | tf_op jit(solution)/shard_map/all_to_all | solution.py:20
  38.7 0.0 copy-done.1
  38.7 1.2 %shard_map.167 = bf16[32,24,128]{2,1,0:T(8,128)(2,1)} custom-call(bf16[32,32,128]{2,1,0:T(8,128)(2,1)S(1)} %all-to-all-done.1.in_ref, f32[24,128]{1,0:T(8,128)S(1)} %get-tuple-element.21.sum_scale_ref, f32[24,128]{1,0:T(8,128)S(1)} %get-tuple-element.22.own_ref, f32[24,128]{1,0:T(8,128)S(1)} %get-tuple-element.23.floor_ref, bf16[128,4096]{1,0:T(8,128)(2,1)S(1)} %copy-done.1), custom_call_target="tpu_custom_call" | custom-call | flops 30000000 | bytes 2000000 | tf_op jit(solution)/shard_map/pallas_call | solution.py:275
  39.9 7.1 %all-to-all-done.3.value_ref = bf16[32,24,128]{2,1,0:T(8,128)(2,1)S(1)} async-done(((bf16[32,24,128]{2,1,0:T(8,128)(2,1)}), bf16[32,24,128]{2,1,0:T(8,128)(2,1)S(1)}, u32[]{:S(2)}, u32[]{:S(2)}) %all-to-all-start.3) | async-done | bytes 196640 | tf_op jit(solution)/shard_map/all_to_all | solution.py:20
  47.0 3.8 %all-to-all-start.2 = ((bf16[32,24,128]{2,1,0:T(8,128)(2,1)}), bf16[32,24,128]{2,1,0:T(8,128)(2,1)S(1)}, u32[]{:S(2)}, u32[]{:S(2)}) async-start(bf16[32,24,128]{2,1,0:T(8,128)(2,1)} %shard_map.167), calls=%async_computation.2 | async-start | bytes 393216 | tf_op jit(solution)/shard_map/all_to_all | solution.py:20
  50.8 0.0 copy-done
  50.8 0.0 copy-start.2
  50.8 2.4 %shard_map.169 = bf16[24,8,8,512]{3,2,1,0:T(8,128)(2,1)} custom-call(bf16[24,8,8,512]{3,2,1,0:T(8,128)(2,1)S(1)} %copy-done, bf16[32,24,128]{2,1,0:T(8,128)(2,1)S(1)} %all-to-all-done.3.value_ref, f32[64,24]{1,0:T(8,128)S(1)} %get-tuple-element.25.f_rows_ref, f32[64,24]{1,0:T(8,128)S(1)} %get-tuple-element.26.ik_rows_ref), custom_call_target="tpu_custom_call" | custom-call | flops 100000000 | bytes 2000000 | tf_op jit(solution)/shard_map/pallas_call | solution.py:279
  53.2 5.9 %all-to-all-done.2.in_ref = bf16[32,24,128]{2,1,0:T(8,128)(2,1)S(1)} async-done(((bf16[32,24,128]{2,1,0:T(8,128)(2,1)}), bf16[32,24,128]{2,1,0:T(8,128)(2,1)S(1)}, u32[]{:S(2)}, u32[]{:S(2)}) %all-to-all-start.2) | async-done | bytes 196640 | tf_op jit(solution)/shard_map/all_to_all | solution.py:20
  59.0 0.0 copy-done.2
  59.0 0.6 %shard_map.168 = f32[24,128]{1,0:T(8,128)} custom-call(bf16[32,24,128]{2,1,0:T(8,128)(2,1)S(1)} %all-to-all-done.2.in_ref, f32[24,128]{1,0:T(8,128)S(1)} %copy-done.2), custom_call_target="tpu_custom_call" | custom-call | flops 1000000 | bytes 2000000 | tf_op jit(solution)/shard_map/pallas_call | solution.py:286
  (1 shorter events, 0.0 us)
Async XLA Ops:
  22.1 16.6 %copy-start.1 = (bf16[128,4096]{1,0:T(8,128)(2,1)S(1)}, bf16[128,4096]{1,0:T(8,128)(2,1)}, u32[]{:S(2)}) copy-start(bf16[128,4096]{1,0:T(8,128)(2,1)} %wo_ref.1) | copy-start | bytes 3145732
  22.1 12.8 %all-to-all-start.1 = ((bf16[32,32,128]{2,1,0:T(8,128)(2,1)}), bf16[32,32,128]{2,1,0:T(8,128)(2,1)S(1)}, u32[]{:S(2)}, u32[]{:S(2)}) async-start(bf16[32,32,128]{2,1,0:T(8,128)(2,1)} %get-tuple-element.16), calls=%async_computation.1 | async-start | bytes 524288 | tf_op jit(solution)/shard_map/all_to_all | solution.py:20
  26.1 0.7 %copy-start.3 = (f32[8,24]{1,0:T(8,128)S(1)}, f32[8,24]{1,0:T(8,128)}, u32[]{:S(2)}) copy-start(f32[8,24]{1,0:T(8,128)} %get-tuple-element.20.stab_ref) | copy-start | bytes 2308
  29.0 21.8 %copy-start = (bf16[24,8,8,512]{3,2,1,0:T(8,128)(2,1)S(1)}, bf16[24,8,8,512]{3,2,1,0:T(8,128)(2,1)}, u32[]{:S(2)}) copy-start(bf16[24,8,8,512]{3,2,1,0:T(8,128)(2,1)} %mem_ref.1) | copy-start | bytes 4718596
  34.9 12.0 %all-to-all-start.3 = ((bf16[32,24,128]{2,1,0:T(8,128)(2,1)}), bf16[32,24,128]{2,1,0:T(8,128)(2,1)S(1)}, u32[]{:S(2)}, u32[]{:S(2)}) async-start(bf16[32,24,128]{2,1,0:T(8,128)(2,1)} %get-tuple-element.24), calls=%async_computation.3 | async-start | bytes 393216 | tf_op jit(solution)/shard_map/all_to_all | solution.py:20
  47.0 12.0 %all-to-all-start.2 = ((bf16[32,24,128]{2,1,0:T(8,128)(2,1)}), bf16[32,24,128]{2,1,0:T(8,128)(2,1)S(1)}, u32[]{:S(2)}, u32[]{:S(2)}) async-start(bf16[32,24,128]{2,1,0:T(8,128)(2,1)} %shard_map.167), calls=%async_computation.2 | async-start | bytes 393216 | tf_op jit(solution)/shard_map/all_to_all | solution.py:20
  50.8 8.2 %copy-start.2 = (f32[24,128]{1,0:T(8,128)S(1)}, f32[24,128]{1,0:T(8,128)}, u32[]{:S(2)}) copy-start(f32[24,128]{1,0:T(8,128)} %residual_ref.1) | copy-start | bytes 36868

commit v3 on v2

--- a/solution.py
+++ b/solution.py
@@ -47,15 +47,30 @@
     return copies
 
 
+def prefetch_kernel(
+    gain_hbm, wi_hbm, wf_hbm, bi_hbm, bf_hbm, nrm_hbm, stab_hbm, wq_hbm, wk_hbm, mem_hbm,
+    gain_ref, wi_ref, wf_ref, bi_ref, bf_ref, nrm_ref, stab_ref, wq_ref, wk_ref, by_head_ref,
+    mem_ref, sems,
+):
+    sources = (mem_hbm, gain_hbm, wi_hbm, wf_hbm, bi_hbm, bf_hbm, nrm_hbm, stab_hbm, wq_hbm, wk_hbm)
+    targets = (mem_ref, gain_ref, wi_ref, wf_ref, bi_ref, bf_ref, nrm_ref, stab_ref, wq_ref, wk_ref)
+    copies = fetch(sources, targets, sems)
+    copies[0].wait()
+    for h in range(H):
+        by_head_ref[h] = mem_ref[:, h].astype(F32).reshape(by_head_ref.shape[1:]).astype(BF16)
+    for copy in copies[1:]:
+        copy.wait()
+
+
 def project_kernel(
-    x_ref, gain_hbm, wi_hbm, wf_hbm, bi_hbm, bf_hbm, nrm_hbm, stab_hbm, wq_hbm, wk_hbm, mem_hbm,
-    out_ref, xn_ref, nrm_out_ref, stab_out_ref, fg_ref, ig_ref, f_rows_ref, ik_rows_ref,
-    stats_ref, gain_ref, wi_ref, wf_ref, bi_ref, bf_ref, nrm_ref, stab_ref, wq_ref, wk_ref, mem_ref, sems,
+    x_ref, gain_ref, wi_ref, wf_ref, bi_ref, bf_ref, nrm_ref, stab_ref, wq_ref, wk_ref, by_head_ref,
+    wv_hbm, wg_hbm,
+    out_ref, nrm_out_ref, stab_out_ref, f_rows_ref, ik_rows_ref, sum_scale_ref, own_ref, floor_ref,
+    xn_ref, tail_ref, fg_ref, ig_ref, wv_ref, wg_ref, sems,
 ):
-    sources = (gain_hbm, wi_hbm, wf_hbm, bi_hbm, bf_hbm, nrm_hbm, stab_hbm, wq_hbm, wk_hbm, mem_hbm)
-    targets = (gain_ref, wi_ref, wf_ref, bi_ref, bf_ref, nrm_ref, stab_ref, wq_ref, wk_ref, mem_ref)
-    copies = fetch(sources, targets, sems)
+    copies = fetch((wv_hbm, wg_hbm), (wv_ref, wg_ref), sems)
     pieces, batch, width = x_ref.shape
+    half = batch // 2
     rows = wq_ref.shape[0] // H
     total = jnp.zeros((batch, width), F32)
     for j in range(pieces):
@@ -63,15 +78,15 @@
         total = total + x * x
     mean = jnp.sum(total, axis=1, keepdims=True) / (pieces * width)
     scale = lax.rsqrt(mean + EPSILON)
-    stats_ref[...] = jnp.zeros(stats_ref.shape, F32)
-    copies[0].wait()
+    tail_ref[...] = jnp.zeros(tail_ref.shape, F32)
     for j in range(pieces):
         cut = slice(j * width, (j + 1) * width)
         xn_ref[:, cut] = (x_ref[j].astype(F32) * scale * gain_ref[:, cut]).astype(BF16)
     x_norm = xn_ref[...]
 
-    for copy in copies[1:7]:
-        copy.wait()
+    query = dot_last(x_norm, wq_ref[...])
+    query_t = dot_last(wq_ref[...], x_norm)
+    key_t = dot_last(wk_ref[...], x_norm) / math.sqrt(DK)
     input_pre = dot_last(wi_ref[...], x_norm) + column(bi_ref[...])
     forget_pre = dot_last(wf_ref[...], x_norm) + column(bf_ref[...])
     log_forget = jnp.minimum(forget_pre, 0.0) - jnp.log1p(jnp.exp(-jnp.abs(forget_pre)))
@@ -82,11 +97,6 @@
     stab_out_ref[...] = stab_new
     fg_ref[...] = forget_gate
     ig_ref[...] = input_gate
-    copies[7].wait()
-    query = dot_last(x_norm, wq_ref[...])
-    query_t = dot_last(wq_ref[...], x_norm)
-    copies[8].wait()
-    key_t = dot_last(wk_ref[...], x_norm) / math.sqrt(DK)
 
     for h in range(H):
         part = slice(h * rows, (h + 1) * rows)
@@ -102,7 +112,8 @@
         key_query = jnp.sum(key_h * query_h, axis=0, keepdims=True)
         kinds = (*split_hi_lo(norm_query), *split_hi_lo(key_query))
         for k, kind in enumerate(kinds):
-            stats_ref[h, k : k + 1, :batch] = kind
+            for core in range(2):
+                tail_ref[core, h, 4 + k : 5 + k, :batch] = kind
 
     spread = batch * rows
     high, low = split_hi_lo(query)
@@ -114,60 +125,62 @@
     own_n = lax.broadcasted_iota(jnp.int32, (2 * batch, spread), 1) // rows
     own = own_b == own_n
     share = pieces // H
-    copies[9].wait()
     for h in range(H):
         wide = dot(both[:, h * rows : (h + 1) * rows], repeat)
         left = jnp.where(own, wide, 0.0).astype(BF16)
-        memory = mem_ref[:, h].astype(F32).reshape(spread, share * width).astype(BF16)
-        product = dot(left, memory)
+        product = dot(left, by_head_ref[h])
         numer = (product[:batch] + product[batch:]).astype(BF16)
-        stats = stats_ref[h].astype(BF16)
         for c in range(share):
             out_ref[h * share + c, :batch] = numer[:, c * width : (c + 1) * width]
-            out_ref[h * share + c, batch:] = stats
-
-
-def gate_kernel(
-    xn_ref, fg_ref, ig_ref, stab_ref, wv_hbm, wg_hbm,
-    values_ref, sum_scale_ref, own_ref, floor_ref,
-    wv_ref, wg_ref, sems,
-):
-    copies = fetch((wv_hbm, wg_hbm), (wv_ref, wg_ref), sems)
-    head = lax.axis_index("head") * xn_ref.shape[1] // lax.axis_size("head") // DV
+
+    copies[0].wait()
+    value = dot(x_norm, wv_ref[...])
+    for core in range(2):
+        first = value[core * half : core * half + 8].astype(BF16)
+        rest = value[core * half + 8 : (core + 1) * half]
+        for h in range(H):
+            tail_ref[core, h, :4] = rest
+        for j in range(core, pieces, 2):
+            out_ref[j, batch : batch + 8] = first
+            out_ref[j, batch + 8 :] = tail_ref[core, j // share].astype(BF16)
+
+    head = lax.axis_index("head") * width // DV
     pick = lambda ref: column(ref[pl.ds(head, 1), :])
-    scales = [pick(ref) for ref in (fg_ref, ig_ref, stab_ref)]
-    floor_ref[...] = jnp.broadcast_to(jnp.exp(-scales[2]), floor_ref.shape)
-    x_norm = xn_ref[...]
-    copies[0].wait()
-    value = dot(x_norm, wv_ref[...]).astype(BF16)
-    for j in range(values_ref.shape[0]):
-        values_ref[j] = value
     copies[1].wait()
     gate = jax.nn.sigmoid(dot(x_norm, wg_ref[...]))
-    sum_scale_ref[...] = gate * scales[0]
-    own_ref[...] = gate * scales[1] * value.astype(F32)
+    sum_scale_ref[...] = gate * pick(fg_ref)
+    own_ref[...] = gate * (pick(ig_ref) * value.astype(BF16).astype(F32))
+    floor_ref[...] = jnp.broadcast_to(jnp.exp(-pick(stab_out_ref)), floor_ref.shape)
 
 
 def output_kernel(in_ref, sum_scale_ref, own_ref, floor_ref, wo_ref, out_ref):
     pieces, batch, width = out_ref.shape
-    total = jnp.zeros(in_ref.shape[1:], F32)
-    for j in range(pieces):
-        total = total + in_ref[j].astype(F32)
-    norm_query = column(total[batch : batch + 1, :batch] + total[batch + 1 : batch + 2, :batch])
-    key_query = column(total[batch + 2 : batch + 3, :batch] + total[batch + 3 : batch + 4, :batch])
-    numer = sum_scale_ref[...] * total[:batch] + own_ref[...] * key_query
+    total = in_ref[0, :batch].astype(F32)
+    tail = in_ref[0, batch + 8 :].astype(F32)
+    for j in range(1, pieces):
+        total = total + in_ref[j, :batch].astype(F32)
+        tail = tail + in_ref[j, batch + 8 :].astype(F32)
+    norm_query = column(tail[4:5, :batch] + tail[5:6, :batch])
+    key_query = column(tail[6:7, :batch] + tail[7:8, :batch])
+    numer = sum_scale_ref[...] * total + own_ref[...] * key_query
     hidden = (numer / jnp.maximum(jnp.abs(norm_query), floor_ref[...])).astype(BF16)
     for j in range(pieces):
         out_ref[j] = dot(hidden, wo_ref[:, j * width : (j + 1) * width]).astype(BF16)
 
 
-def memory_kernel(mem_ref, value_ref, f_rows_ref, ik_rows_ref, out_ref, wide_ref):
-    pieces, batch, width = value_ref.shape
+def memory_kernel(f_rows_ref, ik_rows_ref, mine_ref, other_ref, mem_ref, out_ref, wide_ref):
+    pieces = mine_ref.shape[0]
+    batch, _, rows, _ = mem_ref.shape
+    width = mine_ref.shape[2]
+    half = batch // 2
     share = pieces // H
-    rows = mem_ref.shape[2]
+    even = lax.axis_index("head") % 2 == 0
     for j in range(pieces):
         cut = slice((j % share) * width, (j % share + 1) * width)
-        wide_ref[j // share, :, cut] = value_ref[j].astype(F32)
+        mine = mine_ref[j, batch : batch + 16].astype(F32)[:half]
+        other = other_ref[j].astype(F32)[:half]
+        wide_ref[j // share, :half, cut] = jnp.where(even, mine, other)
+        wide_ref[j // share, half:, cut] = jnp.where(even, other, mine)
 
     def one_head(h, carry):
         at = pl.multiple_of(h * rows, rows)
@@ -243,46 +256,57 @@
         stabilizer.T,
         w_query.reshape(H * rows, features),
         w_key.reshape(H * rows, features),
-        memory,
     )
-    payload, x_norm, norm_new, stab_new, forget_gate, input_gate, f_rows, ik_rows = call(
+    by_head = ((H, batch * rows, DV), BF16)
+    with jax.named_scope("prefetch"):
+        ready = call(
+            prefetch_kernel,
+            [*((a.shape, a.dtype) for a in sources), by_head],
+            0,
+            len(sources) + 1,
+            scratch=[
+                pltpu.VMEM(memory.shape, memory.dtype),
+                pltpu.SemaphoreType.DMA((len(sources) + 1,)),
+            ],
+            flops=100_000_000,
+        )(*in_hbm(*sources, memory))
+    payload, norm_new, stab_new, f_rows, ik_rows, sum_scale, own, floor = call(
         project_kernel,
         [
-            ((count, batch + STATS, width), BF16),
-            ((batch, features), BF16),
+            ((count, batch + batch // 2 + 4, width), BF16),
             ((H * rows, batch), F32),
-            ((H, batch), F32),
-            ((H, batch), F32),
             ((H, batch), F32),
             ((H * rows, batch), F32),
             ((H * rows, batch), F32),
+            ((batch, width), F32),
+            ((batch, width), F32),
+            ((batch, width), F32),
         ],
-        1,
-        len(sources),
-        scratch=[pltpu.VMEM((H, STATS, width), F32), *fetched(*sources)],
+        1 + len(ready),
+        2,
+        scratch=[
+            pltpu.VMEM((batch, features), BF16),
+            pltpu.VMEM((2, H, 8, width), F32),
+            pltpu.VMEM((H, batch), F32),
+            pltpu.VMEM((H, batch), F32),
+            *fetched(w_value, w_gate),
+        ],
         flops=100_000_000,
-    )(gathered, *in_hbm(*sources))
+    )(gathered, *ready, *in_hbm(w_value, w_gate))
     arrived = exchange(payload)
-    values, sum_scale, own, floor = call(
-        gate_kernel,
-        [piece] + [((batch, width), F32)] * 3,
-        4,
-        2,
-        scratch=fetched(w_value, w_gate),
-        flops=100_000_000,
-    )(x_norm, forget_gate, input_gate, stab_new, *in_hbm(w_value, w_gate))
-    value_heads = exchange(values)
     (branch,) = call(output_kernel, [piece], 5, flops=30_000_000)(
         arrived, sum_scale, own, floor, w_out
     )
     returned = exchange(branch)
+    with jax.named_scope("swap"):
+        other = lax.ppermute(arrived[:, batch:], "head", [(i, i ^ 1) for i in range(count)])
     (mem_new,) = call(
         memory_kernel,
         [(memory.shape, BF16)],
-        4,
+        5,
         scratch=[pltpu.VMEM((H, batch, DV), F32)],
         flops=100_000_000,
-    )(memory, value_heads, f_rows, ik_rows)
+    )(f_rows, ik_rows, arrived, other, memory)
     (res_out,) = call(finish_kernel, [((batch, width), F32)], 2)(returned, residual)
     norm_out = norm_new.reshape(H, rows, batch).transpose(2, 0, 1)
     return res_out, mem_new, norm_out, stab_new.T

time: 60.3 us -> 49.3 us (0.82)
  waiting for transfers between devices: 18.8 us -> 11.8 us
  blocking collectives: 16.6 us -> 13.2 us
  Pallas kernels: 10.5 us -> 8.96 us
  starting transfers between devices: 11.5 us -> 12.7 us
    all_to_all x3 -> x2, waiting for transfers between devices: 18.8 us -> 10.8 us  [exchange(): return lax.all_to_all(pieces, 'head', 0, 0, tiled=True)]
    all_to_all x1, blocking collectives: 16.6 us -> 13.2 us  [exchange(): return lax.all_to_all(pieces, 'head', 0, 0, tiled=True)]
    pallas_call x3, Pallas kernels: 8.71 us -> 7.14 us  [the longest x1 2.85 us: body(): call(project_kernel, [((count, batch + batch // 2 + 4, width), BF16), ((H...]
    ppermute x0 -> x1, waiting for transfers between devices: none -> 1 us  [body(): lax.ppermute(arrived[:, batch:], 'head', [(i, i ^ 1) for i in range(count)])]
    all_to_all x3 -> x2, starting transfers between devices: 11.5 us -> 12.3 us  [exchange(): return lax.all_to_all(pieces, 'head', 0, 0, tiled=True)]
    unnamed x8 -> x6, local copies, waits for them, and re-layouts: 0.7 us -> 0.01 us
    broadcast_in_dim x1, local copies, waits for them, and re-layouts: 0.03 us -> 0.7 us  [body(): jnp.broadcast_to(residual.astype(BF16)[None], (count, batch, width))]
  transfers between devices with their start and end apart: 3 -> 3, of which waited for: 3 -> 3; matrix products, arithmetic and copies ran while one was open for 0% -> 0% of each run, Pallas kernels for 10% -> 9%
where the time goes in v3:
time: 49.3 us; the launch traced here: 48.9 us
  blocking collectives  13.2 us (27%)
  starting transfers between devices  12.7 us (26%)
  waiting for transfers between devices  11.8 us (24%)
  Pallas kernels  8.96 us (18%)
  local copies, waits for them, and re-layouts  0.73 us (1%)
  other arithmetic  0.71 us (1%)
  between operations  0.68 us (1%)
    all_to_all x1, blocking collectives, exchange(): return lax.all_to_all(pieces, 'head', 0, 0, tiled=True)  13.2 us
    all_to_all x2, starting transfers between devices, exchange(): return lax.all_to_all(pieces, 'head', 0, 0, tiled=True)  12.3 us
    all_to_all x2, waiting for transfers between devices, exchange(): return lax.all_to_all(pieces, 'head', 0, 0, tiled=True)  10.8 us
    pallas_call x1, Pallas kernels, body(): call(project_kernel, [((count, batch + batch // 2 + 4, width), BF16), ((H...  2.85 us
    pallas_call x1, Pallas kernels, body(): call(memory_kernel, [(memory.shape, BF16)], 5, scratch=[pltpu.VMEM((H, ba...  2.4 us
    pallas_call x1, Pallas kernels, body(): call(prefetch_kernel, [*((a.shape, a.dtype) for a in sources), by_head],...  1.89 us
    pallas_call x1, Pallas kernels, body(): call(output_kernel, [piece], 5, flops=30000000)  1.17 us
    ppermute x1, waiting for transfers between devices, body(): lax.ppermute(arrived[:, batch:], 'head', [(i, i ^ 1) for i in range(count)])  1 us
  transfers between devices with their start and end apart: 3, of which 3 were waited for; matrix products, arithmetic and copies ran while one was open for 0% of the time, Pallas kernels for 9%

profile of v3, /device:TPU:1, one launch (start us, length us, event | category | flops | bytes accessed | tf_op | source)
XLA Modules:
  0.0 48.9 jit_solution(3917369930108325993)
XLA Ops:
  0.6 0.7 %convert_element_type.3 = bf16[24,128]{1,0:T(8,128)(2,1)S(1)} convert(f32[24,128]{1,0:T(8,128)} %residual_ref.1) | non-fusion elementwise | flops 3072 | bytes 18432 | tf_op jit(solution)/shard_map/convert_element_type | solution.py:246
  1.3 0.7 %broadcast_in_dim.15 = bf16[32,24,128]{2,1,0:T(8,128)(2,1)} broadcast(bf16[24,128]{1,0:T(8,128)(2,1)S(1)} %convert_element_type.3), dimensions={1,2} | broadcast | bytes 202752 | tf_op jit(solution)/shard_map/broadcast_in_dim | solution.py:246
  2.0 8.6 %all-to-all-start = ((bf16[32,24,128]{2,1,0:T(8,128)(2,1)}), bf16[32,24,128]{2,1,0:T(8,128)(2,1)S(1)}, u32[]{:S(2)}, u32[]{:S(2)}) async-start(bf16[32,24,128]{2,1,0:T(8,128)(2,1)} %broadcast_in_dim.15), calls=%async_computation | async-start | bytes 393216 | tf_op jit(solution)/shard_map/all_to_all | solution.py:20
  10.6 1.9 %prefetch.1 = (f32[1,4096]{1,0:T(1,128)S(1)}, bf16[8,4096]{1,0:T(8,128)(2,1)S(1)}, bf16[8,4096]{1,0:T(8,128)(2,1)S(1)}, f32[1,8]{1,0:T(1,128)S(1)}, f32[1,8]{1,0...) custom-call(f32[1,4096]{1,0:T(1,128)} %bitcast.16, ...), custom_call_target="tpu_custom_call" | custom-call | flops 100000000 | bytes 2000000 | tf_op jit(solution)/shard_map/prefetch/pallas_call | solution.py:262
  12.5 6.3 %all-to-all-done.x_ref = bf16[32,24,128]{2,1,0:T(8,128)(2,1)S(1)} async-done(((bf16[32,24,128]{2,1,0:T(8,128)(2,1)}), bf16[32,24,128]{2,1,0:T(8,128)(2,1)S(1)}, u32[]{:S(2)}, u32[]{:S(2)}) %all-to-all-start) | async-done | bytes 196640 | tf_op jit(solution)/shard_map/all_to_all | solution.py:20
  18.9 0.0 copy-start.1
  18.9 2.9 %shard_map.165 = (bf16[32,40,128]{2,1,0:T(8,128)(2,1)S(1)}, f32[64,24]{1,0:T(8,128)}, f32[8,24]{1,0:T(8,128)}, f32[64,24]{1,0:T(8,128)S(1)}, f32[64,24]{1,0:T(8,...) custom-call(bf16[32,24,128]{2,1,0:T(8,128)(2,1)S(1)} %all-to-all-done.x_ref, ...), custom_call_target="tpu_custom_call" | custom-call | flops 100000000 | bytes 2000000 | tf_op jit(solution)/shard_map/pallas_call | solution.py:273
  21.7 0.0 copy-start
  21.7 13.2 %all_to_all.15.in_ref.mine_ref = bf16[32,40,128]{2,1,0:T(8,128)(2,1)S(1)} all-to-all(bf16[32,40,128]{2,1,0:T(8,128)(2,1)S(1)} %get-tuple-element.32), channel_id=1, replica_groups=mesh['dp'=8,'head'=32] {'head'}, dimensions={0} | all-to-all | bytes 655360 | tf_op jit(solution)/shard_map/all_to_all | solution.py:20
  35.0 0.0 copy-done.1
  35.0 1.2 %shard_map.166 = bf16[32,24,128]{2,1,0:T(8,128)(2,1)} custom-call(bf16[32,40,128]{2,1,0:T(8,128)(2,1)S(1)} %all_to_all.15.in_ref.mine_ref, f32[24,128]{1,0:T(8,128)S(1)} %get-tuple-element.33.sum_scale_ref, f32[24,128]{1,0:T(8,128)S(1)} %get-tuple-element.34.own_ref, f32[24,128]{1,0:T(8,128)S(1)} %get-tuple-element.35.floor_ref, bf16[128,4096]{1,0:T(8,128)(2,1)S(1)} %copy-done.1), custom_call_target="tpu_custom_call" | custom-call | flops 30000000 | bytes 2000000 | tf_op jit(solution)/shard_map/pallas_call | solution.py:297
  36.2 3.7 %all-to-all-start.2 = ((bf16[32,24,128]{2,1,0:T(8,128)(2,1)}), bf16[32,24,128]{2,1,0:T(8,128)(2,1)S(1)}, u32[]{:S(2)}, u32[]{:S(2)}) async-start(bf16[32,24,128]{2,1,0:T(8,128)(2,1)} %shard_map.166), calls=%async_computation.2 | async-start | bytes 393216 | tf_op jit(solution)/shard_map/all_to_all | solution.py:20
  39.9 0.4 collective-permute-start
  40.4 1.0 %collective-permute-done.other_ref = bf16[32,16,128]{2,1,0:T(8,128)(2,1)S(1)} collective-permute-done((bf16[32,16,128]{2,1,0:T(8,128)(2,1)S(1)}, bf16[32,16,128]{2,1,0:T(8,128)(2,1)S(1)}, u32[]{:S(2)}, u32[]{:S(2)}) %collective-permute-start) | collective-permute-done | bytes 131104 | tf_op jit(solution)/shard_map/swap/ppermute | solution.py:302
  41.4 0.0 copy-done
  41.4 0.0 copy-start.2
  41.4 2.4 %shard_map.168 = bf16[24,8,8,512]{3,2,1,0:T(8,128)(2,1)} custom-call(f32[64,24]{1,0:T(8,128)S(1)} %get-tuple-element.36.f_rows_ref, f32[64,24]{1,0:T(8,128)S(1)} %get-tuple-element.37.ik_rows_ref, bf16[32,40,128]{2,1,0:T(8,128)(2,1)S(1)} %all_to_all.15.in_ref.mine_ref, bf16[32,16,128]{2,1,0:T(8,128)(2,1)S(1)} %collective-permute-done.other_ref, ...), custom_call_target="tpu_custom_call" | custom-call | flops 100000000 | bytes 2000000 | tf_op jit(solution)/shard_map/pallas_call | solution.py:303
  43.8 4.5 %all-to-all-done.2.in_ref = bf16[32,24,128]{2,1,0:T(8,128)(2,1)S(1)} async-done(((bf16[32,24,128]{2,1,0:T(8,128)(2,1)}), bf16[32,24,128]{2,1,0:T(8,128)(2,1)S(1)}, u32[]{:S(2)}, u32[]{:S(2)}) %all-to-all-start.2) | async-done | bytes 196640 | tf_op jit(solution)/shard_map/all_to_all | solution.py:20
  48.2 0.0 copy-done.2
  48.3 0.6 %shard_map.167 = f32[24,128]{1,0:T(8,128)} custom-call(bf16[32,24,128]{2,1,0:T(8,128)(2,1)S(1)} %all-to-all-done.2.in_ref, f32[24,128]{1,0:T(8,128)S(1)} %copy-done.2), custom_call_target="tpu_custom_call" | custom-call | flops 1000000 | bytes 2000000 | tf_op jit(solution)/shard_map/pallas_call | solution.py:310
  (1 shorter events, 0.0 us)
Async XLA Ops:
  2.0 16.8 %all-to-all-start = ((bf16[32,24,128]{2,1,0:T(8,128)(2,1)}), bf16[32,24,128]{2,1,0:T(8,128)(2,1)S(1)}, u32[]{:S(2)}, u32[]{:S(2)}) async-start(bf16[32,24,128]{2,1,0:T(8,128)(2,1)} %broadcast_in_dim.15), calls=%async_computation | async-start | bytes 393216 | tf_op jit(solution)/shard_map/all_to_all | solution.py:20
  18.9 16.1 %copy-start.1 = (bf16[128,4096]{1,0:T(8,128)(2,1)S(1)}, bf16[128,4096]{1,0:T(8,128)(2,1)}, u32[]{:S(2)}) copy-start(bf16[128,4096]{1,0:T(8,128)(2,1)} %wo_ref.1) | copy-start | bytes 3145732
  21.7 19.6 %copy-start = (bf16[24,8,8,512]{3,2,1,0:T(8,128)(2,1)S(1)}, bf16[24,8,8,512]{3,2,1,0:T(8,128)(2,1)}, u32[]{:S(2)}) copy-start(bf16[24,8,8,512]{3,2,1,0:T(8,128)(2,1)} %mem_ref.1) | copy-start | bytes 4718596
  36.2 12.1 %all-to-all-start.2 = ((bf16[32,24,128]{2,1,0:T(8,128)(2,1)}), bf16[32,24,128]{2,1,0:T(8,128)(2,1)S(1)}, u32[]{:S(2)}, u32[]{:S(2)}) async-start(bf16[32,24,128]{2,1,0:T(8,128)(2,1)} %shard_map.166), calls=%async_computation.2 | async-start | bytes 393216 | tf_op jit(solution)/shard_map/all_to_all | solution.py:20
  39.9 1.4 %collective-permute-start = (bf16[32,16,128]{2,1,0:T(8,128)(2,1)S(1)}, bf16[32,16,128]{2,1,0:T(8,128)(2,1)S(1)}, u32[]{:S(2)}, u32[]{:S(2)}) collective-permute-start(bf16[32,16,128]{2,1,0:T(8,128)(2,1)S(1)} %slice.4), channel_id=1, source_target_pairs={{0,1},{1,0},{2,3},{3,2},{4,5},{5,4},{6,7},{7,6},{8,9},{9,8},{10,11... | collective-permute-start | bytes 393224 | tf_op jit(solution)/shard_map/swap/ppermute | solution.py:302
  41.4 6.9 %copy-start.2 = (f32[24,128]{1,0:T(8,128)S(1)}, f32[24,128]{1,0:T(8,128)}, u32[]{:S(2)}) copy-start(f32[24,128]{1,0:T(8,128)} %residual_ref.1) | copy-start | bytes 36868

commit v4 on v3

--- a/solution.py
+++ b/solution.py
@@ -16,6 +16,9 @@
 STATS = 8
 
 
+SPREAD_FLOPS = 10_000_000_000
+
+
 def exchange(pieces):
     return lax.all_to_all(pieces, "head", 0, 0, tiled=True)
 
@@ -40,35 +43,17 @@
     return high, value - high
 
 
-def fetch(sources, targets, sems):
-    copies = [pltpu.make_async_copy(s, t, sems.at[i]) for i, (s, t) in enumerate(zip(sources, targets))]
-    for copy in copies:
-        copy.start()
-    return copies
-
-
-def prefetch_kernel(
-    gain_hbm, wi_hbm, wf_hbm, bi_hbm, bf_hbm, nrm_hbm, stab_hbm, wq_hbm, wk_hbm, mem_hbm,
-    gain_ref, wi_ref, wf_ref, bi_ref, bf_ref, nrm_ref, stab_ref, wq_ref, wk_ref, by_head_ref,
-    mem_ref, sems,
+def spread_kernel(in_ref, out_ref):
+    value = in_ref[...]
+    for j in range(out_ref.shape[0]):
+        out_ref[j] = value
+
+
+def project_kernel(
+    x_ref, gain_ref, wi_ref, wf_ref, bi_ref, bf_ref, nrm_ref, stab_ref, wq_ref, wk_ref, wv_ref, wg_ref, mem_ref,
+    out_ref, nrm_out_ref, stab_out_ref, f_rows_ref, ik_rows_ref, sum_scale_ref, own_ref, floor_ref,
+    xn_ref, tail_ref, fg_ref, ig_ref,
 ):
-    sources = (mem_hbm, gain_hbm, wi_hbm, wf_hbm, bi_hbm, bf_hbm, nrm_hbm, stab_hbm, wq_hbm, wk_hbm)
-    targets = (mem_ref, gain_ref, wi_ref, wf_ref, bi_ref, bf_ref, nrm_ref, stab_ref, wq_ref, wk_ref)
-    copies = fetch(sources, targets, sems)
-    copies[0].wait()
-    for h in range(H):
-        by_head_ref[h] = mem_ref[:, h].astype(F32).reshape(by_head_ref.shape[1:]).astype(BF16)
-    for copy in copies[1:]:
-        copy.wait()
-
-
-def project_kernel(
-    x_ref, gain_ref, wi_ref, wf_ref, bi_ref, bf_ref, nrm_ref, stab_ref, wq_ref, wk_ref, by_head_ref,
-    wv_hbm, wg_hbm,
-    out_ref, nrm_out_ref, stab_out_ref, f_rows_ref, ik_rows_ref, sum_scale_ref, own_ref, floor_ref,
-    xn_ref, tail_ref, fg_ref, ig_ref, wv_ref, wg_ref, sems,
-):
-    copies = fetch((wv_hbm, wg_hbm), (wv_ref, wg_ref), sems)
     pieces, batch, width = x_ref.shape
     half = batch // 2
     rows = wq_ref.shape[0] // H
@@ -128,12 +113,12 @@
     for h in range(H):
         wide = dot(both[:, h * rows : (h + 1) * rows], repeat)
         left = jnp.where(own, wide, 0.0).astype(BF16)
-        product = dot(left, by_head_ref[h])
+        by_head = mem_ref[:, h].astype(F32).reshape(spread, share * width).astype(BF16)
+        product = dot(left, by_head)
         numer = (product[:batch] + product[batch:]).astype(BF16)
         for c in range(share):
             out_ref[h * share + c, :batch] = numer[:, c * width : (c + 1) * width]
 
-    copies[0].wait()
     value = dot(x_norm, wv_ref[...])
     for core in range(2):
         first = value[core * half : core * half + 8].astype(BF16)
@@ -146,7 +131,6 @@
 
     head = lax.axis_index("head") * width // DV
     pick = lambda ref: column(ref[pl.ds(head, 1), :])
-    copies[1].wait()
     gate = jax.nn.sigmoid(dot(x_norm, wg_ref[...]))
     sum_scale_ref[...] = gate * pick(fg_ref)
     own_ref[...] = gate * (pick(ig_ref) * value.astype(BF16).astype(F32))
@@ -168,7 +152,12 @@
         out_ref[j] = dot(hidden, wo_ref[:, j * width : (j + 1) * width]).astype(BF16)
 
 
-def memory_kernel(f_rows_ref, ik_rows_ref, mine_ref, other_ref, mem_ref, out_ref, wide_ref):
+def memory_kernel(
+    f_rows_ref, ik_rows_ref, norm_ref, stab_ref, mine_ref, other_ref, mem_ref,
+    out_ref, norm_out_ref, stab_out_ref, wide_ref,
+):
+    norm_out_ref[...] = norm_ref[...]
+    stab_out_ref[...] = stab_ref[...]
     pieces = mine_ref.shape[0]
     batch, _, rows, _ = mem_ref.shape
     width = mine_ref.shape[2]
@@ -202,25 +191,16 @@
     out_ref[...] = total + acc
 
 
-def call(kernel, outs, n_in, n_hbm=0, scratch=(), flops=1_000_000):
+def call(kernel, outs, n_in, scratch=(), flops=1_000_000):
     return pl.pallas_call(
         kernel,
         out_shape=[jax.ShapeDtypeStruct(*out) for out in outs],
-        in_specs=[pl.BlockSpec(memory_space=pltpu.VMEM)] * n_in
-        + [pl.BlockSpec(memory_space=pltpu.HBM)] * n_hbm,
+        in_specs=[pl.BlockSpec(memory_space=pltpu.VMEM)] * n_in,
         out_specs=[pl.BlockSpec(memory_space=pltpu.VMEM)] * len(outs),
         scratch_shapes=list(scratch),
         compiler_params=pltpu.CompilerParams(vmem_limit_bytes=16 * 2**20),
         cost_estimate=pl.CostEstimate(flops=flops, bytes_accessed=2_000_000, transcendentals=0),
     )
-
-
-def fetched(*arrays):
-    return [pltpu.VMEM(a.shape, a.dtype) for a in arrays] + [pltpu.SemaphoreType.DMA((len(arrays),))]
-
-
-def in_hbm(*arrays):
-    return [pltpu.with_memory_space_constraint(a, pltpu.HBM) for a in arrays]
 
 
 def body(
@@ -243,7 +223,10 @@
     batch, width = residual.shape
     rows = w_query.shape[1]
     features = count * width
-    gathered = exchange(jnp.broadcast_to(residual.astype(BF16)[None], (count, batch, width)))
+    (pieces,) = call(spread_kernel, [((count, batch, width), BF16)], 1, flops=SPREAD_FLOPS)(
+        residual.astype(BF16)
+    )
+    gathered = exchange(pieces)
 
     piece = ((count, batch, width), BF16)
     sources = (
@@ -256,20 +239,10 @@
         stabilizer.T,
         w_query.reshape(H * rows, features),
         w_key.reshape(H * rows, features),
-    )
-    by_head = ((H, batch * rows, DV), BF16)
-    with jax.named_scope("prefetch"):
-        ready = call(
-            prefetch_kernel,
-            [*((a.shape, a.dtype) for a in sources), by_head],
-            0,
-            len(sources) + 1,
-            scratch=[
-                pltpu.VMEM(memory.shape, memory.dtype),
-                pltpu.SemaphoreType.DMA((len(sources) + 1,)),
-            ],
-            flops=100_000_000,
-        )(*in_hbm(*sources, memory))
+        w_value,
+        w_gate,
+        memory,
+    )
     payload, norm_new, stab_new, f_rows, ik_rows, sum_scale, own, floor = call(
         project_kernel,
         [
@@ -282,17 +255,15 @@
             ((batch, width), F32),
             ((batch, width), F32),
         ],
-        1 + len(ready),
-        2,
+        1 + len(sources),
         scratch=[
             pltpu.VMEM((batch, features), BF16),
             pltpu.VMEM((2, H, 8, width), F32),
             pltpu.VMEM((H, batch), F32),
             pltpu.VMEM((H, batch), F32),
-            *fetched(w_value, w_gate),
         ],
         flops=100_000_000,
-    )(gathered, *ready, *in_hbm(w_value, w_gate))
+    )(gathered, *sources)
     arrived = exchange(payload)
     (branch,) = call(output_kernel, [piece], 5, flops=30_000_000)(
         arrived, sum_scale, own, floor, w_out
@@ -300,16 +271,16 @@
     returned = exchange(branch)
     with jax.named_scope("swap"):
         other = lax.ppermute(arrived[:, batch:], "head", [(i, i ^ 1) for i in range(count)])
-    (mem_new,) = call(
+    mem_new, norm_out, stab_out = call(
         memory_kernel,
-        [(memory.shape, BF16)],
-        5,
+        [(memory.shape, BF16), ((H * rows, batch), F32), ((H, batch), F32)],
+        7,
         scratch=[pltpu.VMEM((H, batch, DV), F32)],
         flops=100_000_000,
-    )(f_rows, ik_rows, arrived, other, memory)
+    )(f_rows, ik_rows, norm_new, stab_new, arrived, other, memory)
     (res_out,) = call(finish_kernel, [((batch, width), F32)], 2)(returned, residual)
-    norm_out = norm_new.reshape(H, rows, batch).transpose(2, 0, 1)
-    return res_out, mem_new, norm_out, stab_new.T
+    norm_out = norm_out.reshape(H, rows, batch).transpose(2, 0, 1)
+    return res_out, mem_new, norm_out, stab_out.T
 
 
 def solution(mesh):

time: 49.3 us -> 48.2 us (0.978)
  blocking collectives: 13.2 us -> 30 us
  starting transfers between devices: 12.7 us -> 4.29 us
  waiting for transfers between devices: 11.8 us -> 5.48 us
  Pallas kernels: 8.96 us -> 6.52 us
  local copies, waits for them, and re-layouts: 0.73 us -> 0.09 us
    all_to_all x1 -> x2, blocking collectives: 13.2 us -> 30 us  [exchange(): return lax.all_to_all(pieces, 'head', 0, 0, tiled=True)]
    all_to_all x2 -> x1, starting transfers between devices: 12.3 us -> 3.86 us  [exchange(): return lax.all_to_all(pieces, 'head', 0, 0, tiled=True)]
    all_to_all x2 -> x1, waiting for transfers between devices: 10.8 us -> 4.49 us  [exchange(): return lax.all_to_all(pieces, 'head', 0, 0, tiled=True)]
    pallas_call x2, Pallas kernels: 4.29 us -> 2.44 us  [the longest x1 2.41 us: body(): call(memory_kernel, [(memory.shape, BF16), ((H * rows, batch), F32), ((H,...]
    broadcast_in_dim x1 -> x0, local copies, waits for them, and re-layouts: 0.7 us -> none  [body(): jnp.broadcast_to(residual.astype(BF16)[None], (count, batch, width))]
    pallas_call x1, Pallas kernels: 2.85 us -> 2.25 us  [body(): call(project_kernel, [((count, batch + batch // 2 + 4, width), BF16), ((H...]
  transfers between devices with their start and end apart: 3 -> 2, of which waited for: 3 -> 2; matrix products, arithmetic and copies ran while one was open for 0% -> 0% of each run, Pallas kernels for 9% -> 5%
where the time goes in v4:
time: 48.2 us; the launch traced here: 47.9 us
  blocking collectives  30 us (62%)
  Pallas kernels  6.52 us (14%)
  waiting for transfers between devices  5.48 us (11%)
  starting transfers between devices  4.29 us (9%)
  between operations  0.83 us (2%)
  other arithmetic  0.71 us (1%)
    all_to_all x2, blocking collectives, exchange(): return lax.all_to_all(pieces, 'head', 0, 0, tiled=True)  30 us
    all_to_all x1, waiting for transfers between devices, exchange(): return lax.all_to_all(pieces, 'head', 0, 0, tiled=True)  4.49 us
    all_to_all x1, starting transfers between devices, exchange(): return lax.all_to_all(pieces, 'head', 0, 0, tiled=True)  3.86 us
    pallas_call x1, Pallas kernels, body(): call(memory_kernel, [(memory.shape, BF16), ((H * rows, batch), F32), ((H,...  2.41 us
    pallas_call x1, Pallas kernels, body(): call(project_kernel, [((count, batch + batch // 2 + 4, width), BF16), ((H...  2.25 us
    pallas_call x1, Pallas kernels, body(): call(output_kernel, [piece], 5, flops=30000000)  1.19 us
    ppermute x1, waiting for transfers between devices, body(): lax.ppermute(arrived[:, batch:], 'head', [(i, i ^ 1) for i in range(count)])  1 us
  transfers between devices with their start and end apart: 2, of which 2 were waited for; matrix products, arithmetic and copies ran while one was open for 0% of the time, Pallas kernels for 5%

profile of v4, /device:TPU:1, one launch (start us, length us, event | category | flops | bytes accessed | tf_op | source)
XLA Modules:
  0.0 47.9 jit_solution(16066398780478144525)
XLA Ops:
  0.6 0.7 %convert_element_type.3.in_ref = bf16[24,128]{1,0:T(8,128)(2,1)S(1)} convert(f32[24,128]{1,0:T(8,128)} %residual_ref.1) | non-fusion elementwise | flops 3072 | bytes 18432 | tf_op jit(solution)/shard_map/convert_element_type | solution.py:227
  1.3 0.0 copy-start
  1.3 0.0 copy-start.1
  1.3 0.0 copy-start.2
  1.4 0.0 copy-start.4
  1.4 0.0 copy-start.5
  1.4 0.0 copy-start.6
  1.4 0.0 copy-start.7
  1.4 0.0 copy-start.9
  1.4 0.0 copy-start.10
  1.4 0.0 copy-start.11
  1.4 0.0 copy-start.12
  1.4 0.0 copy-start.13
  1.5 16.9 %all_to_all.15.x_ref = bf16[32,24,128]{2,1,0:T(8,128)(2,1)S(1)} all-to-all(bf16[32,24,128]{2,1,0:T(8,128)(2,1)S(1)} %shard_map.165), channel_id=1, replica_groups=mesh['dp'=8,'head'=32] {'head'}, dimensions={0} | all-to-all | bytes 393216 | tf_op jit(solution)/shard_map/all_to_all | solution.py:23
  18.4 0.0 copy-done
  18.4 0.0 copy-done.1
  18.4 0.0 copy-done.2
  18.4 0.0 copy-done.4
  18.4 0.0 copy-done.5
  18.4 0.0 copy-done.6
  18.4 0.0 copy-done.7
  18.4 0.0 copy-done.9
  18.4 0.0 copy-done.10
  18.4 0.0 copy-done.11
  18.5 0.0 copy-done.12
  18.5 0.0 copy-done.13
  18.5 0.0 copy-start.3
  18.5 2.3 %shard_map.166 = (bf16[32,40,128]{2,1,0:T(8,128)(2,1)S(1)}, f32[64,24]{1,0:T(8,128)S(1)}, f32[8,24]{1,0:T(8,128)S(1)}, f32[64,24]{1,0:T(8,128)S(1)}, f32[64,24]{...) custom-call(bf16[32,24,128]{2,1,0:T(8,128)(2,1)S(1)} %all_to_all.15.x_ref, ...), custom_call_target="tpu_custom_call" | custom-call | flops 100000000 | bytes 2000000 | tf_op jit(solution)/shard_map/pallas_call | solution.py:246
  20.7 13.1 %all_to_all.16.in_ref.mine_ref = bf16[32,40,128]{2,1,0:T(8,128)(2,1)S(1)} all-to-all(bf16[32,40,128]{2,1,0:T(8,128)(2,1)S(1)} %get-tuple-element.15), channel_id=1, replica_groups=mesh['dp'=8,'head'=32] {'head'}, dimensions={0} | all-to-all | bytes 655360 | tf_op jit(solution)/shard_map/all_to_all | solution.py:23
  33.9 0.0 copy-done.3
  33.9 1.2 %shard_map.167 = bf16[32,24,128]{2,1,0:T(8,128)(2,1)} custom-call(bf16[32,40,128]{2,1,0:T(8,128)(2,1)S(1)} %all_to_all.16.in_ref.mine_ref, f32[24,128]{1,0:T(8,128)S(1)} %get-tuple-element.16.sum_scale_ref, f32[24,128]{1,0:T(8,128)S(1)} %get-tuple-element.17.own_ref, f32[24,128]{1,0:T(8,128)S(1)} %get-tuple-element.18.floor_ref, bf16[128,4096]{1,0:T(8,128)(2,1)S(1)} %copy-done.3), custom_call_target="tpu_custom_call" | custom-call | flops 30000000 | bytes 2000000 | tf_op jit(solution)/shard_map/pallas_call | solution.py:268
  35.0 0.0 copy-start.8
  35.0 3.9 %all-to-all-start.2 = ((bf16[32,24,128]{2,1,0:T(8,128)(2,1)}), bf16[32,24,128]{2,1,0:T(8,128)(2,1)S(1)}, u32[]{:S(2)}, u32[]{:S(2)}) async-start(bf16[32,24,128]{2,1,0:T(8,128)(2,1)} %shard_map.167), calls=%async_computation.2 | async-start | bytes 393216 | tf_op jit(solution)/shard_map/all_to_all | solution.py:23
  38.9 0.4 collective-permute-start
  39.4 1.0 %collective-permute-done.other_ref = bf16[32,16,128]{2,1,0:T(8,128)(2,1)S(1)} collective-permute-done((bf16[32,16,128]{2,1,0:T(8,128)(2,1)S(1)}, bf16[32,16,128]{2,1,0:T(8,128)(2,1)S(1)}, u32[]{:S(2)}, u32[]{:S(2)}) %collective-permute-start) | collective-permute-done | bytes 131104 | tf_op jit(solution)/shard_map/swap/ppermute | solution.py:273
  40.4 2.4 %shard_map.169 = (bf16[24,8,8,512]{3,2,1,0:T(8,128)(2,1)}, f32[64,24]{1,0:T(8,128)}, f32[8,24]{1,0:T(8,128)}) custom-call(f32[64,24]{1,0:T(8,128)S(1)} %get-tuple-element.19.f_rows_ref, f32[64,24]{1,0:T(8,128)S(1)} %get-tuple-element.20.ik_rows_ref, f32[64,24]{1,0:T(8,128)S(1)} %get-tuple-element.21.norm_ref, f32[8,24]{1,0:T(8,128)S(1)} %get-tuple-element.22.stab_ref, ...), custom_call_target="tpu_custom_call" | custom-call | flops 100000000 | bytes 2000000 | tf_op jit(solution)/shard_map/pallas_call | solution.py:274
  42.8 4.5 %all-to-all-done.2.in_ref = bf16[32,24,128]{2,1,0:T(8,128)(2,1)S(1)} async-done(((bf16[32,24,128]{2,1,0:T(8,128)(2,1)}), bf16[32,24,128]{2,1,0:T(8,128)(2,1)S(1)}, u32[]{:S(2)}, u32[]{:S(2)}) %all-to-all-start.2) | async-done | bytes 196640 | tf_op jit(solution)/shard_map/all_to_all | solution.py:23
  47.3 0.0 copy-done.8
  47.3 0.6 %shard_map.168 = f32[24,128]{1,0:T(8,128)} custom-call(bf16[32,24,128]{2,1,0:T(8,128)(2,1)S(1)} %all-to-all-done.2.in_ref, f32[24,128]{1,0:T(8,128)S(1)} %copy-done.8), custom_call_target="tpu_custom_call" | custom-call | flops 1000000 | bytes 2000000 | tf_op jit(solution)/shard_map/pallas_call | solution.py:281
  (2 shorter events, 0.0 us)
Async XLA Ops:
  1.3 17.0 %copy-start = (bf16[24,8,8,512]{3,2,1,0:T(8,128)(2,1)S(1)}, bf16[24,8,8,512]{3,2,1,0:T(8,128)(2,1)}, u32[]{:S(2)}) copy-start(bf16[24,8,8,512]{3,2,1,0:T(8,128)(2,1)} %mem_ref.3) | copy-start | bytes 4718596
  1.3 17.0 %copy-start.1 = (bf16[4096,128]{1,0:T(8,128)(2,1)S(1)}, bf16[4096,128]{1,0:T(8,128)(2,1)}, u32[]{:S(2)}) copy-start(bf16[4096,128]{1,0:T(8,128)(2,1)} %wv_ref.1) | copy-start | bytes 3145732
  1.3 17.0 %copy-start.2 = (bf16[4096,128]{1,0:T(8,128)(2,1)S(1)}, bf16[4096,128]{1,0:T(8,128)(2,1)}, u32[]{:S(2)}) copy-start(bf16[4096,128]{1,0:T(8,128)(2,1)} %wg_ref.1) | copy-start | bytes 3145732
  1.4 17.0 %copy-start.4 = (bf16[8,8,4096]{2,1,0:T(8,128)(2,1)S(1)}, bf16[8,8,4096]{2,1,0:T(8,128)(2,1)}, u32[]{:S(2)}) copy-start(bf16[8,8,4096]{2,1,0:T(8,128)(2,1)} %param.16) | copy-start | bytes 1572868
  1.4 17.0 %copy-start.5 = (bf16[8,8,4096]{2,1,0:T(8,128)(2,1)S(1)}, bf16[8,8,4096]{2,1,0:T(8,128)(2,1)}, u32[]{:S(2)}) copy-start(bf16[8,8,4096]{2,1,0:T(8,128)(2,1)} %param.17) | copy-start | bytes 1572868
  1.4 17.0 %copy-start.6 = (bf16[8,4096]{1,0:T(8,128)(2,1)S(1)}, bf16[8,4096]{1,0:T(8,128)(2,1)}, u32[]{:S(2)}) copy-start(bf16[8,4096]{1,0:T(8,128)(2,1)} %wi_ref.1) | copy-start | bytes 196612
  1.4 17.0 %copy-start.7 = (bf16[8,4096]{1,0:T(8,128)(2,1)S(1)}, bf16[8,4096]{1,0:T(8,128)(2,1)}, u32[]{:S(2)}) copy-start(bf16[8,4096]{1,0:T(8,128)(2,1)} %wf_ref.1) | copy-start | bytes 196612
  1.4 17.0 %copy-start.9 = (f32[24,8,8]{0,2,1:T(8,128)S(1)}, f32[24,8,8]{0,2,1:T(8,128)}, u32[]{:S(2)}) copy-start(f32[24,8,8]{0,2,1:T(8,128)} %param.26) | copy-start | bytes 18436
  1.4 17.0 %copy-start.10 = (f32[4096]{0:T(1024)S(1)}, f32[4096]{0:T(1024)}, u32[]{:S(2)}) copy-start(f32[4096]{0:T(1024)} %param.15) | copy-start | bytes 49156
  1.4 17.0 %copy-start.11 = (f32[24,8]{0,1:T(8,128)S(1)}, f32[24,8]{0,1:T(8,128)}, u32[]{:S(2)}) copy-start(f32[24,8]{0,1:T(8,128)} %param.27) | copy-start | bytes 2308
  1.4 17.0 %copy-start.12 = (f32[8]{0:T(128)S(1)}, f32[8]{0:T(128)}, u32[]{:S(2)}) copy-start(f32[8]{0:T(128)} %param.22) | copy-start | bytes 100
  1.4 17.0 %copy-start.13 = (f32[8]{0:T(128)S(1)}, f32[8]{0:T(128)}, u32[]{:S(2)}) copy-start(f32[8]{0:T(128)} %param.23) | copy-start | bytes 100
  18.5 15.4 %copy-start.3 = (bf16[128,4096]{1,0:T(8,128)(2,1)S(1)}, bf16[128,4096]{1,0:T(8,128)(2,1)}, u32[]{:S(2)}) copy-start(bf16[128,4096]{1,0:T(8,128)(2,1)} %wo_ref.1) | copy-start | bytes 3145732
  35.0 12.2 %copy-start.8 = (f32[24,128]{1,0:T(8,128)S(1)}, f32[24,128]{1,0:T(8,128)}, u32[]{:S(2)}) copy-start(f32[24,128]{1,0:T(8,128)} %residual_ref.1) | copy-start | bytes 36868
  35.0 12.2 %all-to-all-start.2 = ((bf16[32,24,128]{2,1,0:T(8,128)(2,1)}), bf16[32,24,128]{2,1,0:T(8,128)(2,1)S(1)}, u32[]{:S(2)}, u32[]{:S(2)}) async-start(bf16[32,24,128]{2,1,0:T(8,128)(2,1)} %shard_map.167), calls=%async_computation.2 | async-start | bytes 393216 | tf_op jit(solution)/shard_map/all_to_all | solution.py:23
  38.9 1.4 %collective-permute-start = (bf16[32,16,128]{2,1,0:T(8,128)(2,1)S(1)}, bf16[32,16,128]{2,1,0:T(8,128)(2,1)S(1)}, u32[]{:S(2)}, u32[]{:S(2)}) collective-permute-start(bf16[32,16,128]{2,1,0:T(8,128)(2,1)S(1)} %slice.4), channel_id=1, source_target_pairs={{0,1},{1,0},{2,3},{3,2},{4,5},{5,4},{6,7},{7,6},{8,9},{9,8},{10,11... | collective-permute-start | bytes 393224 | tf_op jit(solution)/shard_map/swap/ppermute | solution.py:273

commit v5 on v4

--- a/solution.py
+++ b/solution.py
@@ -2,6 +2,7 @@
 
 import jax
 import jax.numpy as jnp
+import numpy as np
 from jax import lax
 from jax.experimental import pallas as pl
 from jax.experimental.pallas import tpu as pltpu
@@ -43,6 +44,15 @@
     return high, value - high
 
 
+def repeat_matrix(rows, batch):
+    spread = batch * rows
+    stride = -(-spread // 256) * 256
+    col = np.arange(H * stride)
+    source = col // stride * rows + col % rows
+    hit = (np.arange(H * rows)[:, None] == source) & (col % stride < spread)
+    return jnp.asarray(hit, BF16)
+
+
 def spread_kernel(in_ref, out_ref):
     value = in_ref[...]
     for j in range(out_ref.shape[0]):
@@ -51,6 +61,7 @@
 
 def project_kernel(
     x_ref, gain_ref, wi_ref, wf_ref, bi_ref, bf_ref, nrm_ref, stab_ref, wq_ref, wk_ref, wv_ref, wg_ref, mem_ref,
+    repeat_ref,
     out_ref, nrm_out_ref, stab_out_ref, f_rows_ref, ik_rows_ref, sum_scale_ref, own_ref, floor_ref,
     xn_ref, tail_ref, fg_ref, ig_ref,
 ):
@@ -69,11 +80,12 @@
         xn_ref[:, cut] = (x_ref[j].astype(F32) * scale * gain_ref[:, cut]).astype(BF16)
     x_norm = xn_ref[...]
 
-    query = dot_last(x_norm, wq_ref[...])
-    query_t = dot_last(wq_ref[...], x_norm)
-    key_t = dot_last(wk_ref[...], x_norm) / math.sqrt(DK)
-    input_pre = dot_last(wi_ref[...], x_norm) + column(bi_ref[...])
-    forget_pre = dot_last(wf_ref[...], x_norm) + column(bf_ref[...])
+    left = jnp.concatenate([wq_ref[...], wk_ref[...], wi_ref[...], wf_ref[...]], axis=0)
+    mixed = dot_last(left, x_norm)
+    query_t = mixed[: H * rows]
+    key_t = mixed[H * rows : 2 * H * rows] / math.sqrt(DK)
+    input_pre = mixed[2 * H * rows : 2 * H * rows + H] + column(bi_ref[...])
+    forget_pre = mixed[2 * H * rows + H :] + column(bf_ref[...])
     log_forget = jnp.minimum(forget_pre, 0.0) - jnp.log1p(jnp.exp(-jnp.abs(forget_pre)))
     kept = log_forget + stab_ref[...]
     stab_new = jnp.maximum(kept, input_pre)
@@ -101,25 +113,24 @@
                 tail_ref[core, h, 4 + k : 5 + k, :batch] = kind
 
     spread = batch * rows
-    high, low = split_hi_lo(query)
+    high, low = split_hi_lo(query_t.T)
     both = jnp.concatenate([high, low], axis=0).astype(BF16)
-    at_k = lax.broadcasted_iota(jnp.int32, (rows, spread), 0)
-    at_n = lax.broadcasted_iota(jnp.int32, (rows, spread), 1)
-    repeat = jnp.where(at_n % rows == at_k, 1.0, 0.0).astype(BF16)
+    stride = repeat_ref.shape[1] // H
+    wide = dot(both, repeat_ref[...])
     own_b = lax.broadcasted_iota(jnp.int32, (2 * batch, spread), 0) % batch
     own_n = lax.broadcasted_iota(jnp.int32, (2 * batch, spread), 1) // rows
     own = own_b == own_n
     share = pieces // H
     for h in range(H):
-        wide = dot(both[:, h * rows : (h + 1) * rows], repeat)
-        left = jnp.where(own, wide, 0.0).astype(BF16)
+        left = jnp.where(own, wide[:, h * stride : h * stride + spread], 0.0).astype(BF16)
         by_head = mem_ref[:, h].astype(F32).reshape(spread, share * width).astype(BF16)
         product = dot(left, by_head)
         numer = (product[:batch] + product[batch:]).astype(BF16)
         for c in range(share):
             out_ref[h * share + c, :batch] = numer[:, c * width : (c + 1) * width]
 
-    value = dot(x_norm, wv_ref[...])
+    value_gate = dot(x_norm, jnp.concatenate([wv_ref[...], wg_ref[...]], axis=1))
+    value = value_gate[:, :width]
     for core in range(2):
         first = value[core * half : core * half + 8].astype(BF16)
         rest = value[core * half + 8 : (core + 1) * half]
@@ -131,7 +142,7 @@
 
     head = lax.axis_index("head") * width // DV
     pick = lambda ref: column(ref[pl.ds(head, 1), :])
-    gate = jax.nn.sigmoid(dot(x_norm, wg_ref[...]))
+    gate = jax.nn.sigmoid(value_gate[:, width:])
     sum_scale_ref[...] = gate * pick(fg_ref)
     own_ref[...] = gate * (pick(ig_ref) * value.astype(BF16).astype(F32))
     floor_ref[...] = jnp.broadcast_to(jnp.exp(-pick(stab_out_ref)), floor_ref.shape)
@@ -148,8 +159,10 @@
     key_query = column(tail[6:7, :batch] + tail[7:8, :batch])
     numer = sum_scale_ref[...] * total + own_ref[...] * key_query
     hidden = (numer / jnp.maximum(jnp.abs(norm_query), floor_ref[...])).astype(BF16)
-    for j in range(pieces):
-        out_ref[j] = dot(hidden, wo_ref[:, j * width : (j + 1) * width]).astype(BF16)
+    for j in range(0, pieces, 2):
+        pair = dot(hidden, wo_ref[:, j * width : (j + 2) * width]).astype(BF16)
+        out_ref[j] = pair[:, :width]
+        out_ref[j + 1] = pair[:, width:]
 
 
 def memory_kernel(
@@ -242,6 +255,7 @@
         w_value,
         w_gate,
         memory,
+        repeat_matrix(rows, batch),
     )
     payload, norm_new, stab_new, f_rows, ik_rows, sum_scale, own, floor = call(
         project_kernel,

time: 48.2 us -> 47.8 us (level)
  no operation moved by 1% of the time
where the time goes in v5:
time: 47.8 us; the launch traced here: 47.5 us
  blocking collectives  30 us (63%)
  Pallas kernels  6.06 us (13%)
  waiting for transfers between devices  5.48 us (11%)
  starting transfers between devices  4.29 us (9%)
  between operations  0.84 us (2%)
  other arithmetic  0.71 us (1%)
    all_to_all x2, blocking collectives, exchange(): return lax.all_to_all(pieces, 'head', 0, 0, tiled=True)  30 us
    all_to_all x1, waiting for transfers between devices, exchange(): return lax.all_to_all(pieces, 'head', 0, 0, tiled=True)  4.49 us
    all_to_all x1, starting transfers between devices, exchange(): return lax.all_to_all(pieces, 'head', 0, 0, tiled=True)  3.86 us
    pallas_call x1, Pallas kernels, body(): call(memory_kernel, [(memory.shape, BF16), ((H * rows, batch), F32), ((H,...  2.41 us
    pallas_call x1, Pallas kernels, body(): call(project_kernel, [((count, batch + batch // 2 + 4, width), BF16), ((H...  1.93 us
    pallas_call x1, Pallas kernels, body(): call(output_kernel, [piece], 5, flops=30000000)  1.05 us
    ppermute x1, waiting for transfers between devices, body(): lax.ppermute(arrived[:, batch:], 'head', [(i, i ^ 1) for i in range(count)])  1 us
  transfers between devices with their start and end apart: 2, of which 2 were waited for; matrix products, arithmetic and copies ran while one was open for 0% of the time, Pallas kernels for 5%

profile of v5, /device:TPU:1, one launch (start us, length us, event | category | flops | bytes accessed | tf_op | source)
XLA Modules:
  0.0 47.5 jit_solution(15072338520065055443)
XLA Ops:
  0.6 0.7 %convert_element_type.3.in_ref = bf16[24,128]{1,0:T(8,128)(2,1)S(1)} convert(f32[24,128]{1,0:T(8,128)} %residual_ref.1) | non-fusion elementwise | flops 3072 | bytes 18432 | tf_op jit(solution)/shard_map/convert_element_type | solution.py:240
  1.3 0.0 copy-start
  1.3 0.0 copy-start.1
  1.3 0.0 copy-start.2
  1.4 0.0 copy-start.4
  1.4 0.0 copy-start.5
  1.4 0.0 copy-start.6
  1.4 0.0 copy-start.7
  1.4 0.0 copy-start.8
  1.4 0.0 copy-start.10
  1.4 0.0 copy-start.11
  1.4 0.0 copy-start.12
  1.4 0.0 copy-start.13
  1.5 0.0 copy-start.14
  1.5 16.9 %all_to_all.15.x_ref = bf16[32,24,128]{2,1,0:T(8,128)(2,1)S(1)} all-to-all(bf16[32,24,128]{2,1,0:T(8,128)(2,1)S(1)} %shard_map.174), channel_id=1, replica_groups=mesh['dp'=8,'head'=32] {'head'}, dimensions={0} | all-to-all | bytes 393216 | tf_op jit(solution)/shard_map/all_to_all | solution.py:24
  18.4 0.0 copy-done
  18.4 0.0 copy-done.1
  18.4 0.0 copy-done.2
  18.4 0.0 copy-done.4
  18.4 0.0 copy-done.5
  18.4 0.0 copy-done.6
  18.4 0.0 copy-done.7
  18.4 0.0 copy-done.8
  18.4 0.0 copy-done.10
  18.5 0.0 copy-done.11
  18.5 0.0 copy-done.12
  18.5 0.0 copy-done.13
  18.5 0.0 copy-done.14
  18.5 0.0 copy-start.3
  18.5 1.9 %shard_map.175 = (bf16[32,40,128]{2,1,0:T(8,128)(2,1)S(1)}, f32[64,24]{1,0:T(8,128)S(1)}, f32[8,24]{1,0:T(8,128)S(1)}, f32[64,24]{1,0:T(8,128)S(1)}, f32[64,24]{...) custom-call(bf16[32,24,128]{2,1,0:T(8,128)(2,1)S(1)} %all_to_all.15.x_ref, ...), custom_call_target="tpu_custom_call" | custom-call | flops 100000000 | bytes 2000000 | tf_op jit(solution)/shard_map/pallas_call | solution.py:260
  20.4 13.1 %all_to_all.16.in_ref.mine_ref = bf16[32,40,128]{2,1,0:T(8,128)(2,1)S(1)} all-to-all(bf16[32,40,128]{2,1,0:T(8,128)(2,1)S(1)} %get-tuple-element.15), channel_id=1, replica_groups=mesh['dp'=8,'head'=32] {'head'}, dimensions={0} | all-to-all | bytes 655360 | tf_op jit(solution)/shard_map/all_to_all | solution.py:24
  33.6 0.0 copy-done.3
  33.6 1.1 %shard_map.176 = bf16[32,24,128]{2,1,0:T(8,128)(2,1)} custom-call(bf16[32,40,128]{2,1,0:T(8,128)(2,1)S(1)} %all_to_all.16.in_ref.mine_ref, f32[24,128]{1,0:T(8,128)S(1)} %get-tuple-element.16.sum_scale_ref, f32[24,128]{1,0:T(8,128)S(1)} %get-tuple-element.17.own_ref, f32[24,128]{1,0:T(8,128)S(1)} %get-tuple-element.18.floor_ref, bf16[128,4096]{1,0:T(8,128)(2,1)S(1)} %copy-done.3), custom_call_target="tpu_custom_call" | custom-call | flops 30000000 | bytes 2000000 | tf_op jit(solution)/shard_map/pallas_call | solution.py:282
  34.6 0.0 copy-start.9
  34.6 3.9 %all-to-all-start.2 = ((bf16[32,24,128]{2,1,0:T(8,128)(2,1)}), bf16[32,24,128]{2,1,0:T(8,128)(2,1)S(1)}, u32[]{:S(2)}, u32[]{:S(2)}) async-start(bf16[32,24,128]{2,1,0:T(8,128)(2,1)} %shard_map.176), calls=%async_computation.2 | async-start | bytes 393216 | tf_op jit(solution)/shard_map/all_to_all | solution.py:24
  38.5 0.4 collective-permute-start
  38.9 1.0 %collective-permute-done.other_ref = bf16[32,16,128]{2,1,0:T(8,128)(2,1)S(1)} collective-permute-done((bf16[32,16,128]{2,1,0:T(8,128)(2,1)S(1)}, bf16[32,16,128]{2,1,0:T(8,128)(2,1)S(1)}, u32[]{:S(2)}, u32[]{:S(2)}) %collective-permute-start) | collective-permute-done | bytes 131104 | tf_op jit(solution)/shard_map/swap/ppermute | solution.py:287
  39.9 2.4 %shard_map.178 = (bf16[24,8,8,512]{3,2,1,0:T(8,128)(2,1)}, f32[64,24]{1,0:T(8,128)}, f32[8,24]{1,0:T(8,128)}) custom-call(f32[64,24]{1,0:T(8,128)S(1)} %get-tuple-element.19.f_rows_ref, f32[64,24]{1,0:T(8,128)S(1)} %get-tuple-element.20.ik_rows_ref, f32[64,24]{1,0:T(8,128)S(1)} %get-tuple-element.21.norm_ref, f32[8,24]{1,0:T(8,128)S(1)} %get-tuple-element.22.stab_ref, ...), custom_call_target="tpu_custom_call" | custom-call | flops 100000000 | bytes 2000000 | tf_op jit(solution)/shard_map/pallas_call | solution.py:288
  42.3 4.5 %all-to-all-done.2.in_ref = bf16[32,24,128]{2,1,0:T(8,128)(2,1)S(1)} async-done(((bf16[32,24,128]{2,1,0:T(8,128)(2,1)}), bf16[32,24,128]{2,1,0:T(8,128)(2,1)S(1)}, u32[]{:S(2)}, u32[]{:S(2)}) %all-to-all-start.2) | async-done | bytes 196640 | tf_op jit(solution)/shard_map/all_to_all | solution.py:24
  46.8 0.0 copy-done.9
  46.8 0.6 %shard_map.177 = f32[24,128]{1,0:T(8,128)} custom-call(bf16[32,24,128]{2,1,0:T(8,128)(2,1)S(1)} %all-to-all-done.2.in_ref, f32[24,128]{1,0:T(8,128)S(1)} %copy-done.9), custom_call_target="tpu_custom_call" | custom-call | flops 1000000 | bytes 2000000 | tf_op jit(solution)/shard_map/pallas_call | solution.py:295
  (2 shorter events, 0.0 us)
Async XLA Ops:
  1.3 17.0 %copy-start = (bf16[24,8,8,512]{3,2,1,0:T(8,128)(2,1)S(1)}, bf16[24,8,8,512]{3,2,1,0:T(8,128)(2,1)}, u32[]{:S(2)}) copy-start(bf16[24,8,8,512]{3,2,1,0:T(8,128)(2,1)} %mem_ref.3) | copy-start | bytes 4718596
  1.3 17.0 %copy-start.1 = (bf16[4096,128]{1,0:T(8,128)(2,1)S(1)}, bf16[4096,128]{1,0:T(8,128)(2,1)}, u32[]{:S(2)}) copy-start(bf16[4096,128]{1,0:T(8,128)(2,1)} %wv_ref.1) | copy-start | bytes 3145732
  1.3 17.0 %copy-start.2 = (bf16[4096,128]{1,0:T(8,128)(2,1)S(1)}, bf16[4096,128]{1,0:T(8,128)(2,1)}, u32[]{:S(2)}) copy-start(bf16[4096,128]{1,0:T(8,128)(2,1)} %wg_ref.1) | copy-start | bytes 3145732
  1.4 17.0 %copy-start.4 = (bf16[8,8,4096]{2,1,0:T(8,128)(2,1)S(1)}, bf16[8,8,4096]{2,1,0:T(8,128)(2,1)}, u32[]{:S(2)}) copy-start(bf16[8,8,4096]{2,1,0:T(8,128)(2,1)} %param.17) | copy-start | bytes 1572868
  1.4 17.0 %copy-start.5 = (bf16[8,8,4096]{2,1,0:T(8,128)(2,1)S(1)}, bf16[8,8,4096]{2,1,0:T(8,128)(2,1)}, u32[]{:S(2)}) copy-start(bf16[8,8,4096]{2,1,0:T(8,128)(2,1)} %param.18) | copy-start | bytes 1572868
  1.4 17.0 %copy-start.6 = (bf16[64,2048]{1,0:T(8,128)(2,1)S(1)}, bf16[64,2048]{1,0:T(8,128)(2,1)}, u32[]{:S(2)}) copy-start(bf16[64,2048]{1,0:T(8,128)(2,1)} %constant.2.clone.repeat_ref) | copy-start | bytes 786436
  1.4 17.0 %copy-start.7 = (bf16[8,4096]{1,0:T(8,128)(2,1)S(1)}, bf16[8,4096]{1,0:T(8,128)(2,1)}, u32[]{:S(2)}) copy-start(bf16[8,4096]{1,0:T(8,128)(2,1)} %wi_ref.1) | copy-start | bytes 196612
  1.4 17.0 %copy-start.8 = (bf16[8,4096]{1,0:T(8,128)(2,1)S(1)}, bf16[8,4096]{1,0:T(8,128)(2,1)}, u32[]{:S(2)}) copy-start(bf16[8,4096]{1,0:T(8,128)(2,1)} %wf_ref.1) | copy-start | bytes 196612
  1.4 17.0 %copy-start.10 = (f32[24,8,8]{0,2,1:T(8,128)S(1)}, f32[24,8,8]{0,2,1:T(8,128)}, u32[]{:S(2)}) copy-start(f32[24,8,8]{0,2,1:T(8,128)} %param.27) | copy-start | bytes 18436
  1.4 17.0 %copy-start.11 = (f32[4096]{0:T(1024)S(1)}, f32[4096]{0:T(1024)}, u32[]{:S(2)}) copy-start(f32[4096]{0:T(1024)} %param.16) | copy-start | bytes 49156
  1.4 17.0 %copy-start.12 = (f32[24,8]{0,1:T(8,128)S(1)}, f32[24,8]{0,1:T(8,128)}, u32[]{:S(2)}) copy-start(f32[24,8]{0,1:T(8,128)} %param.28) | copy-start | bytes 2308
  1.4 17.0 %copy-start.13 = (f32[8]{0:T(128)S(1)}, f32[8]{0:T(128)}, u32[]{:S(2)}) copy-start(f32[8]{0:T(128)} %param.23) | copy-start | bytes 100
  1.5 17.0 %copy-start.14 = (f32[8]{0:T(128)S(1)}, f32[8]{0:T(128)}, u32[]{:S(2)}) copy-start(f32[8]{0:T(128)} %param.24) | copy-start | bytes 100
  18.5 15.1 %copy-start.3 = (bf16[128,4096]{1,0:T(8,128)(2,1)S(1)}, bf16[128,4096]{1,0:T(8,128)(2,1)}, u32[]{:S(2)}) copy-start(bf16[128,4096]{1,0:T(8,128)(2,1)} %wo_ref.1) | copy-start | bytes 3145732
  34.6 12.2 %copy-start.9 = (f32[24,128]{1,0:T(8,128)S(1)}, f32[24,128]{1,0:T(8,128)}, u32[]{:S(2)}) copy-start(f32[24,128]{1,0:T(8,128)} %residual_ref.1) | copy-start | bytes 36868
  34.6 12.2 %all-to-all-start.2 = ((bf16[32,24,128]{2,1,0:T(8,128)(2,1)}), bf16[32,24,128]{2,1,0:T(8,128)(2,1)S(1)}, u32[]{:S(2)}, u32[]{:S(2)}) async-start(bf16[32,24,128]{2,1,0:T(8,128)(2,1)} %shard_map.176), calls=%async_computation.2 | async-start | bytes 393216 | tf_op jit(solution)/shard_map/all_to_all | solution.py:24
  38.5 1.4 %collective-permute-start = (bf16[32,16,128]{2,1,0:T(8,128)(2,1)S(1)}, bf16[32,16,128]{2,1,0:T(8,128)(2,1)S(1)}, u32[]{:S(2)}, u32[]{:S(2)}) collective-permute-start(bf16[32,16,128]{2,1,0:T(8,128)(2,1)S(1)} %slice.4), channel_id=1, source_target_pairs={{0,1},{1,0},{2,3},{3,2},{4,5},{5,4},{6,7},{7,6},{8,9},{9,8},{10,11... | collective-permute-start | bytes 393224 | tf_op jit(solution)/shard_map/swap/ppermute | solution.py:287

commit v6 on v5

--- a/solution.py
+++ b/solution.py
@@ -45,12 +45,15 @@
 
 
 def repeat_matrix(rows, batch):
-    spread = batch * rows
-    stride = -(-spread // 256) * 256
-    col = np.arange(H * stride)
-    source = col // stride * rows + col % rows
-    hit = (np.arange(H * rows)[:, None] == source) & (col % stride < spread)
-    return jnp.asarray(hit, BF16)
+    spread = 2 * rows * batch
+    col = np.arange(H * spread)
+    return jnp.asarray(np.arange(H * rows)[:, None] == col // spread * rows + col % rows, BF16)
+
+
+def own_mask(rows, batch):
+    row = np.arange(4 * batch)[:, None]
+    col = np.arange(2 * rows * batch)
+    return jnp.asarray((row % batch == col // (2 * rows)) & (row // (2 * batch) == col // rows % 2), BF16)
 
 
 def spread_kernel(in_ref, out_ref):
@@ -61,8 +64,8 @@
 
 def project_kernel(
     x_ref, gain_ref, wi_ref, wf_ref, bi_ref, bf_ref, nrm_ref, stab_ref, wq_ref, wk_ref, wv_ref, wg_ref, mem_ref,
-    repeat_ref,
-    out_ref, nrm_out_ref, stab_out_ref, f_rows_ref, ik_rows_ref, sum_scale_ref, own_ref, floor_ref,
+    repeat_ref, own_ref,
+    out_ref, nrm_out_ref, stab_out_ref, f_rows_ref, ik_rows_ref, sum_scale_ref, own_value_ref, floor_ref,
     xn_ref, tail_ref, fg_ref, ig_ref,
 ):
     pieces, batch, width = x_ref.shape
@@ -115,19 +118,20 @@
     spread = batch * rows
     high, low = split_hi_lo(query_t.T)
     both = jnp.concatenate([high, low], axis=0).astype(BF16)
-    stride = repeat_ref.shape[1] // H
-    wide = dot(both, repeat_ref[...])
-    own_b = lax.broadcasted_iota(jnp.int32, (2 * batch, spread), 0) % batch
-    own_n = lax.broadcasted_iota(jnp.int32, (2 * batch, spread), 1) // rows
-    own = own_b == own_n
+    spread = repeat_ref.shape[1] // H
+    wide = dot(both, repeat_ref[...]).astype(BF16)
     share = pieces // H
+    deep = 2 * rows
     for h in range(H):
-        left = jnp.where(own, wide[:, h * stride : h * stride + spread], 0.0).astype(BF16)
-        by_head = mem_ref[:, h].astype(F32).reshape(spread, share * width).astype(BF16)
-        product = dot(left, by_head)
-        numer = (product[:batch] + product[batch:]).astype(BF16)
-        for c in range(share):
-            out_ref[h * share + c, :batch] = numer[:, c * width : (c + 1) * width]
+        wide_h = wide[:, h * spread : (h + 1) * spread]
+        left = jnp.concatenate([wide_h, wide_h], axis=0) * own_ref[...]
+        right = [mem_ref[:, h, k * deep : (k + 1) * deep].reshape(spread, width) for k in range(2)]
+        product = dot(left, jnp.concatenate(right, axis=1))
+        for parity in range(2):
+            at = parity * 2 * batch
+            numer = (product[at : at + batch] + product[at + batch : at + 2 * batch]).astype(BF16)
+            for k in range(2):
+                out_ref[h * share + 2 * k + parity, :batch] = numer[:, k * width : (k + 1) * width]
 
     value_gate = dot(x_norm, jnp.concatenate([wv_ref[...], wg_ref[...]], axis=1))
     value = value_gate[:, :width]
@@ -144,7 +148,7 @@
     pick = lambda ref: column(ref[pl.ds(head, 1), :])
     gate = jax.nn.sigmoid(value_gate[:, width:])
     sum_scale_ref[...] = gate * pick(fg_ref)
-    own_ref[...] = gate * (pick(ig_ref) * value.astype(BF16).astype(F32))
+    own_value_ref[...] = gate * (pick(ig_ref) * value.astype(BF16).astype(F32))
     floor_ref[...] = jnp.broadcast_to(jnp.exp(-pick(stab_out_ref)), floor_ref.shape)
 
 
@@ -254,8 +258,11 @@
         w_key.reshape(H * rows, features),
         w_value,
         w_gate,
-        memory,
+        memory.reshape(batch, H, rows, DV // width, width)
+        .transpose(0, 1, 3, 2, 4)
+        .reshape(batch, H, DV // width * rows, width),
         repeat_matrix(rows, batch),
+        own_mask(rows, batch),
     )
     payload, norm_new, stab_new, f_rows, ik_rows, sum_scale, own, floor = call(
         project_kernel,

time: 47.8 us -> 47.4 us (level)
  no operation moved by 1% of the time
where the time goes in v6:
time: 47.4 us; the launch traced here: 47.1 us
  blocking collectives  30 us (63%)
  Pallas kernels  5.62 us (12%)
  waiting for transfers between devices  5.48 us (12%)
  starting transfers between devices  4.29 us (9%)
  between operations  0.86 us (2%)
  other arithmetic  0.71 us (1%)
    all_to_all x2, blocking collectives, exchange(): return lax.all_to_all(pieces, 'head', 0, 0, tiled=True)  30 us
    all_to_all x1, waiting for transfers between devices, exchange(): return lax.all_to_all(pieces, 'head', 0, 0, tiled=True)  4.49 us
    all_to_all x1, starting transfers between devices, exchange(): return lax.all_to_all(pieces, 'head', 0, 0, tiled=True)  3.86 us
    pallas_call x1, Pallas kernels, body(): call(memory_kernel, [(memory.shape, BF16), ((H * rows, batch), F32), ((H,...  2.41 us
    pallas_call x1, Pallas kernels, body(): call(project_kernel, [((count, batch + batch // 2 + 4, width), BF16), ((H...  1.49 us
    pallas_call x1, Pallas kernels, body(): call(output_kernel, [piece], 5, flops=30000000)  1.05 us
    ppermute x1, waiting for transfers between devices, body(): lax.ppermute(arrived[:, batch:], 'head', [(i, i ^ 1) for i in range(count)])  1 us
  transfers between devices with their start and end apart: 2, of which 2 were waited for; matrix products, arithmetic and copies ran while one was open for 0% of the time, Pallas kernels for 5%

profile of v6, /device:TPU:1, one launch (start us, length us, event | category | flops | bytes accessed | tf_op | source)
XLA Modules:
  0.0 47.1 jit_solution(10292263630860547421)
XLA Ops:
  0.6 0.7 %convert_element_type.3.in_ref = bf16[24,128]{1,0:T(8,128)(2,1)S(1)} convert(f32[24,128]{1,0:T(8,128)} %residual_ref.1) | non-fusion elementwise | flops 3072 | bytes 18432 | tf_op jit(solution)/shard_map/convert_element_type | solution.py:244
  1.3 0.0 copy-start
  1.3 0.0 copy-start.2
  1.3 0.0 copy-start.3
  1.4 0.0 copy-start.4
  1.4 0.0 copy-start.5
  1.4 0.0 copy-start.6
  1.4 0.0 copy-start.7
  1.4 0.0 copy-start.8
  1.4 0.0 copy-start.9
  1.4 0.0 copy-start.11
  1.4 0.0 copy-start.12
  1.4 0.0 copy-start.13
  1.5 0.0 copy-start.14
  1.5 0.0 copy-start.15
  1.5 16.9 %all_to_all.15.x_ref = bf16[32,24,128]{2,1,0:T(8,128)(2,1)S(1)} all-to-all(bf16[32,24,128]{2,1,0:T(8,128)(2,1)S(1)} %shard_map.183), channel_id=1, replica_groups=mesh['dp'=8,'head'=32] {'head'}, dimensions={0} | all-to-all | bytes 393216 | tf_op jit(solution)/shard_map/all_to_all | solution.py:24
  18.4 0.0 copy-done
  18.4 0.0 copy-done.2
  18.4 0.0 copy-done.3
  18.4 0.0 copy-done.4
  18.4 0.0 copy-done.5
  18.4 0.0 copy-done.6
  18.4 0.0 copy-done.7
  18.4 0.0 copy-done.8
  18.5 0.0 copy-done.9
  18.5 0.0 copy-done.11
  18.5 0.0 copy-done.12
  18.5 0.0 copy-done.13
  18.5 0.0 copy-done.14
  18.5 0.0 copy-done.15
  18.5 0.0 copy-start.1
  18.5 1.5 %shard_map.184 = (bf16[32,40,128]{2,1,0:T(8,128)(2,1)S(1)}, f32[64,24]{1,0:T(8,128)S(1)}, f32[8,24]{1,0:T(8,128)S(1)}, f32[64,24]{1,0:T(8,128)S(1)}, f32[64,24]{...) custom-call(bf16[32,24,128]{2,1,0:T(8,128)(2,1)S(1)} %all_to_all.15.x_ref, ...), custom_call_target="tpu_custom_call" | custom-call | flops 100000000 | bytes 2000000 | tf_op jit(solution)/shard_map/pallas_call | solution.py:267
  20.0 13.1 %all_to_all.16.in_ref.mine_ref = bf16[32,40,128]{2,1,0:T(8,128)(2,1)S(1)} all-to-all(bf16[32,40,128]{2,1,0:T(8,128)(2,1)S(1)} %get-tuple-element.15), channel_id=1, replica_groups=mesh['dp'=8,'head'=32] {'head'}, dimensions={0} | all-to-all | bytes 655360 | tf_op jit(solution)/shard_map/all_to_all | solution.py:24
  33.1 0.0 copy-done.1
  33.1 1.0 %shard_map.185 = bf16[32,24,128]{2,1,0:T(8,128)(2,1)} custom-call(bf16[32,40,128]{2,1,0:T(8,128)(2,1)S(1)} %all_to_all.16.in_ref.mine_ref, f32[24,128]{1,0:T(8,128)S(1)} %get-tuple-element.16.sum_scale_ref, f32[24,128]{1,0:T(8,128)S(1)} %get-tuple-element.17.own_ref, f32[24,128]{1,0:T(8,128)S(1)} %get-tuple-element.18.floor_ref, bf16[128,4096]{1,0:T(8,128)(2,1)S(1)} %copy-done.1), custom_call_target="tpu_custom_call" | custom-call | flops 30000000 | bytes 2000000 | tf_op jit(solution)/shard_map/pallas_call | solution.py:289
  34.2 0.0 copy-start.10
  34.2 3.9 %all-to-all-start.2 = ((bf16[32,24,128]{2,1,0:T(8,128)(2,1)}), bf16[32,24,128]{2,1,0:T(8,128)(2,1)S(1)}, u32[]{:S(2)}, u32[]{:S(2)}) async-start(bf16[32,24,128]{2,1,0:T(8,128)(2,1)} %shard_map.185), calls=%async_computation.2 | async-start | bytes 393216 | tf_op jit(solution)/shard_map/all_to_all | solution.py:24
  38.1 0.4 collective-permute-start
  38.5 1.0 %collective-permute-done.other_ref = bf16[32,16,128]{2,1,0:T(8,128)(2,1)S(1)} collective-permute-done((bf16[32,16,128]{2,1,0:T(8,128)(2,1)S(1)}, bf16[32,16,128]{2,1,0:T(8,128)(2,1)S(1)}, u32[]{:S(2)}, u32[]{:S(2)}) %collective-permute-start) | collective-permute-done | bytes 131104 | tf_op jit(solution)/shard_map/swap/ppermute | solution.py:294
  39.5 2.4 %shard_map.187 = (bf16[24,8,8,512]{3,2,1,0:T(8,128)(2,1)}, f32[64,24]{1,0:T(8,128)}, f32[8,24]{1,0:T(8,128)}) custom-call(f32[64,24]{1,0:T(8,128)S(1)} %get-tuple-element.19.f_rows_ref, f32[64,24]{1,0:T(8,128)S(1)} %get-tuple-element.20.ik_rows_ref, f32[64,24]{1,0:T(8,128)S(1)} %get-tuple-element.21.norm_ref, f32[8,24]{1,0:T(8,128)S(1)} %get-tuple-element.22.stab_ref, ...), custom_call_target="tpu_custom_call" | custom-call | flops 100000000 | bytes 2000000 | tf_op jit(solution)/shard_map/pallas_call | solution.py:295
  41.9 4.5 %all-to-all-done.2.in_ref = bf16[32,24,128]{2,1,0:T(8,128)(2,1)S(1)} async-done(((bf16[32,24,128]{2,1,0:T(8,128)(2,1)}), bf16[32,24,128]{2,1,0:T(8,128)(2,1)S(1)}, u32[]{:S(2)}, u32[]{:S(2)}) %all-to-all-start.2) | async-done | bytes 196640 | tf_op jit(solution)/shard_map/all_to_all | solution.py:24
  46.4 0.0 copy-done.10
  46.4 0.6 %shard_map.186 = f32[24,128]{1,0:T(8,128)} custom-call(bf16[32,24,128]{2,1,0:T(8,128)(2,1)S(1)} %all-to-all-done.2.in_ref, f32[24,128]{1,0:T(8,128)S(1)} %copy-done.10), custom_call_target="tpu_custom_call" | custom-call | flops 1000000 | bytes 2000000 | tf_op jit(solution)/shard_map/pallas_call | solution.py:302
  (2 shorter events, 0.0 us)
Async XLA Ops:
  1.3 17.1 %copy-start = (bf16[24,8,8,512]{3,2,1,0:T(8,128)(2,1)S(1)}, bf16[24,8,8,512]{3,2,1,0:T(8,128)(2,1)}, u32[]{:S(2)}) copy-start(bf16[24,8,8,512]{3,2,1,0:T(8,128)(2,1)} %mem_ref.1) | copy-start | bytes 4718596
  1.3 17.1 %copy-start.2 = (bf16[4096,128]{1,0:T(8,128)(2,1)S(1)}, bf16[4096,128]{1,0:T(8,128)(2,1)}, u32[]{:S(2)}) copy-start(bf16[4096,128]{1,0:T(8,128)(2,1)} %wv_ref.1) | copy-start | bytes 3145732
  1.3 17.1 %copy-start.3 = (bf16[4096,128]{1,0:T(8,128)(2,1)S(1)}, bf16[4096,128]{1,0:T(8,128)(2,1)}, u32[]{:S(2)}) copy-start(bf16[4096,128]{1,0:T(8,128)(2,1)} %wg_ref.1) | copy-start | bytes 3145732
  1.4 17.1 %copy-start.4 = (bf16[8,8,4096]{2,1,0:T(8,128)(2,1)S(1)}, bf16[8,8,4096]{2,1,0:T(8,128)(2,1)}, u32[]{:S(2)}) copy-start(bf16[8,8,4096]{2,1,0:T(8,128)(2,1)} %param.18) | copy-start | bytes 1572868
  1.4 17.1 %copy-start.5 = (bf16[8,8,4096]{2,1,0:T(8,128)(2,1)S(1)}, bf16[8,8,4096]{2,1,0:T(8,128)(2,1)}, u32[]{:S(2)}) copy-start(bf16[8,8,4096]{2,1,0:T(8,128)(2,1)} %param.19) | copy-start | bytes 1572868
  1.4 17.1 %copy-start.6 = (bf16[64,3072]{1,0:T(8,128)(2,1)S(1)}, bf16[64,3072]{1,0:T(8,128)(2,1)}, u32[]{:S(2)}) copy-start(bf16[64,3072]{1,0:T(8,128)(2,1)} %constant.4.clone.repeat_ref) | copy-start | bytes 1179652
  1.4 17.1 %copy-start.7 = (bf16[96,384]{1,0:T(8,128)(2,1)S(1)}, bf16[96,384]{1,0:T(8,128)(2,1)}, u32[]{:S(2)}) copy-start(bf16[96,384]{1,0:T(8,128)(2,1)} %constant.5.clone.own_ref) | copy-start | bytes 221188
  1.4 17.1 %copy-start.8 = (bf16[8,4096]{1,0:T(8,128)(2,1)S(1)}, bf16[8,4096]{1,0:T(8,128)(2,1)}, u32[]{:S(2)}) copy-start(bf16[8,4096]{1,0:T(8,128)(2,1)} %wi_ref.1) | copy-start | bytes 196612
  1.4 17.0 %copy-start.9 = (bf16[8,4096]{1,0:T(8,128)(2,1)S(1)}, bf16[8,4096]{1,0:T(8,128)(2,1)}, u32[]{:S(2)}) copy-start(bf16[8,4096]{1,0:T(8,128)(2,1)} %wf_ref.1) | copy-start | bytes 196612
  1.4 17.0 %copy-start.11 = (f32[24,8,8]{0,2,1:T(8,128)S(1)}, f32[24,8,8]{0,2,1:T(8,128)}, u32[]{:S(2)}) copy-start(f32[24,8,8]{0,2,1:T(8,128)} %param.28) | copy-start | bytes 18436
  1.4 17.0 %copy-start.12 = (f32[4096]{0:T(1024)S(1)}, f32[4096]{0:T(1024)}, u32[]{:S(2)}) copy-start(f32[4096]{0:T(1024)} %param.17) | copy-start | bytes 49156
  1.4 17.0 %copy-start.13 = (f32[24,8]{0,1:T(8,128)S(1)}, f32[24,8]{0,1:T(8,128)}, u32[]{:S(2)}) copy-start(f32[24,8]{0,1:T(8,128)} %param.29) | copy-start | bytes 2308
  1.5 17.0 %copy-start.14 = (f32[8]{0:T(128)S(1)}, f32[8]{0:T(128)}, u32[]{:S(2)}) copy-start(f32[8]{0:T(128)} %param.24) | copy-start | bytes 100
  1.5 17.0 %copy-start.15 = (f32[8]{0:T(128)S(1)}, f32[8]{0:T(128)}, u32[]{:S(2)}) copy-start(f32[8]{0:T(128)} %param.25) | copy-start | bytes 100
  18.5 14.6 %copy-start.1 = (bf16[128,4096]{1,0:T(8,128)(2,1)S(1)}, bf16[128,4096]{1,0:T(8,128)(2,1)}, u32[]{:S(2)}) copy-start(bf16[128,4096]{1,0:T(8,128)(2,1)} %wo_ref.1) | copy-start | bytes 3145732
  34.2 12.2 %copy-start.10 = (f32[24,128]{1,0:T(8,128)S(1)}, f32[24,128]{1,0:T(8,128)}, u32[]{:S(2)}) copy-start(f32[24,128]{1,0:T(8,128)} %residual_ref.1) | copy-start | bytes 36868
  34.2 12.2 %all-to-all-start.2 = ((bf16[32,24,128]{2,1,0:T(8,128)(2,1)}), bf16[32,24,128]{2,1,0:T(8,128)(2,1)S(1)}, u32[]{:S(2)}, u32[]{:S(2)}) async-start(bf16[32,24,128]{2,1,0:T(8,128)(2,1)} %shard_map.185), calls=%async_computation.2 | async-start | bytes 393216 | tf_op jit(solution)/shard_map/all_to_all | solution.py:24
  38.1 1.4 %collective-permute-start = (bf16[32,16,128]{2,1,0:T(8,128)(2,1)S(1)}, bf16[32,16,128]{2,1,0:T(8,128)(2,1)S(1)}, u32[]{:S(2)}, u32[]{:S(2)}) collective-permute-start(bf16[32,16,128]{2,1,0:T(8,128)(2,1)S(1)} %slice.4), channel_id=1, source_target_pairs={{0,1},{1,0},{2,3},{3,2},{4,5},{5,4},{6,7},{7,6},{8,9},{9,8},{10,11... | collective-permute-start | bytes 393224 | tf_op jit(solution)/shard_map/swap/ppermute | solution.py:294

commit v7 on v6

--- a/solution.py
+++ b/solution.py
@@ -17,11 +17,15 @@
 STATS = 8
 
 
+FAR = 21
 SPREAD_FLOPS = 10_000_000_000
 
 
-def exchange(pieces):
-    return lax.all_to_all(pieces, "head", 0, 0, tiled=True)
+def exchange(pieces, far=0):
+    count = lax.axis_size("head")
+    return lax.all_to_all(
+        pieces, "head", 0, 0, tiled=True, axis_index_groups=[[k ^ far for k in range(count)]]
+    )
 
 
 def dot_last(left, right):
@@ -79,7 +83,7 @@
     scale = lax.rsqrt(mean + EPSILON)
     tail_ref[...] = jnp.zeros(tail_ref.shape, F32)
     for j in range(pieces):
-        cut = slice(j * width, (j + 1) * width)
+        cut = slice((j ^ FAR) * width, ((j ^ FAR) + 1) * width)
         xn_ref[:, cut] = (x_ref[j].astype(F32) * scale * gain_ref[:, cut]).astype(BF16)
     x_norm = xn_ref[...]
 
@@ -131,7 +135,7 @@
             at = parity * 2 * batch
             numer = (product[at : at + batch] + product[at + batch : at + 2 * batch]).astype(BF16)
             for k in range(2):
-                out_ref[h * share + 2 * k + parity, :batch] = numer[:, k * width : (k + 1) * width]
+                out_ref[(h * share + 2 * k + parity) ^ FAR, :batch] = numer[:, k * width : (k + 1) * width]
 
     value_gate = dot(x_norm, jnp.concatenate([wv_ref[...], wg_ref[...]], axis=1))
     value = value_gate[:, :width]
@@ -141,8 +145,8 @@
         for h in range(H):
             tail_ref[core, h, :4] = rest
         for j in range(core, pieces, 2):
-            out_ref[j, batch : batch + 8] = first
-            out_ref[j, batch + 8 :] = tail_ref[core, j // share].astype(BF16)
+            out_ref[j ^ FAR, batch : batch + 8] = first
+            out_ref[j ^ FAR, batch + 8 :] = tail_ref[core, j // share].astype(BF16)
 
     head = lax.axis_index("head") * width // DV
     pick = lambda ref: column(ref[pl.ds(head, 1), :])
@@ -165,8 +169,8 @@
     hidden = (numer / jnp.maximum(jnp.abs(norm_query), floor_ref[...])).astype(BF16)
     for j in range(0, pieces, 2):
         pair = dot(hidden, wo_ref[:, j * width : (j + 2) * width]).astype(BF16)
-        out_ref[j] = pair[:, :width]
-        out_ref[j + 1] = pair[:, width:]
+        out_ref[j ^ FAR] = pair[:, :width]
+        out_ref[(j + 1) ^ FAR] = pair[:, width:]
 
 
 def memory_kernel(
@@ -183,8 +187,8 @@
     even = lax.axis_index("head") % 2 == 0
     for j in range(pieces):
         cut = slice((j % share) * width, (j % share + 1) * width)
-        mine = mine_ref[j, batch : batch + 16].astype(F32)[:half]
-        other = other_ref[j].astype(F32)[:half]
+        mine = mine_ref[j ^ FAR, batch : batch + 16].astype(F32)[:half]
+        other = other_ref[j ^ FAR].astype(F32)[:half]
         wide_ref[j // share, :half, cut] = jnp.where(even, mine, other)
         wide_ref[j // share, half:, cut] = jnp.where(even, other, mine)
 
@@ -243,7 +247,7 @@
     (pieces,) = call(spread_kernel, [((count, batch, width), BF16)], 1, flops=SPREAD_FLOPS)(
         residual.astype(BF16)
     )
-    gathered = exchange(pieces)
+    gathered = exchange(pieces, FAR)
 
     piece = ((count, batch, width), BF16)
     sources = (
@@ -285,11 +289,11 @@
         ],
         flops=100_000_000,
     )(gathered, *sources)
-    arrived = exchange(payload)
+    arrived = exchange(payload, FAR)
     (branch,) = call(output_kernel, [piece], 5, flops=30_000_000)(
         arrived, sum_scale, own, floor, w_out
     )
-    returned = exchange(branch)
+    returned = exchange(branch, FAR)
     with jax.named_scope("swap"):
         other = lax.ppermute(arrived[:, batch:], "head", [(i, i ^ 1) for i in range(count)])
     mem_new, norm_out, stab_out = call(

time: 47.4 us -> 43.2 us (0.911)
  waiting for transfers between devices: 5.48 us -> 0.99 us
  starting transfers between devices: 4.29 us -> 8.45 us
  blocking collectives: 30 us -> 26.2 us
    all_to_all x1, waiting for transfers between devices: 4.49 us -> 0.01 us  [exchange(): lax.all_to_all(pieces, 'head', 0, 0, tiled=True, axis_index_groups=[[k ^...]
    all_to_all x1, starting transfers between devices: 3.86 us -> 7.97 us  [exchange(): lax.all_to_all(pieces, 'head', 0, 0, tiled=True, axis_index_groups=[[k ^...]
    all_to_all x2, blocking collectives: 30 us -> 26.2 us  [exchange(): lax.all_to_all(pieces, 'head', 0, 0, tiled=True, axis_index_groups=[[k ^...]
  transfers between devices with their start and end apart: 2 -> 2, of which waited for: 2 -> 1; matrix products, arithmetic and copies ran while one was open for 0% -> 0% of each run, Pallas kernels for 5% -> 6%
where the time goes in v7:
time: 43.2 us; the launch traced here: 42.9 us
  blocking collectives  26.2 us (61%)
  starting transfers between devices  8.45 us (20%)
  Pallas kernels  5.62 us (13%)
  waiting for transfers between devices  0.99 us (2%)
  between operations  0.85 us (2%)
  other arithmetic  0.71 us (2%)
    all_to_all x2, blocking collectives, exchange(): lax.all_to_all(pieces, 'head', 0, 0, tiled=True, axis_index_groups=[[k ^...  26.2 us
    all_to_all x1, starting transfers between devices, exchange(): lax.all_to_all(pieces, 'head', 0, 0, tiled=True, axis_index_groups=[[k ^...  7.97 us
    pallas_call x1, Pallas kernels, body(): call(memory_kernel, [(memory.shape, BF16), ((H * rows, batch), F32), ((H,...  2.41 us
    pallas_call x1, Pallas kernels, body(): call(project_kernel, [((count, batch + batch // 2 + 4, width), BF16), ((H...  1.49 us
    pallas_call x1, Pallas kernels, body(): call(output_kernel, [piece], 5, flops=30000000)  1.05 us
    ppermute x1, waiting for transfers between devices, body(): lax.ppermute(arrived[:, batch:], 'head', [(i, i ^ 1) for i in range(count)])  0.99 us
  transfers between devices with their start and end apart: 2, of which 1 were waited for; matrix products, arithmetic and copies ran while one was open for 0% of the time, Pallas kernels for 6%

profile of v7, /device:TPU:1, one launch (start us, length us, event | category | flops | bytes accessed | tf_op | source)
XLA Modules:
  0.0 42.9 jit_solution(3597465724233610300)
XLA Ops:
  0.6 0.7 %convert_element_type.3.in_ref = bf16[24,128]{1,0:T(8,128)(2,1)S(1)} convert(f32[24,128]{1,0:T(8,128)} %residual_ref.1) | non-fusion elementwise | flops 3072 | bytes 18432 | tf_op jit(solution)/shard_map/convert_element_type | solution.py:248
  1.3 0.0 copy-start
  1.3 0.0 copy-start.2
  1.3 0.0 copy-start.3
  1.4 0.0 copy-start.4
  1.4 0.0 copy-start.5
  1.4 0.0 copy-start.6
  1.4 0.0 copy-start.7
  1.4 0.0 copy-start.8
  1.4 0.0 copy-start.9
  1.4 0.0 copy-start.11
  1.4 0.0 copy-start.12
  1.4 0.0 copy-start.13
  1.5 0.0 copy-start.14
  1.5 0.0 copy-start.15
  1.5 13.6 %all_to_all.15.x_ref = bf16[32,24,128]{2,1,0:T(8,128)(2,1)S(1)} all-to-all(bf16[32,24,128]{2,1,0:T(8,128)(2,1)S(1)} %shard_map.183), channel_id=1, replica_groups={{21,20,23,22,17,16,19,18,29,28,31,30,25,24,27,26,5,4,7,6,1,0,3,2,13,12,..., dimensions={0} | all-to-all | bytes 393216 | tf_op jit(solution)/shard_map/all_to_all | solution.py:26
  15.1 0.0 copy-done
  15.1 0.0 copy-done.2
  15.1 0.0 copy-done.3
  15.1 0.0 copy-done.4
  15.1 0.0 copy-done.5
  15.1 0.0 copy-done.6
  15.1 0.0 copy-done.7
  15.1 0.0 copy-done.8
  15.1 0.0 copy-done.9
  15.1 0.0 copy-done.11
  15.2 0.0 copy-done.12
  15.2 0.0 copy-done.13
  15.2 0.0 copy-done.14
  15.2 0.0 copy-done.15
  15.2 0.0 copy-start.1
  15.2 1.5 %shard_map.184 = (bf16[32,40,128]{2,1,0:T(8,128)(2,1)S(1)}, f32[64,24]{1,0:T(8,128)S(1)}, f32[8,24]{1,0:T(8,128)S(1)}, f32[64,24]{1,0:T(8,128)S(1)}, f32[64,24]{...) custom-call(bf16[32,24,128]{2,1,0:T(8,128)(2,1)S(1)} %all_to_all.15.x_ref, ...), custom_call_target="tpu_custom_call" | custom-call | flops 100000000 | bytes 2000000 | tf_op jit(solution)/shard_map/pallas_call | solution.py:271
  16.7 12.6 %all_to_all.16.in_ref.mine_ref = bf16[32,40,128]{2,1,0:T(8,128)(2,1)S(1)} all-to-all(bf16[32,40,128]{2,1,0:T(8,128)(2,1)S(1)} %get-tuple-element.15), channel_id=1, replica_groups={{21,20,23,22,17,16,19,18,29,28,31,30,25,24,27,26,5,4,7,6,1,0,3,2,13,12,..., dimensions={0} | all-to-all | bytes 655360 | tf_op jit(solution)/shard_map/all_to_all | solution.py:26
  29.3 0.0 copy-done.1
  29.3 1.0 %shard_map.185 = bf16[32,24,128]{2,1,0:T(8,128)(2,1)} custom-call(bf16[32,40,128]{2,1,0:T(8,128)(2,1)S(1)} %all_to_all.16.in_ref.mine_ref, f32[24,128]{1,0:T(8,128)S(1)} %get-tuple-element.16.sum_scale_ref, f32[24,128]{1,0:T(8,128)S(1)} %get-tuple-element.17.own_ref, f32[24,128]{1,0:T(8,128)S(1)} %get-tuple-element.18.floor_ref, bf16[128,4096]{1,0:T(8,128)(2,1)S(1)} %copy-done.1), custom_call_target="tpu_custom_call" | custom-call | flops 30000000 | bytes 2000000 | tf_op jit(solution)/shard_map/pallas_call | solution.py:293
  30.4 0.0 copy-start.10
  30.4 8.0 %all-to-all-start.2 = ((bf16[32,24,128]{2,1,0:T(8,128)(2,1)}), bf16[32,24,128]{2,1,0:T(8,128)(2,1)S(1)}, u32[]{:S(2)}, u32[]{:S(2)}) async-start(bf16[32,24,128]{2,1,0:T(8,128)(2,1)} %shard_map.185), calls=%async_computation.2 | async-start | bytes 393216 | tf_op jit(solution)/shard_map/all_to_all | solution.py:26
  38.4 0.5 %collective-permute-start = (bf16[32,16,128]{2,1,0:T(8,128)(2,1)S(1)}, bf16[32,16,128]{2,1,0:T(8,128)(2,1)S(1)}, u32[]{:S(2)}, u32[]{:S(2)}) collective-permute-start(bf16[32,16,128]{2,1,0:T(8,128)(2,1)S(1)} %slice.4), channel_id=1, source_target_pairs={{0,1},{1,0},{2,3},{3,2},{4,5},{5,4},{6,7},{7,6},{8,9},{9,8},{10,11... | collective-permute-start | bytes 393224 | tf_op jit(solution)/shard_map/swap/ppermute | solution.py:298
  38.9 1.0 %collective-permute-done.other_ref = bf16[32,16,128]{2,1,0:T(8,128)(2,1)S(1)} collective-permute-done((bf16[32,16,128]{2,1,0:T(8,128)(2,1)S(1)}, bf16[32,16,128]{2,1,0:T(8,128)(2,1)S(1)}, u32[]{:S(2)}, u32[]{:S(2)}) %collective-permute-start) | collective-permute-done | bytes 131104 | tf_op jit(solution)/shard_map/swap/ppermute | solution.py:298
  39.9 2.4 %shard_map.187 = (bf16[24,8,8,512]{3,2,1,0:T(8,128)(2,1)}, f32[64,24]{1,0:T(8,128)}, f32[8,24]{1,0:T(8,128)}) custom-call(f32[64,24]{1,0:T(8,128)S(1)} %get-tuple-element.19.f_rows_ref, f32[64,24]{1,0:T(8,128)S(1)} %get-tuple-element.20.ik_rows_ref, f32[64,24]{1,0:T(8,128)S(1)} %get-tuple-element.21.norm_ref, f32[8,24]{1,0:T(8,128)S(1)} %get-tuple-element.22.stab_ref, ...), custom_call_target="tpu_custom_call" | custom-call | flops 100000000 | bytes 2000000 | tf_op jit(solution)/shard_map/pallas_call | solution.py:299
  42.3 0.0 all-to-all-done.2.in_ref
  42.3 0.0 copy-done.10
  42.3 0.6 %shard_map.186 = f32[24,128]{1,0:T(8,128)} custom-call(bf16[32,24,128]{2,1,0:T(8,128)(2,1)S(1)} %all-to-all-done.2.in_ref, f32[24,128]{1,0:T(8,128)S(1)} %copy-done.10), custom_call_target="tpu_custom_call" | custom-call | flops 1000000 | bytes 2000000 | tf_op jit(solution)/shard_map/pallas_call | solution.py:306
  (2 shorter events, 0.0 us)
Async XLA Ops:
  1.3 13.7 %copy-start = (bf16[24,8,8,512]{3,2,1,0:T(8,128)(2,1)S(1)}, bf16[24,8,8,512]{3,2,1,0:T(8,128)(2,1)}, u32[]{:S(2)}) copy-start(bf16[24,8,8,512]{3,2,1,0:T(8,128)(2,1)} %mem_ref.1) | copy-start | bytes 4718596
  1.3 13.7 %copy-start.2 = (bf16[4096,128]{1,0:T(8,128)(2,1)S(1)}, bf16[4096,128]{1,0:T(8,128)(2,1)}, u32[]{:S(2)}) copy-start(bf16[4096,128]{1,0:T(8,128)(2,1)} %wv_ref.1) | copy-start | bytes 3145732
  1.3 13.7 %copy-start.3 = (bf16[4096,128]{1,0:T(8,128)(2,1)S(1)}, bf16[4096,128]{1,0:T(8,128)(2,1)}, u32[]{:S(2)}) copy-start(bf16[4096,128]{1,0:T(8,128)(2,1)} %wg_ref.1) | copy-start | bytes 3145732
  1.4 13.7 %copy-start.4 = (bf16[8,8,4096]{2,1,0:T(8,128)(2,1)S(1)}, bf16[8,8,4096]{2,1,0:T(8,128)(2,1)}, u32[]{:S(2)}) copy-start(bf16[8,8,4096]{2,1,0:T(8,128)(2,1)} %param.18) | copy-start | bytes 1572868
  1.4 13.7 %copy-start.5 = (bf16[8,8,4096]{2,1,0:T(8,128)(2,1)S(1)}, bf16[8,8,4096]{2,1,0:T(8,128)(2,1)}, u32[]{:S(2)}) copy-start(bf16[8,8,4096]{2,1,0:T(8,128)(2,1)} %param.19) | copy-start | bytes 1572868
  1.4 13.7 %copy-start.6 = (bf16[64,3072]{1,0:T(8,128)(2,1)S(1)}, bf16[64,3072]{1,0:T(8,128)(2,1)}, u32[]{:S(2)}) copy-start(bf16[64,3072]{1,0:T(8,128)(2,1)} %constant.4.clone.repeat_ref) | copy-start | bytes 1179652
  1.4 13.7 %copy-start.7 = (bf16[96,384]{1,0:T(8,128)(2,1)S(1)}, bf16[96,384]{1,0:T(8,128)(2,1)}, u32[]{:S(2)}) copy-start(bf16[96,384]{1,0:T(8,128)(2,1)} %constant.5.clone.own_ref) | copy-start | bytes 221188
  1.4 13.7 %copy-start.8 = (bf16[8,4096]{1,0:T(8,128)(2,1)S(1)}, bf16[8,4096]{1,0:T(8,128)(2,1)}, u32[]{:S(2)}) copy-start(bf16[8,4096]{1,0:T(8,128)(2,1)} %wi_ref.1) | copy-start | bytes 196612
  1.4 13.7 %copy-start.9 = (bf16[8,4096]{1,0:T(8,128)(2,1)S(1)}, bf16[8,4096]{1,0:T(8,128)(2,1)}, u32[]{:S(2)}) copy-start(bf16[8,4096]{1,0:T(8,128)(2,1)} %wf_ref.1) | copy-start | bytes 196612
  1.4 13.7 %copy-start.11 = (f32[24,8,8]{0,2,1:T(8,128)S(1)}, f32[24,8,8]{0,2,1:T(8,128)}, u32[]{:S(2)}) copy-start(f32[24,8,8]{0,2,1:T(8,128)} %param.28) | copy-start | bytes 18436
  1.4 13.7 %copy-start.12 = (f32[4096]{0:T(1024)S(1)}, f32[4096]{0:T(1024)}, u32[]{:S(2)}) copy-start(f32[4096]{0:T(1024)} %param.17) | copy-start | bytes 49156
  1.4 13.7 %copy-start.13 = (f32[24,8]{0,1:T(8,128)S(1)}, f32[24,8]{0,1:T(8,128)}, u32[]{:S(2)}) copy-start(f32[24,8]{0,1:T(8,128)} %param.29) | copy-start | bytes 2308
  1.5 13.7 %copy-start.14 = (f32[8]{0:T(128)S(1)}, f32[8]{0:T(128)}, u32[]{:S(2)}) copy-start(f32[8]{0:T(128)} %param.24) | copy-start | bytes 100
  1.5 13.7 %copy-start.15 = (f32[8]{0:T(128)S(1)}, f32[8]{0:T(128)}, u32[]{:S(2)}) copy-start(f32[8]{0:T(128)} %param.25) | copy-start | bytes 100
  15.2 14.1 %copy-start.1 = (bf16[128,4096]{1,0:T(8,128)(2,1)S(1)}, bf16[128,4096]{1,0:T(8,128)(2,1)}, u32[]{:S(2)}) copy-start(bf16[128,4096]{1,0:T(8,128)(2,1)} %wo_ref.1) | copy-start | bytes 3145732
  30.4 11.9 %copy-start.10 = (f32[24,128]{1,0:T(8,128)S(1)}, f32[24,128]{1,0:T(8,128)}, u32[]{:S(2)}) copy-start(f32[24,128]{1,0:T(8,128)} %residual_ref.1) | copy-start | bytes 36868
  30.4 11.9 %all-to-all-start.2 = ((bf16[32,24,128]{2,1,0:T(8,128)(2,1)}), bf16[32,24,128]{2,1,0:T(8,128)(2,1)S(1)}, u32[]{:S(2)}, u32[]{:S(2)}) async-start(bf16[32,24,128]{2,1,0:T(8,128)(2,1)} %shard_map.185), calls=%async_computation.2 | async-start | bytes 393216 | tf_op jit(solution)/shard_map/all_to_all | solution.py:26
  38.4 1.5 %collective-permute-start = (bf16[32,16,128]{2,1,0:T(8,128)(2,1)S(1)}, bf16[32,16,128]{2,1,0:T(8,128)(2,1)S(1)}, u32[]{:S(2)}, u32[]{:S(2)}) collective-permute-start(bf16[32,16,128]{2,1,0:T(8,128)(2,1)S(1)} %slice.4), channel_id=1, source_target_pairs={{0,1},{1,0},{2,3},{3,2},{4,5},{5,4},{6,7},{7,6},{8,9},{9,8},{10,11... | collective-permute-start | bytes 393224 | tf_op jit(solution)/shard_map/swap/ppermute | solution.py:298

commit v8 on v7

--- a/solution.py
+++ b/solution.py
@@ -17,6 +17,7 @@
 STATS = 8
 
 
+CHUNKS = 3
 FAR = 21
 SPREAD_FLOPS = 10_000_000_000
 
@@ -173,35 +174,55 @@
         out_ref[(j + 1) ^ FAR] = pair[:, width:]
 
 
-def memory_kernel(
-    f_rows_ref, ik_rows_ref, norm_ref, stab_ref, mine_ref, other_ref, mem_ref,
-    out_ref, norm_out_ref, stab_out_ref, wide_ref,
-):
-    norm_out_ref[...] = norm_ref[...]
-    stab_out_ref[...] = stab_ref[...]
-    pieces = mine_ref.shape[0]
-    batch, _, rows, _ = mem_ref.shape
-    width = mine_ref.shape[2]
-    half = batch // 2
+def memory_half(side, f_rows_ref, ik_rows_ref, half_ref, mem_ref, out_hbm, wide_ref, new_ref, sems):
+    pieces, depth, width = half_ref.shape
+    _, _, rows, _ = mem_ref.shape
+    half = wide_ref.shape[1]
     share = pieces // H
-    even = lax.axis_index("head") % 2 == 0
+    first = depth - 16
+    lower = lax.axis_index("head") % 2 == side
+    base = jnp.where(lower, 0, half)
     for j in range(pieces):
         cut = slice((j % share) * width, (j % share + 1) * width)
-        mine = mine_ref[j ^ FAR, batch : batch + 16].astype(F32)[:half]
-        other = other_ref[j ^ FAR].astype(F32)[:half]
-        wide_ref[j // share, :half, cut] = jnp.where(even, mine, other)
-        wide_ref[j // share, half:, cut] = jnp.where(even, other, mine)
-
-    def one_head(h, carry):
-        at = pl.multiple_of(h * rows, rows)
-        f_rows = f_rows_ref[pl.ds(at, rows), :]
-        ik_rows = ik_rows_ref[pl.ds(at, rows), :]
-        for b in range(batch):
-            kept = f_rows[:, b : b + 1] * mem_ref[b, h].astype(F32)
-            out_ref[b, h] = (kept + ik_rows[:, b : b + 1] * wide_ref[h, b : b + 1, :]).astype(BF16)
-        return carry
-
-    lax.fori_loop(0, H, one_head, 0)
+        wide_ref[j // share, :, cut] = half_ref[j ^ FAR, first:].astype(F32)[:half]
+
+    f_mine = jnp.where(lower, f_rows_ref[:, :half], f_rows_ref[:, half:])
+    ik_mine = jnp.where(lower, ik_rows_ref[:, :half], ik_rows_ref[:, half:])
+    step = half // CHUNKS
+    copies = []
+    for k in range(CHUNKS):
+        for h in range(H):
+            part = slice(h * rows, (h + 1) * rows)
+            for i in range(k * step, (k + 1) * step):
+                kept = f_mine[part, i : i + 1] * mem_ref[base + i, h].astype(F32)
+                added = ik_mine[part, i : i + 1] * wide_ref[h, i : i + 1, :]
+                new_ref[i, h] = (kept + added).astype(BF16)
+        source = new_ref.at[k * step : (k + 1) * step]
+        target = out_hbm.at[pl.ds(base + k * step, step)]
+        copies.append(pltpu.make_async_copy(source, target, sems.at[k]))
+        copies[-1].start()
+    for copy in copies:
+        copy.wait()
+
+
+def memory_mine_kernel(
+    f_rows_ref, ik_rows_ref, norm_ref, stab_ref, half_ref, mem_ref,
+    out_hbm, norm_out_hbm, stab_out_hbm, wide_ref, new_ref, sems, small_sems,
+):
+    norm_copy = pltpu.make_async_copy(norm_ref, norm_out_hbm, small_sems.at[0])
+    stab_copy = pltpu.make_async_copy(stab_ref, stab_out_hbm, small_sems.at[1])
+    norm_copy.start()
+    stab_copy.start()
+    memory_half(0, f_rows_ref, ik_rows_ref, half_ref, mem_ref, out_hbm, wide_ref, new_ref, sems)
+    norm_copy.wait()
+    stab_copy.wait()
+
+
+def memory_other_kernel(
+    f_rows_ref, ik_rows_ref, half_ref, mem_ref, partial_hbm, out_hbm, wide_ref, new_ref, sems
+):
+    del partial_hbm
+    memory_half(1, f_rows_ref, ik_rows_ref, half_ref, mem_ref, out_hbm, wide_ref, new_ref, sems)
 
 
 def finish_kernel(in_ref, residual_ref, out_ref):
@@ -212,13 +233,15 @@
     out_ref[...] = total + acc
 
 
-def call(kernel, outs, n_in, scratch=(), flops=1_000_000):
+def call(kernel, outs, n_in, scratch=(), flops=1_000_000, hbm_out=False, alias=False):
+    vmem, hbm = (pl.BlockSpec(memory_space=space) for space in (pltpu.VMEM, pltpu.HBM))
     return pl.pallas_call(
         kernel,
         out_shape=[jax.ShapeDtypeStruct(*out) for out in outs],
-        in_specs=[pl.BlockSpec(memory_space=pltpu.VMEM)] * n_in,
-        out_specs=[pl.BlockSpec(memory_space=pltpu.VMEM)] * len(outs),
+        in_specs=[vmem] * n_in + [hbm] * alias,
+        out_specs=[hbm if hbm_out else vmem] * len(outs),
         scratch_shapes=list(scratch),
+        input_output_aliases={n_in: 0} if alias else {},
         compiler_params=pltpu.CompilerParams(vmem_limit_bytes=16 * 2**20),
         cost_estimate=pl.CostEstimate(flops=flops, bytes_accessed=2_000_000, transcendentals=0),
     )
@@ -296,13 +319,28 @@
     returned = exchange(branch, FAR)
     with jax.named_scope("swap"):
         other = lax.ppermute(arrived[:, batch:], "head", [(i, i ^ 1) for i in range(count)])
-    mem_new, norm_out, stab_out = call(
-        memory_kernel,
+    half_scratch = [
+        pltpu.VMEM((H, batch // 2, DV), F32),
+        pltpu.VMEM((batch // 2, *memory.shape[1:]), BF16),
+        pltpu.SemaphoreType.DMA((CHUNKS,)),
+    ]
+    mem_half, norm_out, stab_out = call(
+        memory_mine_kernel,
         [(memory.shape, BF16), ((H * rows, batch), F32), ((H, batch), F32)],
-        7,
-        scratch=[pltpu.VMEM((H, batch, DV), F32)],
-        flops=100_000_000,
-    )(f_rows, ik_rows, norm_new, stab_new, arrived, other, memory)
+        6,
+        scratch=[*half_scratch, pltpu.SemaphoreType.DMA((2,))],
+        flops=50_000_000,
+        hbm_out=True,
+    )(f_rows, ik_rows, norm_new, stab_new, arrived, memory)
+    (mem_new,) = call(
+        memory_other_kernel,
+        [(memory.shape, BF16)],
+        4,
+        scratch=half_scratch,
+        flops=50_000_000,
+        hbm_out=True,
+        alias=True,
+    )(f_rows, ik_rows, other, memory, mem_half)
     (res_out,) = call(finish_kernel, [((batch, width), F32)], 2)(returned, residual)
     norm_out = norm_out.reshape(H, rows, batch).transpose(2, 0, 1)
     return res_out, mem_new, norm_out, stab_out.T

time: 43.2 us -> 42.8 us (level)
    ppermute x1, waiting for transfers between devices: 0.99 us -> 0.01 us  [body(): lax.ppermute(arrived[:, batch:], 'head', [(i, i ^ 1) for i in range(count)])]
    all_to_all x1, waiting for transfers between devices: 0.01 us -> 0.61 us  [exchange(): lax.all_to_all(pieces, 'head', 0, 0, tiled=True, axis_index_groups=[[k ^...]
    pallas_call x1 -> x2, Pallas kernels: 2.41 us -> 2.42 us  [the longest x1 1.22 us: body(): call(memory_mine_kernel, [(memory.shape, BF16), ((H * rows, batch), F32),...]
where the time goes in v8:
time: 42.8 us; the launch traced here: 42.5 us
  blocking collectives  26.2 us (61%)
  starting transfers between devices  8.32 us (19%)
  Pallas kernels  5.63 us (13%)
  between operations  0.88 us (2%)
  other arithmetic  0.71 us (2%)
  waiting for transfers between devices  0.61 us (1%)
    all_to_all x2, blocking collectives, exchange(): lax.all_to_all(pieces, 'head', 0, 0, tiled=True, axis_index_groups=[[k ^...  26.2 us
    all_to_all x1, starting transfers between devices, exchange(): lax.all_to_all(pieces, 'head', 0, 0, tiled=True, axis_index_groups=[[k ^...  7.83 us
    pallas_call x1, Pallas kernels, body(): call(project_kernel, [((count, batch + batch // 2 + 4, width), BF16), ((H...  1.49 us
    pallas_call x1, Pallas kernels, body(): call(memory_mine_kernel, [(memory.shape, BF16), ((H * rows, batch), F32),...  1.22 us
    pallas_call x1, Pallas kernels, body(): call(memory_other_kernel, [(memory.shape, BF16)], 4, scratch=half_scratch...  1.2 us
    pallas_call x1, Pallas kernels, body(): call(output_kernel, [piece], 5, flops=30000000)  1.05 us
  transfers between devices with their start and end apart: 2, of which 1 were waited for; matrix products, arithmetic and copies ran while one was open for 0% of the time, Pallas kernels for 6%

profile of v8, /device:TPU:1, one launch (start us, length us, event | category | flops | bytes accessed | tf_op | source)
XLA Modules:
  0.0 42.5 jit_solution(16525663656864561259)
XLA Ops:
  0.6 0.7 %convert_element_type.3.in_ref = bf16[24,128]{1,0:T(8,128)(2,1)S(1)} convert(f32[24,128]{1,0:T(8,128)} %residual_ref.1) | non-fusion elementwise | flops 3072 | bytes 18432 | tf_op jit(solution)/shard_map/convert_element_type | solution.py:271
  1.3 0.0 copy-start
  1.3 0.0 copy-start.2
  1.3 0.0 copy-start.3
  1.4 0.0 copy-start.4
  1.4 0.0 copy-start.5
  1.4 0.0 copy-start.6
  1.4 0.0 copy-start.7
  1.4 0.0 copy-start.8
  1.4 0.0 copy-start.9
  1.4 0.0 copy-start.11
  1.4 0.0 copy-start.12
  1.4 0.0 copy-start.13
  1.5 0.0 copy-start.14
  1.5 0.0 copy-start.15
  1.5 13.6 %all_to_all.15.x_ref = bf16[32,24,128]{2,1,0:T(8,128)(2,1)S(1)} all-to-all(bf16[32,24,128]{2,1,0:T(8,128)(2,1)S(1)} %shard_map.183), channel_id=1, replica_groups={{21,20,23,22,17,16,19,18,29,28,31,30,25,24,27,26,5,4,7,6,1,0,3,2,13,12,..., dimensions={0} | all-to-all | bytes 393216 | tf_op jit(solution)/shard_map/all_to_all | solution.py:27
  15.1 0.0 copy-done
  15.1 0.0 copy-done.2
  15.1 0.0 copy-done.3
  15.1 0.0 copy-done.4
  15.1 0.0 copy-done.5
  15.1 0.0 copy-done.6
  15.1 0.0 copy-done.7
  15.1 0.0 copy-done.8
  15.1 0.0 copy-done.9
  15.1 0.0 copy-done.11
  15.2 0.0 copy-done.12
  15.2 0.0 copy-done.13
  15.2 0.0 copy-done.14
  15.2 0.0 copy-done.15
  15.2 0.0 copy-start.1
  15.2 1.5 %shard_map.184 = (bf16[32,40,128]{2,1,0:T(8,128)(2,1)S(1)}, f32[64,24]{1,0:T(8,128)S(1)}, f32[8,24]{1,0:T(8,128)S(1)}, f32[64,24]{1,0:T(8,128)S(1)}, f32[64,24]{...) custom-call(bf16[32,24,128]{2,1,0:T(8,128)(2,1)S(1)} %all_to_all.15.x_ref, ...), custom_call_target="tpu_custom_call" | custom-call | flops 100000000 | bytes 2000000 | tf_op jit(solution)/shard_map/pallas_call | solution.py:294
  16.7 12.6 %all_to_all.16.in_ref.half_ref = bf16[32,40,128]{2,1,0:T(8,128)(2,1)S(1)} all-to-all(bf16[32,40,128]{2,1,0:T(8,128)(2,1)S(1)} %get-tuple-element.15), channel_id=1, replica_groups={{21,20,23,22,17,16,19,18,29,28,31,30,25,24,27,26,5,4,7,6,1,0,3,2,13,12,..., dimensions={0} | all-to-all | bytes 655360 | tf_op jit(solution)/shard_map/all_to_all | solution.py:27
  29.3 0.0 copy-done.1
  29.3 1.0 %shard_map.185 = bf16[32,24,128]{2,1,0:T(8,128)(2,1)} custom-call(bf16[32,40,128]{2,1,0:T(8,128)(2,1)S(1)} %all_to_all.16.in_ref.half_ref, f32[24,128]{1,0:T(8,128)S(1)} %get-tuple-element.16.sum_scale_ref, f32[24,128]{1,0:T(8,128)S(1)} %get-tuple-element.17.own_ref, f32[24,128]{1,0:T(8,128)S(1)} %get-tuple-element.18.floor_ref, bf16[128,4096]{1,0:T(8,128)(2,1)S(1)} %copy-done.1), custom_call_target="tpu_custom_call" | custom-call | flops 30000000 | bytes 2000000 | tf_op jit(solution)/shard_map/pallas_call | solution.py:316
  30.4 7.8 %all-to-all-start.2 = ((bf16[32,24,128]{2,1,0:T(8,128)(2,1)}), bf16[32,24,128]{2,1,0:T(8,128)(2,1)S(1)}, u32[]{:S(2)}, u32[]{:S(2)}) async-start(bf16[32,24,128]{2,1,0:T(8,128)(2,1)} %shard_map.185), calls=%async_computation.2 | async-start | bytes 393216 | tf_op jit(solution)/shard_map/all_to_all | solution.py:27
  38.2 0.5 %collective-permute-start = (bf16[32,16,128]{2,1,0:T(8,128)(2,1)S(1)}, bf16[32,16,128]{2,1,0:T(8,128)(2,1)S(1)}, u32[]{:S(2)}, u32[]{:S(2)}) collective-permute-start(bf16[32,16,128]{2,1,0:T(8,128)(2,1)S(1)} %slice.4), channel_id=1, source_target_pairs={{0,1},{1,0},{2,3},{3,2},{4,5},{5,4},{6,7},{7,6},{8,9},{9,8},{10,11... | collective-permute-start | bytes 393224 | tf_op jit(solution)/shard_map/swap/ppermute | solution.py:321
  38.7 1.2 %shard_map.187 = (bf16[24,8,8,512]{3,2,1,0:T(8,128)(2,1)}, f32[64,24]{1,0:T(8,128)}, f32[8,24]{1,0:T(8,128)}) custom-call(f32[64,24]{1,0:T(8,128)S(1)} %get-tuple-element.19.f_rows_ref, f32[64,24]{1,0:T(8,128)S(1)} %get-tuple-element.20.ik_rows_ref, f32[64,24]{1,0:T(8,128)S(1)} %get-tuple-element.21.norm_ref, f32[8,24]{1,0:T(8,128)S(1)} %get-tuple-element.22.stab_ref, ...), custom_call_target="tpu_custom_call" | custom-call | flops 50000000 | bytes 2000000 | tf_op jit(solution)/shard_map/pallas_call | solution.py:327
  40.0 0.0 collective-permute-done.half_ref
  40.0 0.0 copy-start.10
  40.0 1.2 %shard_map.188 = bf16[24,8,8,512]{3,2,1,0:T(8,128)(2,1)} custom-call(f32[64,24]{1,0:T(8,128)S(1)} %get-tuple-element.19.f_rows_ref, f32[64,24]{1,0:T(8,128)S(1)} %get-tuple-element.20.ik_rows_ref, bf16[32,16,128]{2,1,0:T(8,128)(2,1)S(1)} %collective-permute-done.half_ref, bf16[24,8,8,512]{3,2,1,0:T(8,128)(2,1)S(1)} %copy-done, ...), custom_call_target="tpu_custom_call", output_to_operand_aliasing={{}: (4, {})} | custom-call | flops 50000000 | bytes 2000000 | tf_op jit(solution)/shard_map/pallas_call | solution.py:335
  41.2 0.6 %all-to-all-done.2.in_ref = bf16[32,24,128]{2,1,0:T(8,128)(2,1)S(1)} async-done(((bf16[32,24,128]{2,1,0:T(8,128)(2,1)}), bf16[32,24,128]{2,1,0:T(8,128)(2,1)S(1)}, u32[]{:S(2)}, u32[]{:S(2)}) %all-to-all-start.2) | async-done | bytes 196640 | tf_op jit(solution)/shard_map/all_to_all | solution.py:27
  41.8 0.0 copy-done.10
  41.8 0.6 %shard_map.186 = f32[24,128]{1,0:T(8,128)} custom-call(bf16[32,24,128]{2,1,0:T(8,128)(2,1)S(1)} %all-to-all-done.2.in_ref, f32[24,128]{1,0:T(8,128)S(1)} %copy-done.10), custom_call_target="tpu_custom_call" | custom-call | flops 1000000 | bytes 2000000 | tf_op jit(solution)/shard_map/pallas_call | solution.py:344
  (2 shorter events, 0.0 us)
Async XLA Ops:
  1.3 13.7 %copy-start = (bf16[24,8,8,512]{3,2,1,0:T(8,128)(2,1)S(1)}, bf16[24,8,8,512]{3,2,1,0:T(8,128)(2,1)}, u32[]{:S(2)}) copy-start(bf16[24,8,8,512]{3,2,1,0:T(8,128)(2,1)} %mem_ref.3) | copy-start | bytes 4718596
  1.3 13.7 %copy-start.2 = (bf16[4096,128]{1,0:T(8,128)(2,1)S(1)}, bf16[4096,128]{1,0:T(8,128)(2,1)}, u32[]{:S(2)}) copy-start(bf16[4096,128]{1,0:T(8,128)(2,1)} %wv_ref.1) | copy-start | bytes 3145732
  1.3 13.7 %copy-start.3 = (bf16[4096,128]{1,0:T(8,128)(2,1)S(1)}, bf16[4096,128]{1,0:T(8,128)(2,1)}, u32[]{:S(2)}) copy-start(bf16[4096,128]{1,0:T(8,128)(2,1)} %wg_ref.1) | copy-start | bytes 3145732
  1.4 13.7 %copy-start.4 = (bf16[8,8,4096]{2,1,0:T(8,128)(2,1)S(1)}, bf16[8,8,4096]{2,1,0:T(8,128)(2,1)}, u32[]{:S(2)}) copy-start(bf16[8,8,4096]{2,1,0:T(8,128)(2,1)} %param.18) | copy-start | bytes 1572868
  1.4 13.7 %copy-start.5 = (bf16[8,8,4096]{2,1,0:T(8,128)(2,1)S(1)}, bf16[8,8,4096]{2,1,0:T(8,128)(2,1)}, u32[]{:S(2)}) copy-start(bf16[8,8,4096]{2,1,0:T(8,128)(2,1)} %param.19) | copy-start | bytes 1572868
  1.4 13.7 %copy-start.6 = (bf16[64,3072]{1,0:T(8,128)(2,1)S(1)}, bf16[64,3072]{1,0:T(8,128)(2,1)}, u32[]{:S(2)}) copy-start(bf16[64,3072]{1,0:T(8,128)(2,1)} %constant.4.clone.repeat_ref) | copy-start | bytes 1179652
  1.4 13.7 %copy-start.7 = (bf16[96,384]{1,0:T(8,128)(2,1)S(1)}, bf16[96,384]{1,0:T(8,128)(2,1)}, u32[]{:S(2)}) copy-start(bf16[96,384]{1,0:T(8,128)(2,1)} %constant.5.clone.own_ref) | copy-start | bytes 221188
  1.4 13.7 %copy-start.8 = (bf16[8,4096]{1,0:T(8,128)(2,1)S(1)}, bf16[8,4096]{1,0:T(8,128)(2,1)}, u32[]{:S(2)}) copy-start(bf16[8,4096]{1,0:T(8,128)(2,1)} %wi_ref.1) | copy-start | bytes 196612
  1.4 13.7 %copy-start.9 = (bf16[8,4096]{1,0:T(8,128)(2,1)S(1)}, bf16[8,4096]{1,0:T(8,128)(2,1)}, u32[]{:S(2)}) copy-start(bf16[8,4096]{1,0:T(8,128)(2,1)} %wf_ref.1) | copy-start | bytes 196612
  1.4 13.7 %copy-start.11 = (f32[24,8,8]{0,2,1:T(8,128)S(1)}, f32[24,8,8]{0,2,1:T(8,128)}, u32[]{:S(2)}) copy-start(f32[24,8,8]{0,2,1:T(8,128)} %param.28) | copy-start | bytes 18436
  1.4 13.7 %copy-start.12 = (f32[4096]{0:T(1024)S(1)}, f32[4096]{0:T(1024)}, u32[]{:S(2)}) copy-start(f32[4096]{0:T(1024)} %param.17) | copy-start | bytes 49156
  1.4 13.7 %copy-start.13 = (f32[24,8]{0,1:T(8,128)S(1)}, f32[24,8]{0,1:T(8,128)}, u32[]{:S(2)}) copy-start(f32[24,8]{0,1:T(8,128)} %param.29) | copy-start | bytes 2308
  1.5 13.7 %copy-start.14 = (f32[8]{0:T(128)S(1)}, f32[8]{0:T(128)}, u32[]{:S(2)}) copy-start(f32[8]{0:T(128)} %param.24) | copy-start | bytes 100
  1.5 13.7 %copy-start.15 = (f32[8]{0:T(128)S(1)}, f32[8]{0:T(128)}, u32[]{:S(2)}) copy-start(f32[8]{0:T(128)} %param.25) | copy-start | bytes 100
  15.2 14.1 %copy-start.1 = (bf16[128,4096]{1,0:T(8,128)(2,1)S(1)}, bf16[128,4096]{1,0:T(8,128)(2,1)}, u32[]{:S(2)}) copy-start(bf16[128,4096]{1,0:T(8,128)(2,1)} %wo_ref.1) | copy-start | bytes 3145732
  30.4 11.4 %all-to-all-start.2 = ((bf16[32,24,128]{2,1,0:T(8,128)(2,1)}), bf16[32,24,128]{2,1,0:T(8,128)(2,1)S(1)}, u32[]{:S(2)}, u32[]{:S(2)}) async-start(bf16[32,24,128]{2,1,0:T(8,128)(2,1)} %shard_map.185), calls=%async_computation.2 | async-start | bytes 393216 | tf_op jit(solution)/shard_map/all_to_all | solution.py:27
  38.2 1.7 %collective-permute-start = (bf16[32,16,128]{2,1,0:T(8,128)(2,1)S(1)}, bf16[32,16,128]{2,1,0:T(8,128)(2,1)S(1)}, u32[]{:S(2)}, u32[]{:S(2)}) collective-permute-start(bf16[32,16,128]{2,1,0:T(8,128)(2,1)S(1)} %slice.4), channel_id=1, source_target_pairs={{0,1},{1,0},{2,3},{3,2},{4,5},{5,4},{6,7},{7,6},{8,9},{9,8},{10,11... | collective-permute-start | bytes 393224 | tf_op jit(solution)/shard_map/swap/ppermute | solution.py:321
  40.0 1.8 %copy-start.10 = (f32[24,128]{1,0:T(8,128)S(1)}, f32[24,128]{1,0:T(8,128)}, u32[]{:S(2)}) copy-start(f32[24,128]{1,0:T(8,128)} %residual_ref.1) | copy-start | bytes 36868

commit v9 on v8

--- a/solution.py
+++ b/solution.py
@@ -18,15 +18,13 @@
 
 
 CHUNKS = 3
-FAR = 21
+ORDER = [21 ^ k for k in (*range(0, 32, 2), *range(1, 32, 2))]
+SLOT = [ORDER.index(k) for k in range(32)]
 SPREAD_FLOPS = 10_000_000_000
 
 
-def exchange(pieces, far=0):
-    count = lax.axis_size("head")
-    return lax.all_to_all(
-        pieces, "head", 0, 0, tiled=True, axis_index_groups=[[k ^ far for k in range(count)]]
-    )
+def exchange(pieces):
+    return lax.all_to_all(pieces, "head", 0, 0, tiled=True, axis_index_groups=[ORDER])
 
 
 def dot_last(left, right):
@@ -84,7 +82,7 @@
     scale = lax.rsqrt(mean + EPSILON)
     tail_ref[...] = jnp.zeros(tail_ref.shape, F32)
     for j in range(pieces):
-        cut = slice((j ^ FAR) * width, ((j ^ FAR) + 1) * width)
+        cut = slice(ORDER[j] * width, (ORDER[j] + 1) * width)
         xn_ref[:, cut] = (x_ref[j].astype(F32) * scale * gain_ref[:, cut]).astype(BF16)
     x_norm = xn_ref[...]
 
@@ -136,7 +134,7 @@
             at = parity * 2 * batch
             numer = (product[at : at + batch] + product[at + batch : at + 2 * batch]).astype(BF16)
             for k in range(2):
-                out_ref[(h * share + 2 * k + parity) ^ FAR, :batch] = numer[:, k * width : (k + 1) * width]
+                out_ref[SLOT[h * share + 2 * k + parity], :batch] = numer[:, k * width : (k + 1) * width]
 
     value_gate = dot(x_norm, jnp.concatenate([wv_ref[...], wg_ref[...]], axis=1))
     value = value_gate[:, :width]
@@ -146,8 +144,8 @@
         for h in range(H):
             tail_ref[core, h, :4] = rest
         for j in range(core, pieces, 2):
-            out_ref[j ^ FAR, batch : batch + 8] = first
-            out_ref[j ^ FAR, batch + 8 :] = tail_ref[core, j // share].astype(BF16)
+            out_ref[SLOT[j], batch : batch + 8] = first
+            out_ref[SLOT[j], batch + 8 :] = tail_ref[core, j // share].astype(BF16)
 
     head = lax.axis_index("head") * width // DV
     pick = lambda ref: column(ref[pl.ds(head, 1), :])
@@ -170,8 +168,8 @@
     hidden = (numer / jnp.maximum(jnp.abs(norm_query), floor_ref[...])).astype(BF16)
     for j in range(0, pieces, 2):
         pair = dot(hidden, wo_ref[:, j * width : (j + 2) * width]).astype(BF16)
-        out_ref[j ^ FAR] = pair[:, :width]
-        out_ref[(j + 1) ^ FAR] = pair[:, width:]
+        out_ref[SLOT[j]] = pair[:, :width]
+        out_ref[SLOT[j + 1]] = pair[:, width:]
 
 
 def memory_half(side, f_rows_ref, ik_rows_ref, half_ref, mem_ref, out_hbm, wide_ref, new_ref, sems):
@@ -184,7 +182,7 @@
     base = jnp.where(lower, 0, half)
     for j in range(pieces):
         cut = slice((j % share) * width, (j % share + 1) * width)
-        wide_ref[j // share, :, cut] = half_ref[j ^ FAR, first:].astype(F32)[:half]
+        wide_ref[j // share, :, cut] = half_ref[SLOT[j], first:].astype(F32)[:half]
 
     f_mine = jnp.where(lower, f_rows_ref[:, :half], f_rows_ref[:, half:])
     ik_mine = jnp.where(lower, ik_rows_ref[:, :half], ik_rows_ref[:, half:])
@@ -270,7 +268,7 @@
     (pieces,) = call(spread_kernel, [((count, batch, width), BF16)], 1, flops=SPREAD_FLOPS)(
         residual.astype(BF16)
     )
-    gathered = exchange(pieces, FAR)
+    gathered = exchange(pieces)
 
     piece = ((count, batch, width), BF16)
     sources = (
@@ -312,11 +310,11 @@
         ],
         flops=100_000_000,
     )(gathered, *sources)
-    arrived = exchange(payload, FAR)
+    arrived = exchange(payload)
     (branch,) = call(output_kernel, [piece], 5, flops=30_000_000)(
         arrived, sum_scale, own, floor, w_out
     )
-    returned = exchange(branch, FAR)
+    returned = exchange(branch)
     with jax.named_scope("swap"):
         other = lax.ppermute(arrived[:, batch:], "head", [(i, i ^ 1) for i in range(count)])
     half_scratch = [

time: 42.8 us -> 42.5 us (level)
  no operation moved by 1% of the time
where the time goes in v9:
time: 42.5 us; the launch traced here: 42.2 us
  blocking collectives  26 us (61%)
  starting transfers between devices  8.41 us (20%)
  Pallas kernels  5.63 us (13%)
  between operations  0.89 us (2%)
  other arithmetic  0.71 us (2%)
  waiting for transfers between devices  0.45 us (1%)
    all_to_all x2, blocking collectives, exchange(): lax.all_to_all(pieces, 'head', 0, 0, tiled=True, axis_index_groups=[ORDER])  26 us
    all_to_all x1, starting transfers between devices, exchange(): lax.all_to_all(pieces, 'head', 0, 0, tiled=True, axis_index_groups=[ORDER])  7.88 us
    pallas_call x1, Pallas kernels, body(): call(project_kernel, [((count, batch + batch // 2 + 4, width), BF16), ((H...  1.49 us
    pallas_call x1, Pallas kernels, body(): call(memory_mine_kernel, [(memory.shape, BF16), ((H * rows, batch), F32),...  1.22 us
    pallas_call x1, Pallas kernels, body(): call(memory_other_kernel, [(memory.shape, BF16)], 4, scratch=half_scratch...  1.2 us
    pallas_call x1, Pallas kernels, body(): call(output_kernel, [piece], 5, flops=30000000)  1.05 us
  transfers between devices with their start and end apart: 2, of which 1 were waited for; matrix products, arithmetic and copies ran while one was open for 0% of the time, Pallas kernels for 6%

profile of v9, /device:TPU:1, one launch (start us, length us, event | category | flops | bytes accessed | tf_op | source)
XLA Modules:
  0.0 42.2 jit_solution(15612289764092513571)
XLA Ops:
  0.6 0.7 %convert_element_type.3.in_ref = bf16[24,128]{1,0:T(8,128)(2,1)S(1)} convert(f32[24,128]{1,0:T(8,128)} %residual_ref.1) | non-fusion elementwise | flops 3072 | bytes 18432 | tf_op jit(solution)/shard_map/convert_element_type | solution.py:269
  1.3 0.0 copy-start
  1.3 0.0 copy-start.2
  1.3 0.0 copy-start.3
  1.4 0.0 copy-start.4
  1.4 0.0 copy-start.5
  1.4 0.0 copy-start.6
  1.4 0.0 copy-start.7
  1.4 0.0 copy-start.8
  1.4 0.0 copy-start.9
  1.4 0.0 copy-start.11
  1.4 0.0 copy-start.12
  1.4 0.0 copy-start.13
  1.5 0.0 copy-start.14
  1.5 0.0 copy-start.15
  1.5 13.4 %all_to_all.15.x_ref = bf16[32,24,128]{2,1,0:T(8,128)(2,1)S(1)} all-to-all(bf16[32,24,128]{2,1,0:T(8,128)(2,1)S(1)} %shard_map.183), channel_id=1, replica_groups={{21,23,17,19,29,31,25,27,5,7,1,3,13,15,9,11,20,22,16,18,28,30,24,26,4,6..., dimensions={0} | all-to-all | bytes 393216 | tf_op jit(solution)/shard_map/all_to_all | solution.py:27
  14.9 0.0 copy-done
  14.9 0.0 copy-done.2
  14.9 0.0 copy-done.3
  15.0 0.0 copy-done.4
  15.0 0.0 copy-done.5
  15.0 0.0 copy-done.6
  15.0 0.0 copy-done.7
  15.0 0.0 copy-done.8
  15.0 0.0 copy-done.9
  15.0 0.0 copy-done.11
  15.0 0.0 copy-done.12
  15.0 0.0 copy-done.13
  15.0 0.0 copy-done.14
  15.1 0.0 copy-done.15
  15.1 0.0 copy-start.1
  15.1 1.5 %shard_map.184 = (bf16[32,40,128]{2,1,0:T(8,128)(2,1)S(1)}, f32[64,24]{1,0:T(8,128)S(1)}, f32[8,24]{1,0:T(8,128)S(1)}, f32[64,24]{1,0:T(8,128)S(1)}, f32[64,24]{...) custom-call(bf16[32,24,128]{2,1,0:T(8,128)(2,1)S(1)} %all_to_all.15.x_ref, ...), custom_call_target="tpu_custom_call" | custom-call | flops 100000000 | bytes 2000000 | tf_op jit(solution)/shard_map/pallas_call | solution.py:292
  16.6 12.5 %all_to_all.16.in_ref.half_ref = bf16[32,40,128]{2,1,0:T(8,128)(2,1)S(1)} all-to-all(bf16[32,40,128]{2,1,0:T(8,128)(2,1)S(1)} %get-tuple-element.15), channel_id=1, replica_groups={{21,23,17,19,29,31,25,27,5,7,1,3,13,15,9,11,20,22,16,18,28,30,24,26,4,6..., dimensions={0} | all-to-all | bytes 655360 | tf_op jit(solution)/shard_map/all_to_all | solution.py:27
  29.1 0.0 copy-done.1
  29.1 1.1 %shard_map.185 = bf16[32,24,128]{2,1,0:T(8,128)(2,1)} custom-call(bf16[32,40,128]{2,1,0:T(8,128)(2,1)S(1)} %all_to_all.16.in_ref.half_ref, f32[24,128]{1,0:T(8,128)S(1)} %get-tuple-element.16.sum_scale_ref, f32[24,128]{1,0:T(8,128)S(1)} %get-tuple-element.17.own_ref, f32[24,128]{1,0:T(8,128)S(1)} %get-tuple-element.18.floor_ref, bf16[128,4096]{1,0:T(8,128)(2,1)S(1)} %copy-done.1), custom_call_target="tpu_custom_call" | custom-call | flops 30000000 | bytes 2000000 | tf_op jit(solution)/shard_map/pallas_call | solution.py:314
  30.2 7.9 %all-to-all-start.2 = ((bf16[32,24,128]{2,1,0:T(8,128)(2,1)}), bf16[32,24,128]{2,1,0:T(8,128)(2,1)S(1)}, u32[]{:S(2)}, u32[]{:S(2)}) async-start(bf16[32,24,128]{2,1,0:T(8,128)(2,1)} %shard_map.185), calls=%async_computation.2 | async-start | bytes 393216 | tf_op jit(solution)/shard_map/all_to_all | solution.py:27
  38.1 0.5 %collective-permute-start = (bf16[32,16,128]{2,1,0:T(8,128)(2,1)S(1)}, bf16[32,16,128]{2,1,0:T(8,128)(2,1)S(1)}, u32[]{:S(2)}, u32[]{:S(2)}) collective-permute-start(bf16[32,16,128]{2,1,0:T(8,128)(2,1)S(1)} %slice.4), channel_id=1, source_target_pairs={{0,1},{1,0},{2,3},{3,2},{4,5},{5,4},{6,7},{7,6},{8,9},{9,8},{10,11... | collective-permute-start | bytes 393224 | tf_op jit(solution)/shard_map/swap/ppermute | solution.py:319
  38.6 1.2 %shard_map.187 = (bf16[24,8,8,512]{3,2,1,0:T(8,128)(2,1)}, f32[64,24]{1,0:T(8,128)}, f32[8,24]{1,0:T(8,128)}) custom-call(f32[64,24]{1,0:T(8,128)S(1)} %get-tuple-element.19.f_rows_ref, f32[64,24]{1,0:T(8,128)S(1)} %get-tuple-element.20.ik_rows_ref, f32[64,24]{1,0:T(8,128)S(1)} %get-tuple-element.21.norm_ref, f32[8,24]{1,0:T(8,128)S(1)} %get-tuple-element.22.stab_ref, ...), custom_call_target="tpu_custom_call" | custom-call | flops 50000000 | bytes 2000000 | tf_op jit(solution)/shard_map/pallas_call | solution.py:325
  39.8 0.0 collective-permute-done.half_ref
  39.8 0.0 copy-start.10
  39.9 1.2 %shard_map.188 = bf16[24,8,8,512]{3,2,1,0:T(8,128)(2,1)} custom-call(f32[64,24]{1,0:T(8,128)S(1)} %get-tuple-element.19.f_rows_ref, f32[64,24]{1,0:T(8,128)S(1)} %get-tuple-element.20.ik_rows_ref, bf16[32,16,128]{2,1,0:T(8,128)(2,1)S(1)} %collective-permute-done.half_ref, bf16[24,8,8,512]{3,2,1,0:T(8,128)(2,1)S(1)} %copy-done, ...), custom_call_target="tpu_custom_call", output_to_operand_aliasing={{}: (4, {})} | custom-call | flops 50000000 | bytes 2000000 | tf_op jit(solution)/shard_map/pallas_call | solution.py:333
  41.1 0.4 %all-to-all-done.2.in_ref = bf16[32,24,128]{2,1,0:T(8,128)(2,1)S(1)} async-done(((bf16[32,24,128]{2,1,0:T(8,128)(2,1)}), bf16[32,24,128]{2,1,0:T(8,128)(2,1)S(1)}, u32[]{:S(2)}, u32[]{:S(2)}) %all-to-all-start.2) | async-done | bytes 196640 | tf_op jit(solution)/shard_map/all_to_all | solution.py:27
  41.5 0.0 copy-done.10
  41.5 0.6 %shard_map.186 = f32[24,128]{1,0:T(8,128)} custom-call(bf16[32,24,128]{2,1,0:T(8,128)(2,1)S(1)} %all-to-all-done.2.in_ref, f32[24,128]{1,0:T(8,128)S(1)} %copy-done.10), custom_call_target="tpu_custom_call" | custom-call | flops 1000000 | bytes 2000000 | tf_op jit(solution)/shard_map/pallas_call | solution.py:342
  (2 shorter events, 0.0 us)
Async XLA Ops:
  1.3 13.6 %copy-start = (bf16[24,8,8,512]{3,2,1,0:T(8,128)(2,1)S(1)}, bf16[24,8,8,512]{3,2,1,0:T(8,128)(2,1)}, u32[]{:S(2)}) copy-start(bf16[24,8,8,512]{3,2,1,0:T(8,128)(2,1)} %mem_ref.3) | copy-start | bytes 4718596
  1.3 13.6 %copy-start.2 = (bf16[4096,128]{1,0:T(8,128)(2,1)S(1)}, bf16[4096,128]{1,0:T(8,128)(2,1)}, u32[]{:S(2)}) copy-start(bf16[4096,128]{1,0:T(8,128)(2,1)} %wv_ref.1) | copy-start | bytes 3145732
  1.3 13.6 %copy-start.3 = (bf16[4096,128]{1,0:T(8,128)(2,1)S(1)}, bf16[4096,128]{1,0:T(8,128)(2,1)}, u32[]{:S(2)}) copy-start(bf16[4096,128]{1,0:T(8,128)(2,1)} %wg_ref.1) | copy-start | bytes 3145732
  1.4 13.6 %copy-start.4 = (bf16[8,8,4096]{2,1,0:T(8,128)(2,1)S(1)}, bf16[8,8,4096]{2,1,0:T(8,128)(2,1)}, u32[]{:S(2)}) copy-start(bf16[8,8,4096]{2,1,0:T(8,128)(2,1)} %param.18) | copy-start | bytes 1572868
  1.4 13.6 %copy-start.5 = (bf16[8,8,4096]{2,1,0:T(8,128)(2,1)S(1)}, bf16[8,8,4096]{2,1,0:T(8,128)(2,1)}, u32[]{:S(2)}) copy-start(bf16[8,8,4096]{2,1,0:T(8,128)(2,1)} %param.19) | copy-start | bytes 1572868
  1.4 13.6 %copy-start.6 = (bf16[64,3072]{1,0:T(8,128)(2,1)S(1)}, bf16[64,3072]{1,0:T(8,128)(2,1)}, u32[]{:S(2)}) copy-start(bf16[64,3072]{1,0:T(8,128)(2,1)} %constant.4.clone.repeat_ref) | copy-start | bytes 1179652
  1.4 13.6 %copy-start.7 = (bf16[96,384]{1,0:T(8,128)(2,1)S(1)}, bf16[96,384]{1,0:T(8,128)(2,1)}, u32[]{:S(2)}) copy-start(bf16[96,384]{1,0:T(8,128)(2,1)} %constant.5.clone.own_ref) | copy-start | bytes 221188
  1.4 13.6 %copy-start.8 = (bf16[8,4096]{1,0:T(8,128)(2,1)S(1)}, bf16[8,4096]{1,0:T(8,128)(2,1)}, u32[]{:S(2)}) copy-start(bf16[8,4096]{1,0:T(8,128)(2,1)} %wi_ref.1) | copy-start | bytes 196612
  1.4 13.6 %copy-start.9 = (bf16[8,4096]{1,0:T(8,128)(2,1)S(1)}, bf16[8,4096]{1,0:T(8,128)(2,1)}, u32[]{:S(2)}) copy-start(bf16[8,4096]{1,0:T(8,128)(2,1)} %wf_ref.1) | copy-start | bytes 196612
  1.4 13.6 %copy-start.11 = (f32[24,8,8]{0,2,1:T(8,128)S(1)}, f32[24,8,8]{0,2,1:T(8,128)}, u32[]{:S(2)}) copy-start(f32[24,8,8]{0,2,1:T(8,128)} %param.28) | copy-start | bytes 18436
  1.4 13.6 %copy-start.12 = (f32[4096]{0:T(1024)S(1)}, f32[4096]{0:T(1024)}, u32[]{:S(2)}) copy-start(f32[4096]{0:T(1024)} %param.17) | copy-start | bytes 49156
  1.4 13.6 %copy-start.13 = (f32[24,8]{0,1:T(8,128)S(1)}, f32[24,8]{0,1:T(8,128)}, u32[]{:S(2)}) copy-start(f32[24,8]{0,1:T(8,128)} %param.29) | copy-start | bytes 2308
  1.5 13.6 %copy-start.14 = (f32[8]{0:T(128)S(1)}, f32[8]{0:T(128)}, u32[]{:S(2)}) copy-start(f32[8]{0:T(128)} %param.24) | copy-start | bytes 100
  1.5 13.6 %copy-start.15 = (f32[8]{0:T(128)S(1)}, f32[8]{0:T(128)}, u32[]{:S(2)}) copy-start(f32[8]{0:T(128)} %param.25) | copy-start | bytes 100
  15.1 14.0 %copy-start.1 = (bf16[128,4096]{1,0:T(8,128)(2,1)S(1)}, bf16[128,4096]{1,0:T(8,128)(2,1)}, u32[]{:S(2)}) copy-start(bf16[128,4096]{1,0:T(8,128)(2,1)} %wo_ref.1) | copy-start | bytes 3145732
  30.2 11.3 %all-to-all-start.2 = ((bf16[32,24,128]{2,1,0:T(8,128)(2,1)}), bf16[32,24,128]{2,1,0:T(8,128)(2,1)S(1)}, u32[]{:S(2)}, u32[]{:S(2)}) async-start(bf16[32,24,128]{2,1,0:T(8,128)(2,1)} %shard_map.185), calls=%async_computation.2 | async-start | bytes 393216 | tf_op jit(solution)/shard_map/all_to_all | solution.py:27
  38.1 1.8 %collective-permute-start = (bf16[32,16,128]{2,1,0:T(8,128)(2,1)S(1)}, bf16[32,16,128]{2,1,0:T(8,128)(2,1)S(1)}, u32[]{:S(2)}, u32[]{:S(2)}) collective-permute-start(bf16[32,16,128]{2,1,0:T(8,128)(2,1)S(1)} %slice.4), channel_id=1, source_target_pairs={{0,1},{1,0},{2,3},{3,2},{4,5},{5,4},{6,7},{7,6},{8,9},{9,8},{10,11... | collective-permute-start | bytes 393224 | tf_op jit(solution)/shard_map/swap/ppermute | solution.py:319
  39.8 1.7 %copy-start.10 = (f32[24,128]{1,0:T(8,128)S(1)}, f32[24,128]{1,0:T(8,128)}, u32[]{:S(2)}) copy-start(f32[24,128]{1,0:T(8,128)} %residual_ref.1) | copy-start | bytes 36868

commit v10 on v9

--- a/solution.py
+++ b/solution.py
@@ -60,7 +60,7 @@
 
 
 def spread_kernel(in_ref, out_ref):
-    value = in_ref[...]
+    value = in_ref[...].astype(BF16)
     for j in range(out_ref.shape[0]):
         out_ref[j] = value
 
@@ -86,6 +86,7 @@
         xn_ref[:, cut] = (x_ref[j].astype(F32) * scale * gain_ref[:, cut]).astype(BF16)
     x_norm = xn_ref[...]
 
+    value_gate = dot(x_norm, jnp.concatenate([wv_ref[...], wg_ref[...]], axis=1))
     left = jnp.concatenate([wq_ref[...], wk_ref[...], wi_ref[...], wf_ref[...]], axis=0)
     mixed = dot_last(left, x_norm)
     query_t = mixed[: H * rows]
@@ -136,7 +137,6 @@
             for k in range(2):
                 out_ref[SLOT[h * share + 2 * k + parity], :batch] = numer[:, k * width : (k + 1) * width]
 
-    value_gate = dot(x_norm, jnp.concatenate([wv_ref[...], wg_ref[...]], axis=1))
     value = value_gate[:, :width]
     for core in range(2):
         first = value[core * half : core * half + 8].astype(BF16)
@@ -265,9 +265,7 @@
     batch, width = residual.shape
     rows = w_query.shape[1]
     features = count * width
-    (pieces,) = call(spread_kernel, [((count, batch, width), BF16)], 1, flops=SPREAD_FLOPS)(
-        residual.astype(BF16)
-    )
+    (pieces,) = call(spread_kernel, [((count, batch, width), BF16)], 1, flops=SPREAD_FLOPS)(residual)
     gathered = exchange(pieces)
 
     piece = ((count, batch, width), BF16)

time: 42.5 us -> 42.4 us (level)
  local copies, waits for them, and re-layouts: 0.1 us -> 0.94 us
  other arithmetic: 0.71 us -> 0 us
    unnamed x32 -> x34, local copies, waits for them, and re-layouts: 0.09 us -> 0.93 us
    convert_element_type x1 -> x0, other arithmetic: 0.71 us -> none  [body(): residual.astype(BF16)]
where the time goes in v10:
time: 42.4 us; the launch traced here: 42.1 us
  blocking collectives  25.8 us (61%)
  starting transfers between devices  8.41 us (20%)
  Pallas kernels  5.6 us (13%)
  local copies, waits for them, and re-layouts  0.94 us (2%)
  between operations  0.89 us (2%)
  waiting for transfers between devices  0.45 us (1%)
    all_to_all x2, blocking collectives, exchange(): lax.all_to_all(pieces, 'head', 0, 0, tiled=True, axis_index_groups=[ORDER])  25.8 us
    all_to_all x1, starting transfers between devices, exchange(): lax.all_to_all(pieces, 'head', 0, 0, tiled=True, axis_index_groups=[ORDER])  7.88 us
    pallas_call x1, Pallas kernels, body(): call(project_kernel, [((count, batch + batch // 2 + 4, width), BF16), ((H...  1.47 us
    pallas_call x1, Pallas kernels, body(): call(memory_mine_kernel, [(memory.shape, BF16), ((H * rows, batch), F32),...  1.22 us
    pallas_call x1, Pallas kernels, body(): call(memory_other_kernel, [(memory.shape, BF16)], 4, scratch=half_scratch...  1.2 us
    pallas_call x1, Pallas kernels, body(): call(output_kernel, [piece], 5, flops=30000000)  1.05 us
    unnamed x34, local copies, waits for them, and re-layouts  0.93 us
  transfers between devices with their start and end apart: 2, of which 1 were waited for; matrix products, arithmetic and copies ran while one was open for 0% of the time, Pallas kernels for 6%

profile of v10, /device:TPU:1, one launch (start us, length us, event | category | flops | bytes accessed | tf_op | source)
XLA Modules:
  0.0 42.1 jit_solution(13213106670639398859)
XLA Ops:
  0.6 0.0 copy-start.6
  0.6 0.0 copy-start.7
  0.7 0.0 copy-start
  0.7 0.0 copy-start.10
  0.7 0.0 copy-start.9
  0.7 0.0 copy-start.8
  0.7 0.0 copy-start.3
  0.7 0.0 copy-start.2
  0.7 0.0 copy-start.5
  0.7 0.0 copy-start.4
  0.7 0.0 copy-start.11
  0.8 0.0 copy-start.12
  0.8 0.8 %copy-done.12 = f32[24,128]{1,0:T(8,128)S(1)} copy-done((f32[24,128]{1,0:T(8,128)S(1)}, f32[24,128]{1,0:T(8,128)}, u32[]{:S(2)}) %copy-start.12) | copy-done | bytes 12312
  1.6 0.0 copy-start.14
  1.6 0.0 copy-start.15
  1.6 0.0 copy-start.16
  1.6 13.3 %all_to_all.15.x_ref = bf16[32,24,128]{2,1,0:T(8,128)(2,1)S(1)} all-to-all(bf16[32,24,128]{2,1,0:T(8,128)(2,1)S(1)} %shard_map.183), channel_id=1, replica_groups={{21,23,17,19,29,31,25,27,5,7,1,3,13,15,9,11,20,22,16,18,28,30,24,26,4,6..., dimensions={0} | all-to-all | bytes 393216 | tf_op jit(solution)/shard_map/all_to_all | solution.py:27
  14.9 0.0 copy-done.6
  14.9 0.0 copy-done.7
  14.9 0.0 copy-done
  14.9 0.0 copy-done.10
  14.9 0.0 copy-done.9
  15.0 0.0 copy-done.8
  15.0 0.0 copy-done.3
  15.0 0.0 copy-done.2
  15.0 0.0 copy-done.5
  15.0 0.0 copy-done.4
  15.0 0.0 copy-done.11
  15.0 0.0 copy-done.14
  15.0 0.0 copy-done.15
  15.0 0.0 copy-done.16
  15.0 0.0 copy-start.1
  15.1 1.5 %shard_map.184 = (bf16[32,40,128]{2,1,0:T(8,128)(2,1)S(1)}, f32[64,24]{1,0:T(8,128)S(1)}, f32[8,24]{1,0:T(8,128)S(1)}, f32[64,24]{1,0:T(8,128)S(1)}, f32[64,24]{...) custom-call(bf16[32,24,128]{2,1,0:T(8,128)(2,1)S(1)} %all_to_all.15.x_ref, ...), custom_call_target="tpu_custom_call" | custom-call | flops 100000000 | bytes 2000000 | tf_op jit(solution)/shard_map/pallas_call | solution.py:290
  16.5 12.5 %all_to_all.16.in_ref.half_ref = bf16[32,40,128]{2,1,0:T(8,128)(2,1)S(1)} all-to-all(bf16[32,40,128]{2,1,0:T(8,128)(2,1)S(1)} %get-tuple-element.15), channel_id=1, replica_groups={{21,23,17,19,29,31,25,27,5,7,1,3,13,15,9,11,20,22,16,18,28,30,24,26,4,6..., dimensions={0} | all-to-all | bytes 655360 | tf_op jit(solution)/shard_map/all_to_all | solution.py:27
  29.1 0.0 copy-done.1
  29.1 1.0 %shard_map.185 = bf16[32,24,128]{2,1,0:T(8,128)(2,1)} custom-call(bf16[32,40,128]{2,1,0:T(8,128)(2,1)S(1)} %all_to_all.16.in_ref.half_ref, f32[24,128]{1,0:T(8,128)S(1)} %get-tuple-element.16.sum_scale_ref, f32[24,128]{1,0:T(8,128)S(1)} %get-tuple-element.17.own_ref, f32[24,128]{1,0:T(8,128)S(1)} %get-tuple-element.18.floor_ref, bf16[128,4096]{1,0:T(8,128)(2,1)S(1)} %copy-done.1), custom_call_target="tpu_custom_call" | custom-call | flops 30000000 | bytes 2000000 | tf_op jit(solution)/shard_map/pallas_call | solution.py:312
  30.1 7.9 %all-to-all-start.2 = ((bf16[32,24,128]{2,1,0:T(8,128)(2,1)}), bf16[32,24,128]{2,1,0:T(8,128)(2,1)S(1)}, u32[]{:S(2)}, u32[]{:S(2)}) async-start(bf16[32,24,128]{2,1,0:T(8,128)(2,1)} %shard_map.185), calls=%async_computation.2 | async-start | bytes 393216 | tf_op jit(solution)/shard_map/all_to_all | solution.py:27
  38.0 0.5 %collective-permute-start = (bf16[32,16,128]{2,1,0:T(8,128)(2,1)S(1)}, bf16[32,16,128]{2,1,0:T(8,128)(2,1)S(1)}, u32[]{:S(2)}, u32[]{:S(2)}) collective-permute-start(bf16[32,16,128]{2,1,0:T(8,128)(2,1)S(1)} %slice.4), channel_id=1, source_target_pairs={{0,1},{1,0},{2,3},{3,2},{4,5},{5,4},{6,7},{7,6},{8,9},{9,8},{10,11... | collective-permute-start | bytes 393224 | tf_op jit(solution)/shard_map/swap/ppermute | solution.py:317
  38.6 1.2 %shard_map.187 = (bf16[24,8,8,512]{3,2,1,0:T(8,128)(2,1)}, f32[64,24]{1,0:T(8,128)}, f32[8,24]{1,0:T(8,128)}) custom-call(f32[64,24]{1,0:T(8,128)S(1)} %get-tuple-element.19.f_rows_ref, f32[64,24]{1,0:T(8,128)S(1)} %get-tuple-element.20.ik_rows_ref, f32[64,24]{1,0:T(8,128)S(1)} %get-tuple-element.21.norm_ref, f32[8,24]{1,0:T(8,128)S(1)} %get-tuple-element.22.stab_ref, ...), custom_call_target="tpu_custom_call" | custom-call | flops 50000000 | bytes 2000000 | tf_op jit(solution)/shard_map/pallas_call | solution.py:323
  39.8 0.0 collective-permute-done.half_ref
  39.8 0.0 copy-start.13
  39.8 1.2 %shard_map.188 = bf16[24,8,8,512]{3,2,1,0:T(8,128)(2,1)} custom-call(f32[64,24]{1,0:T(8,128)S(1)} %get-tuple-element.19.f_rows_ref, f32[64,24]{1,0:T(8,128)S(1)} %get-tuple-element.20.ik_rows_ref, bf16[32,16,128]{2,1,0:T(8,128)(2,1)S(1)} %collective-permute-done.half_ref, bf16[24,8,8,512]{3,2,1,0:T(8,128)(2,1)S(1)} %copy-done, ...), custom_call_target="tpu_custom_call", output_to_operand_aliasing={{}: (4, {})} | custom-call | flops 50000000 | bytes 2000000 | tf_op jit(solution)/shard_map/pallas_call | solution.py:331
  41.0 0.4 %all-to-all-done.2.in_ref = bf16[32,24,128]{2,1,0:T(8,128)(2,1)S(1)} async-done(((bf16[32,24,128]{2,1,0:T(8,128)(2,1)}), bf16[32,24,128]{2,1,0:T(8,128)(2,1)S(1)}, u32[]{:S(2)}, u32[]{:S(2)}) %all-to-all-start.2) | async-done | bytes 196640 | tf_op jit(solution)/shard_map/all_to_all | solution.py:27
  41.5 0.0 copy-done.13
  41.5 0.6 %shard_map.186 = f32[24,128]{1,0:T(8,128)} custom-call(bf16[32,24,128]{2,1,0:T(8,128)(2,1)S(1)} %all-to-all-done.2.in_ref, f32[24,128]{1,0:T(8,128)S(1)} %copy-done.13), custom_call_target="tpu_custom_call" | custom-call | flops 1000000 | bytes 2000000 | tf_op jit(solution)/shard_map/pallas_call | solution.py:340
  (2 shorter events, 0.0 us)
Async XLA Ops:
  0.6 14.3 %copy-start.6 = (bf16[64,3072]{1,0:T(8,128)(2,1)S(1)}, bf16[64,3072]{1,0:T(8,128)(2,1)}, u32[]{:S(2)}) copy-start(bf16[64,3072]{1,0:T(8,128)(2,1)} %constant.4.clone.repeat_ref) | copy-start | bytes 1179652
  0.6 14.3 %copy-start.7 = (bf16[96,384]{1,0:T(8,128)(2,1)S(1)}, bf16[96,384]{1,0:T(8,128)(2,1)}, u32[]{:S(2)}) copy-start(bf16[96,384]{1,0:T(8,128)(2,1)} %constant.5.clone.own_ref) | copy-start | bytes 221188
  0.7 14.3 %copy-start = (bf16[24,8,8,512]{3,2,1,0:T(8,128)(2,1)S(1)}, bf16[24,8,8,512]{3,2,1,0:T(8,128)(2,1)}, u32[]{:S(2)}) copy-start(bf16[24,8,8,512]{3,2,1,0:T(8,128)(2,1)} %mem_ref.3) | copy-start | bytes 4718596
  0.7 14.3 %copy-start.10 = (f32[24,8,8]{0,2,1:T(8,128)S(1)}, f32[24,8,8]{0,2,1:T(8,128)}, u32[]{:S(2)}) copy-start(f32[24,8,8]{0,2,1:T(8,128)} %param.28) | copy-start | bytes 18436
  0.7 14.3 %copy-start.9 = (bf16[8,4096]{1,0:T(8,128)(2,1)S(1)}, bf16[8,4096]{1,0:T(8,128)(2,1)}, u32[]{:S(2)}) copy-start(bf16[8,4096]{1,0:T(8,128)(2,1)} %wf_ref.1) | copy-start | bytes 196612
  0.7 14.3 %copy-start.8 = (bf16[8,4096]{1,0:T(8,128)(2,1)S(1)}, bf16[8,4096]{1,0:T(8,128)(2,1)}, u32[]{:S(2)}) copy-start(bf16[8,4096]{1,0:T(8,128)(2,1)} %wi_ref.1) | copy-start | bytes 196612
  0.7 14.3 %copy-start.3 = (bf16[4096,128]{1,0:T(8,128)(2,1)S(1)}, bf16[4096,128]{1,0:T(8,128)(2,1)}, u32[]{:S(2)}) copy-start(bf16[4096,128]{1,0:T(8,128)(2,1)} %wg_ref.1) | copy-start | bytes 3145732
  0.7 14.3 %copy-start.2 = (bf16[4096,128]{1,0:T(8,128)(2,1)S(1)}, bf16[4096,128]{1,0:T(8,128)(2,1)}, u32[]{:S(2)}) copy-start(bf16[4096,128]{1,0:T(8,128)(2,1)} %wv_ref.1) | copy-start | bytes 3145732
  0.7 14.3 %copy-start.5 = (bf16[8,8,4096]{2,1,0:T(8,128)(2,1)S(1)}, bf16[8,8,4096]{2,1,0:T(8,128)(2,1)}, u32[]{:S(2)}) copy-start(bf16[8,8,4096]{2,1,0:T(8,128)(2,1)} %param.19) | copy-start | bytes 1572868
  0.7 14.3 %copy-start.4 = (bf16[8,8,4096]{2,1,0:T(8,128)(2,1)S(1)}, bf16[8,8,4096]{2,1,0:T(8,128)(2,1)}, u32[]{:S(2)}) copy-start(bf16[8,8,4096]{2,1,0:T(8,128)(2,1)} %param.18) | copy-start | bytes 1572868
  0.7 14.3 %copy-start.11 = (f32[4096]{0:T(1024)S(1)}, f32[4096]{0:T(1024)}, u32[]{:S(2)}) copy-start(f32[4096]{0:T(1024)} %param.17) | copy-start | bytes 49156
  0.8 0.9 %copy-start.12 = (f32[24,128]{1,0:T(8,128)S(1)}, f32[24,128]{1,0:T(8,128)}, u32[]{:S(2)}) copy-start(f32[24,128]{1,0:T(8,128)} %residual_ref.1) | copy-start | bytes 36868
  1.6 13.4 %copy-start.14 = (f32[24,8]{0,1:T(8,128)S(1)}, f32[24,8]{0,1:T(8,128)}, u32[]{:S(2)}) copy-start(f32[24,8]{0,1:T(8,128)} %param.29) | copy-start | bytes 2308
  1.6 13.4 %copy-start.15 = (f32[8]{0:T(128)S(1)}, f32[8]{0:T(128)}, u32[]{:S(2)}) copy-start(f32[8]{0:T(128)} %param.24) | copy-start | bytes 100
  1.6 13.4 %copy-start.16 = (f32[8]{0:T(128)S(1)}, f32[8]{0:T(128)}, u32[]{:S(2)}) copy-start(f32[8]{0:T(128)} %param.25) | copy-start | bytes 100
  15.0 14.0 %copy-start.1 = (bf16[128,4096]{1,0:T(8,128)(2,1)S(1)}, bf16[128,4096]{1,0:T(8,128)(2,1)}, u32[]{:S(2)}) copy-start(bf16[128,4096]{1,0:T(8,128)(2,1)} %wo_ref.1) | copy-start | bytes 3145732
  30.1 11.3 %all-to-all-start.2 = ((bf16[32,24,128]{2,1,0:T(8,128)(2,1)}), bf16[32,24,128]{2,1,0:T(8,128)(2,1)S(1)}, u32[]{:S(2)}, u32[]{:S(2)}) async-start(bf16[32,24,128]{2,1,0:T(8,128)(2,1)} %shard_map.185), calls=%async_computation.2 | async-start | bytes 393216 | tf_op jit(solution)/shard_map/all_to_all | solution.py:27
  38.0 1.8 %collective-permute-start = (bf16[32,16,128]{2,1,0:T(8,128)(2,1)S(1)}, bf16[32,16,128]{2,1,0:T(8,128)(2,1)S(1)}, u32[]{:S(2)}, u32[]{:S(2)}) collective-permute-start(bf16[32,16,128]{2,1,0:T(8,128)(2,1)S(1)} %slice.4), channel_id=1, source_target_pairs={{0,1},{1,0},{2,3},{3,2},{4,5},{5,4},{6,7},{7,6},{8,9},{9,8},{10,11... | collective-permute-start | bytes 393224 | tf_op jit(solution)/shard_map/swap/ppermute | solution.py:317
  39.8 1.7 %copy-start.13 = (f32[24,128]{1,0:T(8,128)S(1)}, f32[24,128]{1,0:T(8,128)}, u32[]{:S(2)}) copy-start(f32[24,128]{1,0:T(8,128)} %residual_ref.1) | copy-start | bytes 36868

commit v11 on v9

--- a/solution.py
+++ b/solution.py
@@ -86,6 +86,7 @@
         xn_ref[:, cut] = (x_ref[j].astype(F32) * scale * gain_ref[:, cut]).astype(BF16)
     x_norm = xn_ref[...]
 
+    value_gate = dot(x_norm, jnp.concatenate([wv_ref[...], wg_ref[...]], axis=1))
     left = jnp.concatenate([wq_ref[...], wk_ref[...], wi_ref[...], wf_ref[...]], axis=0)
     mixed = dot_last(left, x_norm)
     query_t = mixed[: H * rows]
@@ -136,7 +137,6 @@
             for k in range(2):
                 out_ref[SLOT[h * share + 2 * k + parity], :batch] = numer[:, k * width : (k + 1) * width]
 
-    value_gate = dot(x_norm, jnp.concatenate([wv_ref[...], wg_ref[...]], axis=1))
     value = value_gate[:, :width]
     for core in range(2):
         first = value[core * half : core * half + 8].astype(BF16)

time: 42.5 us -> 42.5 us (level)
  no operation moved by 1% of the time
where the time goes in v11:
time: 42.5 us; the launch traced here: 42.1 us
  blocking collectives  26 us (61%)
  starting transfers between devices  8.42 us (20%)
  Pallas kernels  5.6 us (13%)
  between operations  0.89 us (2%)
  other arithmetic  0.71 us (2%)
  waiting for transfers between devices  0.45 us (1%)
    all_to_all x2, blocking collectives, exchange(): lax.all_to_all(pieces, 'head', 0, 0, tiled=True, axis_index_groups=[ORDER])  26 us
    all_to_all x1, starting transfers between devices, exchange(): lax.all_to_all(pieces, 'head', 0, 0, tiled=True, axis_index_groups=[ORDER])  7.89 us
    pallas_call x1, Pallas kernels, body(): call(project_kernel, [((count, batch + batch // 2 + 4, width), BF16), ((H...  1.46 us
    pallas_call x1, Pallas kernels, body(): call(memory_mine_kernel, [(memory.shape, BF16), ((H * rows, batch), F32),...  1.22 us
    pallas_call x1, Pallas kernels, body(): call(memory_other_kernel, [(memory.shape, BF16)], 4, scratch=half_scratch...  1.2 us
    pallas_call x1, Pallas kernels, body(): call(output_kernel, [piece], 5, flops=30000000)  1.05 us
  transfers between devices with their start and end apart: 2, of which 1 were waited for; matrix products, arithmetic and copies ran while one was open for 0% of the time, Pallas kernels for 6%

profile of v11, /device:TPU:1, one launch (start us, length us, event | category | flops | bytes accessed | tf_op | source)
XLA Modules:
  0.0 42.1 jit_solution(12865081172614202505)
XLA Ops:
  0.6 0.7 %convert_element_type.3.in_ref = bf16[24,128]{1,0:T(8,128)(2,1)S(1)} convert(f32[24,128]{1,0:T(8,128)} %residual_ref.1) | non-fusion elementwise | flops 3072 | bytes 18432 | tf_op jit(solution)/shard_map/convert_element_type | solution.py:269
  1.3 0.0 copy-start
  1.3 0.0 copy-start.2
  1.3 0.0 copy-start.3
  1.4 0.0 copy-start.4
  1.4 0.0 copy-start.5
  1.4 0.0 copy-start.6
  1.4 0.0 copy-start.7
  1.4 0.0 copy-start.8
  1.4 0.0 copy-start.9
  1.4 0.0 copy-start.11
  1.4 0.0 copy-start.12
  1.4 0.0 copy-start.13
  1.5 0.0 copy-start.14
  1.5 0.0 copy-start.15
  1.5 13.4 %all_to_all.15.x_ref = bf16[32,24,128]{2,1,0:T(8,128)(2,1)S(1)} all-to-all(bf16[32,24,128]{2,1,0:T(8,128)(2,1)S(1)} %shard_map.183), channel_id=1, replica_groups={{21,23,17,19,29,31,25,27,5,7,1,3,13,15,9,11,20,22,16,18,28,30,24,26,4,6..., dimensions={0} | all-to-all | bytes 393216 | tf_op jit(solution)/shard_map/all_to_all | solution.py:27
  14.9 0.0 copy-done
  14.9 0.0 copy-done.2
  14.9 0.0 copy-done.3
  15.0 0.0 copy-done.4
  15.0 0.0 copy-done.5
  15.0 0.0 copy-done.6
  15.0 0.0 copy-done.7
  15.0 0.0 copy-done.8
  15.0 0.0 copy-done.9
  15.0 0.0 copy-done.11
  15.0 0.0 copy-done.12
  15.0 0.0 copy-done.13
  15.0 0.0 copy-done.14
  15.1 0.0 copy-done.15
  15.1 0.0 copy-start.1
  15.1 1.5 %shard_map.184 = (bf16[32,40,128]{2,1,0:T(8,128)(2,1)S(1)}, f32[64,24]{1,0:T(8,128)S(1)}, f32[8,24]{1,0:T(8,128)S(1)}, f32[64,24]{1,0:T(8,128)S(1)}, f32[64,24]{...) custom-call(bf16[32,24,128]{2,1,0:T(8,128)(2,1)S(1)} %all_to_all.15.x_ref, ...), custom_call_target="tpu_custom_call" | custom-call | flops 100000000 | bytes 2000000 | tf_op jit(solution)/shard_map/pallas_call | solution.py:292
  16.5 12.5 %all_to_all.16.in_ref.half_ref = bf16[32,40,128]{2,1,0:T(8,128)(2,1)S(1)} all-to-all(bf16[32,40,128]{2,1,0:T(8,128)(2,1)S(1)} %get-tuple-element.15), channel_id=1, replica_groups={{21,23,17,19,29,31,25,27,5,7,1,3,13,15,9,11,20,22,16,18,28,30,24,26,4,6..., dimensions={0} | all-to-all | bytes 655360 | tf_op jit(solution)/shard_map/all_to_all | solution.py:27
  29.1 0.0 copy-done.1
  29.1 1.0 %shard_map.185 = bf16[32,24,128]{2,1,0:T(8,128)(2,1)} custom-call(bf16[32,40,128]{2,1,0:T(8,128)(2,1)S(1)} %all_to_all.16.in_ref.half_ref, f32[24,128]{1,0:T(8,128)S(1)} %get-tuple-element.16.sum_scale_ref, f32[24,128]{1,0:T(8,128)S(1)} %get-tuple-element.17.own_ref, f32[24,128]{1,0:T(8,128)S(1)} %get-tuple-element.18.floor_ref, bf16[128,4096]{1,0:T(8,128)(2,1)S(1)} %copy-done.1), custom_call_target="tpu_custom_call" | custom-call | flops 30000000 | bytes 2000000 | tf_op jit(solution)/shard_map/pallas_call | solution.py:314
  30.1 7.9 %all-to-all-start.2 = ((bf16[32,24,128]{2,1,0:T(8,128)(2,1)}), bf16[32,24,128]{2,1,0:T(8,128)(2,1)S(1)}, u32[]{:S(2)}, u32[]{:S(2)}) async-start(bf16[32,24,128]{2,1,0:T(8,128)(2,1)} %shard_map.185), calls=%async_computation.2 | async-start | bytes 393216 | tf_op jit(solution)/shard_map/all_to_all | solution.py:27
  38.0 0.5 %collective-permute-start = (bf16[32,16,128]{2,1,0:T(8,128)(2,1)S(1)}, bf16[32,16,128]{2,1,0:T(8,128)(2,1)S(1)}, u32[]{:S(2)}, u32[]{:S(2)}) collective-permute-start(bf16[32,16,128]{2,1,0:T(8,128)(2,1)S(1)} %slice.4), channel_id=1, source_target_pairs={{0,1},{1,0},{2,3},{3,2},{4,5},{5,4},{6,7},{7,6},{8,9},{9,8},{10,11... | collective-permute-start | bytes 393224 | tf_op jit(solution)/shard_map/swap/ppermute | solution.py:319
  38.6 1.2 %shard_map.187 = (bf16[24,8,8,512]{3,2,1,0:T(8,128)(2,1)}, f32[64,24]{1,0:T(8,128)}, f32[8,24]{1,0:T(8,128)}) custom-call(f32[64,24]{1,0:T(8,128)S(1)} %get-tuple-element.19.f_rows_ref, f32[64,24]{1,0:T(8,128)S(1)} %get-tuple-element.20.ik_rows_ref, f32[64,24]{1,0:T(8,128)S(1)} %get-tuple-element.21.norm_ref, f32[8,24]{1,0:T(8,128)S(1)} %get-tuple-element.22.stab_ref, ...), custom_call_target="tpu_custom_call" | custom-call | flops 50000000 | bytes 2000000 | tf_op jit(solution)/shard_map/pallas_call | solution.py:325
  39.8 0.0 collective-permute-done.half_ref
  39.8 0.0 copy-start.10
  39.8 1.2 %shard_map.188 = bf16[24,8,8,512]{3,2,1,0:T(8,128)(2,1)} custom-call(f32[64,24]{1,0:T(8,128)S(1)} %get-tuple-element.19.f_rows_ref, f32[64,24]{1,0:T(8,128)S(1)} %get-tuple-element.20.ik_rows_ref, bf16[32,16,128]{2,1,0:T(8,128)(2,1)S(1)} %collective-permute-done.half_ref, bf16[24,8,8,512]{3,2,1,0:T(8,128)(2,1)S(1)} %copy-done, ...), custom_call_target="tpu_custom_call", output_to_operand_aliasing={{}: (4, {})} | custom-call | flops 50000000 | bytes 2000000 | tf_op jit(solution)/shard_map/pallas_call | solution.py:333
  41.0 0.4 %all-to-all-done.2.in_ref = bf16[32,24,128]{2,1,0:T(8,128)(2,1)S(1)} async-done(((bf16[32,24,128]{2,1,0:T(8,128)(2,1)}), bf16[32,24,128]{2,1,0:T(8,128)(2,1)S(1)}, u32[]{:S(2)}, u32[]{:S(2)}) %all-to-all-start.2) | async-done | bytes 196640 | tf_op jit(solution)/shard_map/all_to_all | solution.py:27
  41.5 0.0 copy-done.10
  41.5 0.6 %shard_map.186 = f32[24,128]{1,0:T(8,128)} custom-call(bf16[32,24,128]{2,1,0:T(8,128)(2,1)S(1)} %all-to-all-done.2.in_ref, f32[24,128]{1,0:T(8,128)S(1)} %copy-done.10), custom_call_target="tpu_custom_call" | custom-call | flops 1000000 | bytes 2000000 | tf_op jit(solution)/shard_map/pallas_call | solution.py:342
  (2 shorter events, 0.0 us)
Async XLA Ops:
  1.3 13.6 %copy-start = (bf16[24,8,8,512]{3,2,1,0:T(8,128)(2,1)S(1)}, bf16[24,8,8,512]{3,2,1,0:T(8,128)(2,1)}, u32[]{:S(2)}) copy-start(bf16[24,8,8,512]{3,2,1,0:T(8,128)(2,1)} %mem_ref.3) | copy-start | bytes 4718596
  1.3 13.6 %copy-start.2 = (bf16[4096,128]{1,0:T(8,128)(2,1)S(1)}, bf16[4096,128]{1,0:T(8,128)(2,1)}, u32[]{:S(2)}) copy-start(bf16[4096,128]{1,0:T(8,128)(2,1)} %wv_ref.1) | copy-start | bytes 3145732
  1.3 13.6 %copy-start.3 = (bf16[4096,128]{1,0:T(8,128)(2,1)S(1)}, bf16[4096,128]{1,0:T(8,128)(2,1)}, u32[]{:S(2)}) copy-start(bf16[4096,128]{1,0:T(8,128)(2,1)} %wg_ref.1) | copy-start | bytes 3145732
  1.4 13.6 %copy-start.4 = (bf16[8,8,4096]{2,1,0:T(8,128)(2,1)S(1)}, bf16[8,8,4096]{2,1,0:T(8,128)(2,1)}, u32[]{:S(2)}) copy-start(bf16[8,8,4096]{2,1,0:T(8,128)(2,1)} %param.18) | copy-start | bytes 1572868
  1.4 13.6 %copy-start.5 = (bf16[8,8,4096]{2,1,0:T(8,128)(2,1)S(1)}, bf16[8,8,4096]{2,1,0:T(8,128)(2,1)}, u32[]{:S(2)}) copy-start(bf16[8,8,4096]{2,1,0:T(8,128)(2,1)} %param.19) | copy-start | bytes 1572868
  1.4 13.6 %copy-start.6 = (bf16[64,3072]{1,0:T(8,128)(2,1)S(1)}, bf16[64,3072]{1,0:T(8,128)(2,1)}, u32[]{:S(2)}) copy-start(bf16[64,3072]{1,0:T(8,128)(2,1)} %constant.4.clone.repeat_ref) | copy-start | bytes 1179652
  1.4 13.6 %copy-start.7 = (bf16[96,384]{1,0:T(8,128)(2,1)S(1)}, bf16[96,384]{1,0:T(8,128)(2,1)}, u32[]{:S(2)}) copy-start(bf16[96,384]{1,0:T(8,128)(2,1)} %constant.5.clone.own_ref) | copy-start | bytes 221188
  1.4 13.6 %copy-start.8 = (bf16[8,4096]{1,0:T(8,128)(2,1)S(1)}, bf16[8,4096]{1,0:T(8,128)(2,1)}, u32[]{:S(2)}) copy-start(bf16[8,4096]{1,0:T(8,128)(2,1)} %wi_ref.1) | copy-start | bytes 196612
  1.4 13.6 %copy-start.9 = (bf16[8,4096]{1,0:T(8,128)(2,1)S(1)}, bf16[8,4096]{1,0:T(8,128)(2,1)}, u32[]{:S(2)}) copy-start(bf16[8,4096]{1,0:T(8,128)(2,1)} %wf_ref.1) | copy-start | bytes 196612
  1.4 13.6 %copy-start.11 = (f32[24,8,8]{0,2,1:T(8,128)S(1)}, f32[24,8,8]{0,2,1:T(8,128)}, u32[]{:S(2)}) copy-start(f32[24,8,8]{0,2,1:T(8,128)} %param.28) | copy-start | bytes 18436
  1.4 13.6 %copy-start.12 = (f32[4096]{0:T(1024)S(1)}, f32[4096]{0:T(1024)}, u32[]{:S(2)}) copy-start(f32[4096]{0:T(1024)} %param.17) | copy-start | bytes 49156
  1.4 13.6 %copy-start.13 = (f32[24,8]{0,1:T(8,128)S(1)}, f32[24,8]{0,1:T(8,128)}, u32[]{:S(2)}) copy-start(f32[24,8]{0,1:T(8,128)} %param.29) | copy-start | bytes 2308
  1.5 13.6 %copy-start.14 = (f32[8]{0:T(128)S(1)}, f32[8]{0:T(128)}, u32[]{:S(2)}) copy-start(f32[8]{0:T(128)} %param.24) | copy-start | bytes 100
  1.5 13.6 %copy-start.15 = (f32[8]{0:T(128)S(1)}, f32[8]{0:T(128)}, u32[]{:S(2)}) copy-start(f32[8]{0:T(128)} %param.25) | copy-start | bytes 100
  15.1 14.0 %copy-start.1 = (bf16[128,4096]{1,0:T(8,128)(2,1)S(1)}, bf16[128,4096]{1,0:T(8,128)(2,1)}, u32[]{:S(2)}) copy-start(bf16[128,4096]{1,0:T(8,128)(2,1)} %wo_ref.1) | copy-start | bytes 3145732
  30.1 11.4 %all-to-all-start.2 = ((bf16[32,24,128]{2,1,0:T(8,128)(2,1)}), bf16[32,24,128]{2,1,0:T(8,128)(2,1)S(1)}, u32[]{:S(2)}, u32[]{:S(2)}) async-start(bf16[32,24,128]{2,1,0:T(8,128)(2,1)} %shard_map.185), calls=%async_computation.2 | async-start | bytes 393216 | tf_op jit(solution)/shard_map/all_to_all | solution.py:27
  38.0 1.8 %collective-permute-start = (bf16[32,16,128]{2,1,0:T(8,128)(2,1)S(1)}, bf16[32,16,128]{2,1,0:T(8,128)(2,1)S(1)}, u32[]{:S(2)}, u32[]{:S(2)}) collective-permute-start(bf16[32,16,128]{2,1,0:T(8,128)(2,1)S(1)} %slice.4), channel_id=1, source_target_pairs={{0,1},{1,0},{2,3},{3,2},{4,5},{5,4},{6,7},{7,6},{8,9},{9,8},{10,11... | collective-permute-start | bytes 393224 | tf_op jit(solution)/shard_map/swap/ppermute | solution.py:319
  39.8 1.7 %copy-start.10 = (f32[24,128]{1,0:T(8,128)S(1)}, f32[24,128]{1,0:T(8,128)}, u32[]{:S(2)}) copy-start(f32[24,128]{1,0:T(8,128)} %residual_ref.1) | copy-start | bytes 36868

commit v12 on v10

--- a/solution.py
+++ b/solution.py
@@ -116,8 +116,7 @@
         key_query = jnp.sum(key_h * query_h, axis=0, keepdims=True)
         kinds = (*split_hi_lo(norm_query), *split_hi_lo(key_query))
         for k, kind in enumerate(kinds):
-            for core in range(2):
-                tail_ref[core, h, 4 + k : 5 + k, :batch] = kind
+            tail_ref[h, 4 + k : 5 + k, :batch] = kind
 
     spread = batch * rows
     high, low = split_hi_lo(query_t.T)
@@ -138,14 +137,15 @@
                 out_ref[SLOT[h * share + 2 * k + parity], :batch] = numer[:, k * width : (k + 1) * width]
 
     value = value_gate[:, :width]
+    top = lax.broadcasted_iota(jnp.int32, (8, width), 0) < 4
     for core in range(2):
         first = value[core * half : core * half + 8].astype(BF16)
         rest = value[core * half + 8 : (core + 1) * half]
-        for h in range(H):
-            tail_ref[core, h, :4] = rest
+        rest = jnp.concatenate([rest, rest], axis=0)
+        tails = [jnp.where(top, rest, tail_ref[h]).astype(BF16) for h in range(H)]
         for j in range(core, pieces, 2):
             out_ref[SLOT[j], batch : batch + 8] = first
-            out_ref[SLOT[j], batch + 8 :] = tail_ref[core, j // share].astype(BF16)
+            out_ref[SLOT[j], batch + 8 :] = tails[j // share]
 
     head = lax.axis_index("head") * width // DV
     pick = lambda ref: column(ref[pl.ds(head, 1), :])
@@ -302,7 +302,7 @@
         1 + len(sources),
         scratch=[
             pltpu.VMEM((batch, features), BF16),
-            pltpu.VMEM((2, H, 8, width), F32),
+            pltpu.VMEM((H, 8, width), F32),
             pltpu.VMEM((H, batch), F32),
             pltpu.VMEM((H, batch), F32),
         ],

time: 42.4 us -> 42.4 us (level)
  no operation moved by 1% of the time
where the time goes in v12:
time: 42.4 us; the launch traced here: 42.1 us
  blocking collectives  25.8 us (61%)
  starting transfers between devices  8.42 us (20%)
  Pallas kernels  5.56 us (13%)
  local copies, waits for them, and re-layouts  0.94 us (2%)
  between operations  0.89 us (2%)
  waiting for transfers between devices  0.45 us (1%)
    all_to_all x2, blocking collectives, exchange(): lax.all_to_all(pieces, 'head', 0, 0, tiled=True, axis_index_groups=[ORDER])  25.8 us
    all_to_all x1, starting transfers between devices, exchange(): lax.all_to_all(pieces, 'head', 0, 0, tiled=True, axis_index_groups=[ORDER])  7.88 us
    pallas_call x1, Pallas kernels, body(): call(project_kernel, [((count, batch + batch // 2 + 4, width), BF16), ((H...  1.44 us
    pallas_call x1, Pallas kernels, body(): call(memory_mine_kernel, [(memory.shape, BF16), ((H * rows, batch), F32),...  1.22 us
    pallas_call x1, Pallas kernels, body(): call(memory_other_kernel, [(memory.shape, BF16)], 4, scratch=half_scratch...  1.2 us
    pallas_call x1, Pallas kernels, body(): call(output_kernel, [piece], 5, flops=30000000)  1.04 us
    unnamed x34, local copies, waits for them, and re-layouts  0.93 us
  transfers between devices with their start and end apart: 2, of which 1 were waited for; matrix products, arithmetic and copies ran while one was open for 0% of the time, Pallas kernels for 6%

profile of v12, /device:TPU:1, one launch (start us, length us, event | category | flops | bytes accessed | tf_op | source)
XLA Modules:
  0.0 42.1 jit_solution(5004038762646055445)
XLA Ops:
  0.6 0.0 copy-start.6
  0.6 0.0 copy-start.7
  0.7 0.0 copy-start
  0.7 0.0 copy-start.10
  0.7 0.0 copy-start.9
  0.7 0.0 copy-start.8
  0.7 0.0 copy-start.3
  0.7 0.0 copy-start.2
  0.7 0.0 copy-start.5
  0.7 0.0 copy-start.4
  0.7 0.0 copy-start.11
  0.8 0.0 copy-start.12
  0.8 0.8 %copy-done.12 = f32[24,128]{1,0:T(8,128)S(1)} copy-done((f32[24,128]{1,0:T(8,128)S(1)}, f32[24,128]{1,0:T(8,128)}, u32[]{:S(2)}) %copy-start.12) | copy-done | bytes 12312
  1.6 0.0 copy-start.14
  1.6 0.0 copy-start.15
  1.6 0.0 copy-start.16
  1.6 13.3 %all_to_all.15.x_ref = bf16[32,24,128]{2,1,0:T(8,128)(2,1)S(1)} all-to-all(bf16[32,24,128]{2,1,0:T(8,128)(2,1)S(1)} %shard_map.183), channel_id=1, replica_groups={{21,23,17,19,29,31,25,27,5,7,1,3,13,15,9,11,20,22,16,18,28,30,24,26,4,6..., dimensions={0} | all-to-all | bytes 393216 | tf_op jit(solution)/shard_map/all_to_all | solution.py:27
  14.9 0.0 copy-done.6
  14.9 0.0 copy-done.7
  14.9 0.0 copy-done
  14.9 0.0 copy-done.10
  14.9 0.0 copy-done.9
  15.0 0.0 copy-done.8
  15.0 0.0 copy-done.3
  15.0 0.0 copy-done.2
  15.0 0.0 copy-done.5
  15.0 0.0 copy-done.4
  15.0 0.0 copy-done.11
  15.0 0.0 copy-done.14
  15.0 0.0 copy-done.15
  15.0 0.0 copy-done.16
  15.0 0.0 copy-start.1
  15.1 1.4 %shard_map.184 = (bf16[32,40,128]{2,1,0:T(8,128)(2,1)S(1)}, f32[64,24]{1,0:T(8,128)S(1)}, f32[8,24]{1,0:T(8,128)S(1)}, f32[64,24]{1,0:T(8,128)S(1)}, f32[64,24]{...) custom-call(bf16[32,24,128]{2,1,0:T(8,128)(2,1)S(1)} %all_to_all.15.x_ref, ...), custom_call_target="tpu_custom_call" | custom-call | flops 100000000 | bytes 2000000 | tf_op jit(solution)/shard_map/pallas_call | solution.py:290
  16.5 12.5 %all_to_all.16.in_ref.half_ref = bf16[32,40,128]{2,1,0:T(8,128)(2,1)S(1)} all-to-all(bf16[32,40,128]{2,1,0:T(8,128)(2,1)S(1)} %get-tuple-element.15), channel_id=1, replica_groups={{21,23,17,19,29,31,25,27,5,7,1,3,13,15,9,11,20,22,16,18,28,30,24,26,4,6..., dimensions={0} | all-to-all | bytes 655360 | tf_op jit(solution)/shard_map/all_to_all | solution.py:27
  29.1 0.0 copy-done.1
  29.1 1.0 %shard_map.185 = bf16[32,24,128]{2,1,0:T(8,128)(2,1)} custom-call(bf16[32,40,128]{2,1,0:T(8,128)(2,1)S(1)} %all_to_all.16.in_ref.half_ref, f32[24,128]{1,0:T(8,128)S(1)} %get-tuple-element.16.sum_scale_ref, f32[24,128]{1,0:T(8,128)S(1)} %get-tuple-element.17.own_ref, f32[24,128]{1,0:T(8,128)S(1)} %get-tuple-element.18.floor_ref, bf16[128,4096]{1,0:T(8,128)(2,1)S(1)} %copy-done.1), custom_call_target="tpu_custom_call" | custom-call | flops 30000000 | bytes 2000000 | tf_op jit(solution)/shard_map/pallas_call | solution.py:312
  30.1 7.9 %all-to-all-start.2 = ((bf16[32,24,128]{2,1,0:T(8,128)(2,1)}), bf16[32,24,128]{2,1,0:T(8,128)(2,1)S(1)}, u32[]{:S(2)}, u32[]{:S(2)}) async-start(bf16[32,24,128]{2,1,0:T(8,128)(2,1)} %shard_map.185), calls=%async_computation.2 | async-start | bytes 393216 | tf_op jit(solution)/shard_map/all_to_all | solution.py:27
  38.0 0.5 %collective-permute-start = (bf16[32,16,128]{2,1,0:T(8,128)(2,1)S(1)}, bf16[32,16,128]{2,1,0:T(8,128)(2,1)S(1)}, u32[]{:S(2)}, u32[]{:S(2)}) collective-permute-start(bf16[32,16,128]{2,1,0:T(8,128)(2,1)S(1)} %slice.4), channel_id=1, source_target_pairs={{0,1},{1,0},{2,3},{3,2},{4,5},{5,4},{6,7},{7,6},{8,9},{9,8},{10,11... | collective-permute-start | bytes 393224 | tf_op jit(solution)/shard_map/swap/ppermute | solution.py:317
  38.5 1.2 %shard_map.187 = (bf16[24,8,8,512]{3,2,1,0:T(8,128)(2,1)}, f32[64,24]{1,0:T(8,128)}, f32[8,24]{1,0:T(8,128)}) custom-call(f32[64,24]{1,0:T(8,128)S(1)} %get-tuple-element.19.f_rows_ref, f32[64,24]{1,0:T(8,128)S(1)} %get-tuple-element.20.ik_rows_ref, f32[64,24]{1,0:T(8,128)S(1)} %get-tuple-element.21.norm_ref, f32[8,24]{1,0:T(8,128)S(1)} %get-tuple-element.22.stab_ref, ...), custom_call_target="tpu_custom_call" | custom-call | flops 50000000 | bytes 2000000 | tf_op jit(solution)/shard_map/pallas_call | solution.py:323
  39.8 0.0 collective-permute-done.half_ref
  39.8 0.0 copy-start.13
  39.8 1.2 %shard_map.188 = bf16[24,8,8,512]{3,2,1,0:T(8,128)(2,1)} custom-call(f32[64,24]{1,0:T(8,128)S(1)} %get-tuple-element.19.f_rows_ref, f32[64,24]{1,0:T(8,128)S(1)} %get-tuple-element.20.ik_rows_ref, bf16[32,16,128]{2,1,0:T(8,128)(2,1)S(1)} %collective-permute-done.half_ref, bf16[24,8,8,512]{3,2,1,0:T(8,128)(2,1)S(1)} %copy-done, ...), custom_call_target="tpu_custom_call", output_to_operand_aliasing={{}: (4, {})} | custom-call | flops 50000000 | bytes 2000000 | tf_op jit(solution)/shard_map/pallas_call | solution.py:331
  41.0 0.4 %all-to-all-done.2.in_ref = bf16[32,24,128]{2,1,0:T(8,128)(2,1)S(1)} async-done(((bf16[32,24,128]{2,1,0:T(8,128)(2,1)}), bf16[32,24,128]{2,1,0:T(8,128)(2,1)S(1)}, u32[]{:S(2)}, u32[]{:S(2)}) %all-to-all-start.2) | async-done | bytes 196640 | tf_op jit(solution)/shard_map/all_to_all | solution.py:27
  41.5 0.0 copy-done.13
  41.5 0.6 %shard_map.186 = f32[24,128]{1,0:T(8,128)} custom-call(bf16[32,24,128]{2,1,0:T(8,128)(2,1)S(1)} %all-to-all-done.2.in_ref, f32[24,128]{1,0:T(8,128)S(1)} %copy-done.13), custom_call_target="tpu_custom_call" | custom-call | flops 1000000 | bytes 2000000 | tf_op jit(solution)/shard_map/pallas_call | solution.py:340
  (2 shorter events, 0.0 us)
Async XLA Ops:
  0.6 14.3 %copy-start.6 = (bf16[64,3072]{1,0:T(8,128)(2,1)S(1)}, bf16[64,3072]{1,0:T(8,128)(2,1)}, u32[]{:S(2)}) copy-start(bf16[64,3072]{1,0:T(8,128)(2,1)} %constant.4.clone.repeat_ref) | copy-start | bytes 1179652
  0.6 14.3 %copy-start.7 = (bf16[96,384]{1,0:T(8,128)(2,1)S(1)}, bf16[96,384]{1,0:T(8,128)(2,1)}, u32[]{:S(2)}) copy-start(bf16[96,384]{1,0:T(8,128)(2,1)} %constant.5.clone.own_ref) | copy-start | bytes 221188
  0.7 14.3 %copy-start = (bf16[24,8,8,512]{3,2,1,0:T(8,128)(2,1)S(1)}, bf16[24,8,8,512]{3,2,1,0:T(8,128)(2,1)}, u32[]{:S(2)}) copy-start(bf16[24,8,8,512]{3,2,1,0:T(8,128)(2,1)} %mem_ref.3) | copy-start | bytes 4718596
  0.7 14.3 %copy-start.10 = (f32[24,8,8]{0,2,1:T(8,128)S(1)}, f32[24,8,8]{0,2,1:T(8,128)}, u32[]{:S(2)}) copy-start(f32[24,8,8]{0,2,1:T(8,128)} %param.28) | copy-start | bytes 18436
  0.7 14.3 %copy-start.9 = (bf16[8,4096]{1,0:T(8,128)(2,1)S(1)}, bf16[8,4096]{1,0:T(8,128)(2,1)}, u32[]{:S(2)}) copy-start(bf16[8,4096]{1,0:T(8,128)(2,1)} %wf_ref.1) | copy-start | bytes 196612
  0.7 14.3 %copy-start.8 = (bf16[8,4096]{1,0:T(8,128)(2,1)S(1)}, bf16[8,4096]{1,0:T(8,128)(2,1)}, u32[]{:S(2)}) copy-start(bf16[8,4096]{1,0:T(8,128)(2,1)} %wi_ref.1) | copy-start | bytes 196612
  0.7 14.3 %copy-start.3 = (bf16[4096,128]{1,0:T(8,128)(2,1)S(1)}, bf16[4096,128]{1,0:T(8,128)(2,1)}, u32[]{:S(2)}) copy-start(bf16[4096,128]{1,0:T(8,128)(2,1)} %wg_ref.1) | copy-start | bytes 3145732
  0.7 14.3 %copy-start.2 = (bf16[4096,128]{1,0:T(8,128)(2,1)S(1)}, bf16[4096,128]{1,0:T(8,128)(2,1)}, u32[]{:S(2)}) copy-start(bf16[4096,128]{1,0:T(8,128)(2,1)} %wv_ref.1) | copy-start | bytes 3145732
  0.7 14.3 %copy-start.5 = (bf16[8,8,4096]{2,1,0:T(8,128)(2,1)S(1)}, bf16[8,8,4096]{2,1,0:T(8,128)(2,1)}, u32[]{:S(2)}) copy-start(bf16[8,8,4096]{2,1,0:T(8,128)(2,1)} %param.19) | copy-start | bytes 1572868
  0.7 14.3 %copy-start.4 = (bf16[8,8,4096]{2,1,0:T(8,128)(2,1)S(1)}, bf16[8,8,4096]{2,1,0:T(8,128)(2,1)}, u32[]{:S(2)}) copy-start(bf16[8,8,4096]{2,1,0:T(8,128)(2,1)} %param.18) | copy-start | bytes 1572868
  0.7 14.3 %copy-start.11 = (f32[4096]{0:T(1024)S(1)}, f32[4096]{0:T(1024)}, u32[]{:S(2)}) copy-start(f32[4096]{0:T(1024)} %param.17) | copy-start | bytes 49156
  0.8 0.9 %copy-start.12 = (f32[24,128]{1,0:T(8,128)S(1)}, f32[24,128]{1,0:T(8,128)}, u32[]{:S(2)}) copy-start(f32[24,128]{1,0:T(8,128)} %residual_ref.1) | copy-start | bytes 36868
  1.6 13.4 %copy-start.14 = (f32[24,8]{0,1:T(8,128)S(1)}, f32[24,8]{0,1:T(8,128)}, u32[]{:S(2)}) copy-start(f32[24,8]{0,1:T(8,128)} %param.29) | copy-start | bytes 2308
  1.6 13.4 %copy-start.15 = (f32[8]{0:T(128)S(1)}, f32[8]{0:T(128)}, u32[]{:S(2)}) copy-start(f32[8]{0:T(128)} %param.24) | copy-start | bytes 100
  1.6 13.4 %copy-start.16 = (f32[8]{0:T(128)S(1)}, f32[8]{0:T(128)}, u32[]{:S(2)}) copy-start(f32[8]{0:T(128)} %param.25) | copy-start | bytes 100
  15.0 14.0 %copy-start.1 = (bf16[128,4096]{1,0:T(8,128)(2,1)S(1)}, bf16[128,4096]{1,0:T(8,128)(2,1)}, u32[]{:S(2)}) copy-start(bf16[128,4096]{1,0:T(8,128)(2,1)} %wo_ref.1) | copy-start | bytes 3145732
  30.1 11.4 %all-to-all-start.2 = ((bf16[32,24,128]{2,1,0:T(8,128)(2,1)}), bf16[32,24,128]{2,1,0:T(8,128)(2,1)S(1)}, u32[]{:S(2)}, u32[]{:S(2)}) async-start(bf16[32,24,128]{2,1,0:T(8,128)(2,1)} %shard_map.185), calls=%async_computation.2 | async-start | bytes 393216 | tf_op jit(solution)/shard_map/all_to_all | solution.py:27
  38.0 1.8 %collective-permute-start = (bf16[32,16,128]{2,1,0:T(8,128)(2,1)S(1)}, bf16[32,16,128]{2,1,0:T(8,128)(2,1)S(1)}, u32[]{:S(2)}, u32[]{:S(2)}) collective-permute-start(bf16[32,16,128]{2,1,0:T(8,128)(2,1)S(1)} %slice.4), channel_id=1, source_target_pairs={{0,1},{1,0},{2,3},{3,2},{4,5},{5,4},{6,7},{7,6},{8,9},{9,8},{10,11... | collective-permute-start | bytes 393224 | tf_op jit(solution)/shard_map/swap/ppermute | solution.py:317
  39.8 1.7 %copy-start.13 = (f32[24,128]{1,0:T(8,128)S(1)}, f32[24,128]{1,0:T(8,128)}, u32[]{:S(2)}) copy-start(f32[24,128]{1,0:T(8,128)} %residual_ref.1) | copy-start | bytes 36868
